TPU v7x, 32 devices: a whole 2x2x4 slice. The times are simulated.
32 devices in a mesh: vehicle: 4 (over y, x), track: 2 (over core), cross: 4 (over z).
Axes of the slice: x: 2, y: 2, z: 4, core: 2. Of those that a mesh axis runs over, the one named last changes fastest.
Arguments:
- particle_offset: float32 [3, 16, 32, 128], P(None, ('vehicle', 'track'), 'cross'), may hold values from 0 to 1
- particle_velocity: float32 [3, 16, 32, 128], P(None, ('vehicle', 'track'), 'cross'), may hold values from -4 to 4
- cell_count: int32 [16, 32], P(('vehicle', 'track'), 'cross'), may hold values from 32 to 128
- face_offset: float32 [2048, 3, 128], P(('vehicle', 'track', 'cross')), may hold values from 0 to 1
- face_velocity: float32 [2048, 3, 128], P(('vehicle', 'track', 'cross')), may hold values from -4 to 4
- face_route: int32 [2048, 1], P(('vehicle', 'track', 'cross')), may hold values from 0 to 7; in each aligned block of 64 rows (0 to 63, 64 to 127, ...) at most 32 rows name the same one
- face_cell: int32 [2048], P(('vehicle', 'track', 'cross')), may hold values from 0 to 15
Outputs:
- moved_offset: float32 [3, 16, 32, 128], P(None, ('vehicle', 'track'), 'cross')
- new_velocity: float32 [3, 16, 32, 128], P(None, ('vehicle', 'track'), 'cross')
- face_impulse: float32 [2048, 3, 128], P(('vehicle', 'track', 'cross'))
Inputs may be any that keep to these rules, and one draw needn't show every extreme that they name: `face_route`: among the 64 face blocks of one owner device, at most 32 name the same terrain device, and that many is reached.
All inputs are finite; a program needn't handle non-finite values.
Results may differ from a plain program's by a relative error of at most 0.0003.
Values sent between devices are 32-bit elements; how exact they have to be, the bound alone decides.
No kernel may reach another device: no remote copies, remote signals or barrier semaphores. Data moves between devices by JAX's collectives and lax.ppermute only.
A program may use at most 64 MiB of HBM per device.

v0:
```python
import jax
import jax.numpy as jnp
from jax import lax
from jax.sharding import PartitionSpec as P

radius = 0.1
face_radius = 0.15
stiffness = 100.0
damping = 40.0
soften = 0.05
time_step = 0.02
gravity = 9.81


def with_halo(block, sides, width):
    for axis, dim in sides:
        count = lax.axis_size(axis)
        forward = [(i, i + 1) for i in range(count - 1)]
        backward = [(target, source) for source, target in forward]
        low = lax.ppermute(
            lax.slice_in_dim(block, block.shape[dim] - width, None, axis=dim), axis, forward
        )
        high = lax.ppermute(lax.slice_in_dim(block, 0, width, axis=dim), axis, backward)
        block = jnp.concatenate([low, block, high], axis=dim)
    return block


def contact(own_pos, own_vel, other_pos, other_vel, other_live, reach):
    apart = own_pos[:, :, :, None] - other_pos[:, :, None, :]
    distance = jnp.sqrt(jnp.sum(apart * apart, axis=0) + soften * soften)
    normal = apart / distance[None]
    closing = jnp.sum((own_vel[:, :, :, None] - other_vel[:, :, None, :]) * normal, axis=0)
    intersection = jnp.maximum(reach - distance, 0.0)
    weight = intersection * (stiffness - damping * closing) * other_live[:, None, :]
    return weight[None] * normal


def particle_forces(stacked, padded):
    across = stacked.shape[2]
    slot_count = stacked.shape[3]
    others = 1.0 - jnp.eye(slot_count, dtype=jnp.float32)

    def row_force(row_index):
        own_part = lax.dynamic_slice_in_dim(stacked, row_index, 1, 1)[:, 0]
        total_force = jnp.zeros((3, across, slot_count), jnp.float32)
        for shift_t in (-1, 0, 1):
            band_rows = lax.dynamic_slice_in_dim(padded, row_index + 1 + shift_t, 1, 1)[:, 0]
            for shift_c in (-1, 0, 1):
                neighbour = band_rows[:, 1 + shift_c : 1 + shift_c + across]
                offset = jnp.array([shift_t, shift_c, 0.0], jnp.float32)[:, None, None]
                pushes = contact(
                    own_part[0:3],
                    own_part[3:6],
                    neighbour[0:3] + offset,
                    neighbour[3:6],
                    neighbour[6],
                    2.0 * radius,
                )
                if shift_t == 0 and shift_c == 0:
                    pushes = pushes * others
                total_force = total_force + jnp.sum(pushes, axis=3)
        return total_force * own_part[6][None]

    forces = lax.map(row_force, jnp.arange(stacked.shape[1], dtype=jnp.int32))
    return jnp.transpose(forces, (1, 0, 2, 3))


def tire_contact(chosen, face_pos, face_vel):
    ones_live = jnp.ones((face_pos.shape[1], face_pos.shape[2]), jnp.float32)
    pushes = contact(chosen[0:3], chosen[3:6], face_pos, face_vel, ones_live, radius + face_radius)
    pushes = pushes * chosen[6][None, :, :, None]
    return (jnp.sum(pushes, axis=3), -jnp.sum(pushes, axis=2))


def advance(offsets, velocity, stacked, face_push):
    padded = with_halo(stacked, ((("vehicle", "track"), 1), ("cross", 2)), 1)
    total_push = particle_forces(stacked, padded) + face_push
    fall = jnp.array([0.0, 0.0, -gravity], jnp.float32)[:, None, None, None]
    velocity = velocity + time_step * (total_push + fall)
    offsets = offsets + time_step * velocity
    return (offsets, velocity)


def body(
    particle_offset,
    particle_velocity,
    cell_count,
    face_offset,
    face_velocity,
    face_route,
    face_cell,
):
    travel_rows, cross_rows, slot_count = particle_offset.shape[1:]
    nblocks = travel_rows * cross_rows
    own_faces = face_offset.shape[0]
    faces = face_offset.shape[2]
    peers = lax.axis_size("track") * lax.axis_size("cross")
    capacity = max(2, 4 * own_faces // peers)
    items = peers * capacity
    live = (
        lax.broadcasted_iota(jnp.int32, (travel_rows, cross_rows, slot_count), 2)
        < cell_count[:, :, None]
    ).astype(jnp.float32)
    target = face_route[:, 0]
    first_index = lax.broadcasted_iota(jnp.int32, (own_faces, own_faces), 0)
    second_index = lax.broadcasted_iota(jnp.int32, (own_faces, own_faces), 1)
    earlier = (target[None, :] == target[:, None]) & (second_index < first_index)
    slot_index = jnp.sum(earlier.astype(jnp.int32), axis=1)
    hits = (
        lax.broadcasted_iota(jnp.int32, (own_faces, items), 1)
        == (target * capacity + slot_index)[:, None]
    )
    placement = hits.astype(jnp.float32)
    block_ids = lax.broadcasted_iota(jnp.int32, (1, nblocks), 1) + 1
    highest = lax.Precision.HIGHEST
    offsets = particle_offset
    velocity = particle_velocity
    requests = jnp.sum(hits.astype(jnp.int32) * (face_cell + 1)[:, None], axis=0)
    asked = lax.all_to_all(
        requests.reshape(peers, capacity),
        ("track", "cross"),
        split_axis=0,
        concat_axis=0,
        tiled=True,
    )
    selector = (asked.reshape(items)[:, None] == block_ids).astype(jnp.float32)
    group_size = own_faces // 4
    vel_spans = jnp.transpose(face_velocity.reshape(4, group_size, 3, faces), (0, 2, 1, 3))
    reaction = jnp.zeros((own_faces, 3, faces), jnp.float32)
    for substep in range(2):
        stacked = jnp.concatenate([offsets, velocity, live[None]], axis=0)
        chosen = jnp.einsum(
            "mk,rks->mrs", selector, stacked.reshape(7, nblocks, slot_count), precision=highest
        ).reshape(peers, capacity, 7, slot_count)
        fetched = lax.all_to_all(
            chosen, ("track", "cross"), split_axis=0, concat_axis=0, tiled=True
        )
        mine = jnp.einsum(
            "ip,prs->irs", placement, fetched.reshape(items, 7, slot_count), precision=highest
        )
        mine_spans = jnp.transpose(mine.reshape(4, group_size, 7, slot_count), (0, 2, 1, 3))
        faces_now = face_offset + substep * time_step * face_velocity
        pos_spans = jnp.transpose(faces_now.reshape(4, group_size, 3, faces), (0, 2, 1, 3))

        def owner_pass(pieces):
            return tire_contact(pieces[0], pieces[1], pieces[2])

        on_particles, on_faces = lax.map(owner_pass, (mine_spans, pos_spans, vel_spans))
        on_particles = jnp.transpose(on_particles, (0, 2, 1, 3)).reshape(own_faces, 3, slot_count)
        on_faces = jnp.transpose(on_faces, (0, 2, 1, 3)).reshape(own_faces, 3, faces)
        outgoing = jnp.einsum("ip,irs->prs", placement, on_particles, precision=highest)
        incoming = lax.all_to_all(
            outgoing.reshape(peers, capacity, 3, slot_count),
            ("track", "cross"),
            split_axis=0,
            concat_axis=0,
            tiled=True,
        )
        summed = jnp.einsum(
            "mk,mrs->rks", selector, incoming.reshape(items, 3, slot_count), precision=highest
        )
        face_push = summed.reshape(3, travel_rows, cross_rows, slot_count)
        offsets, velocity = advance(offsets, velocity, stacked, face_push)
        reaction = reaction + on_faces
    impulse = time_step * reaction
    return (offsets, velocity, impulse)


def solution(mesh):
    in_specs = (
        P(None, ("vehicle", "track"), "cross", None),
        P(None, ("vehicle", "track"), "cross", None),
        P(("vehicle", "track"), "cross"),
        P(("vehicle", "track", "cross"), None, None),
        P(("vehicle", "track", "cross"), None, None),
        P(("vehicle", "track", "cross"), None),
        P(("vehicle", "track", "cross")),
    )
    out_specs = (
        P(None, ("vehicle", "track"), "cross", None),
        P(None, ("vehicle", "track"), "cross", None),
        P(("vehicle", "track", "cross"), None, None),
    )
    return jax.shard_map(body, mesh=mesh, in_specs=in_specs, out_specs=out_specs, check_vma=False)
```

profile of v0, /device:TPU:11, one launch (start us, length us, event | category | flops | bytes accessed | tf_op | source)
XLA Modules:
  0.0 224.1 jit_solution(9749662036510042449)
XLA Ops:
  3.6 5.6 %all-to-all-start = ((s32[8,1,32]{2,1,0:T(1,128)}), s32[8,1,32]{2,1,0:T(1,128)S(1)}, u32[]{:S(2)}, u32[]{:S(2)}) async-start(s32[8,1,32]{2,1,0:T(1,128)} %all_to_all.18), calls=%async_computation | async-start | bytes 8192 | tf_op jit(solution)/shard_map/all_to_all | solution.py:119
  15.4 5.4 %all-to-all-start.1 = ((f32[8,32,7,128]{3,1,2,0:T(8,128)}), f32[8,32,7,128]{3,1,2,0:T(8,128)S(1)}, u32[]{:S(2)}, u32[]{:S(2)}) async-start(f32[8,32,7,128]{3,1,2,0:T(8,128)} %fusion.48), calls=%async_computation.1 | async-start | bytes 1835008 | tf_op jit(solution)/shard_map/all_to_all | solution.py:135
  20.9 3.4 %collective-permute-start = (f32[7,1,8,128]{3,2,0,1:T(8,128)S(1)}, f32[7,1,8,128]{3,2,0,1:T(8,128)S(1)}, u32[]{:S(2)}, u32[]{:S(2)}) collective-permute-start(f32[7,1,8,128]{3,2,0,1:T(8,128)S(1)} %copy.90), channel_id=1, source_target_pairs={{0,4},{4,8},{8,12},{12,16},{16,20},{20,24},{24,28},{1,5},{5,9},{9,... | collective-permute-start | bytes 86024 | tf_op jit(solution)/shard_map/ppermute | solution.py:20
  26.4 4.3 %collective-permute-done.1 = f32[7,1,8,128]{3,2,0,1:T(8,128)S(1)} collective-permute-done((f32[7,1,8,128]{3,2,0,1:T(8,128)S(1)}, f32[7,1,8,128]{3,2,0,1:T(8,128)S(1)}, u32[]{:S(2)}, u32[]{:S(2)}) %collective-permute-start.1) | collective-permute-done | bytes 28704 | tf_op jit(solution)/shard_map/ppermute | solution.py:23
  30.7 3.1 %collective-permute-start.2 = (f32[7,4,1,128]{3,2,0,1:T(1,128)S(1)}, f32[7,4,1,128]{3,2,0,1:T(1,128)S(1)}, u32[]{:S(2)}, u32[]{:S(2)}) collective-permute-start(f32[7,4,1,128]{3,2,0,1:T(1,128)S(1)} %get-tuple-element.998), channel_id=1, source_target_pairs={{0,1},{1,2},{2,3},{4,5},{5,6},{6,7},{8,9},{9,10},{10,11},{12,13},{... | collective-permute-start | bytes 43016 | tf_op jit(solution)/shard_map/ppermute | solution.py:20
  37.3 4.0 %collective-permute-done.2 = f32[7,4,1,128]{3,2,0,1:T(1,128)S(1)} collective-permute-done((f32[7,4,1,128]{3,2,0,1:T(1,128)S(1)}, f32[7,4,1,128]{3,2,0,1:T(1,128)S(1)}, u32[]{:S(2)}, u32[]{:S(2)}) %collective-permute-start.2) | collective-permute-done | bytes 14368 | tf_op jit(solution)/shard_map/ppermute | solution.py:20
  43.2 25.4 %while.56 = (s32[]{:T(128)}, f32[4,3,16,128]{3,2,0,1:T(8,128)S(1)}, f32[4,3,16,128]{3,2,1,0:T(8,128)S(1)}, f32[4,7,16,128]{3,2,1,0:T(8,128)S(1)}, f32[4,3,16,128...) while((s32[]{:T(128)}, f32[4,3,16,128]{3,2,0,1:T(8,128)S(1)}, ...), condition=%wide.region_36.37_spmd, body=%wide.region_31.36_spmd.sunk | while | flops 12314628 | bytes 11051161 | solution.py:148
  69.8 5.5 %all-to-all-start.2 = ((f32[8,32,3,128]{3,1,2,0:T(8,128)}), f32[8,32,3,128]{3,1,2,0:T(8,128)S(1)}, u32[]{:S(2)}, u32[]{:S(2)}) async-start(f32[8,32,3,128]{3,1,2,0:T(8,128)} %fusion.38), calls=%async_computation.2 | async-start | bytes 786432 | tf_op jit(solution)/shard_map/all_to_all | solution.py:152
  75.4 42.7 %while.58 = (s32[]{:T(128)}, f32[2,3,8,128]{3,2,0,1:T(8,128)S(1)}, s32[2]{0:T(128)S(1)}, f32[7,2,8,128]{3,2,1,0:T(8,128)S(1)}, f32[7,4,10,128]{3,2,0,1:T(8,128)S...) while((s32[]{:T(128)}, f32[2,3,8,128]{3,2,0,1:T(8,128)S(1)}, ...), condition=%wide.region_28.29_spmd.clone.clone, body=%wide.region_0.28_spmd.sunk.clone.clone.sunk | while | flops 50012176 | bytes 48908780 | solution.py:64
  86.8 3.1 %multiply_reduce_fusion.51 = (f32[3,8,128]{2,1,0:T(8,128)S(1)}, f32[8,128,128]{2,1,0:T(8,128)S(1)}, f32[8,128,128]{2,1,0:T(8,128)S(1)}, f32[8,128,128]{2,1,0:T(8...) fusion(f32[8,128,128]{2,1,0:T(8,128)S(1)} %multiply_multiply_fu, ...), kind=kLoop, calls=%fused_computation.75.clone.1 | loop fusion | flops 10866688 | bytes 6516736 | tf_op jit(solution)/shard_map/while/body/eval_jaxpr/reduce_sum | solution.py:61
  93.5 3.2 %multiply_reduce_fusion.53 = (f32[3,8,128]{2,1,0:T(8,128)S(1)}, f32[3,8,128]{2,1,0:T(8,128)S(1)}, f32[3,8,128]{2,1,0:T(8,128)S(1)}, f32[3,8,128]{2,1,0:T(8,128)S(1)}, f32[3,8,128]{2,1,0:T(8,128)S(1)}) fusion(f32[8,128,128]{2,1,0:T(8,128)S(1)} %multiply_multiply_fusion.42, f32[8,128,128]{2,1,0:T(8,128)S(1)} %add_sqrt_fusion.47, ...), kind=kLoop, calls=%fused_computation.77.clone.1 | loop fusion | flops 7848960 | bytes 5378048 | tf_op jit(solution)/shard_map/while/body/eval_jaxpr/reduce_sum | solution.py:61
  108.2 3.1 %multiply_reduce_fusion.51 = (f32[3,8,128]{2,1,0:T(8,128)S(1)}, f32[8,128,128]{2,1,0:T(8,128)S(1)}, f32[8,128,128]{2,1,0:T(8,128)S(1)}, f32[8,128,128]{2,1,0:T(8...) fusion(f32[8,128,128]{2,1,0:T(8,128)S(1)} %multiply_multiply_fu, ...), kind=kLoop, calls=%fused_computation.75.clone.1 | loop fusion | flops 10866688 | bytes 6516736 | tf_op jit(solution)/shard_map/while/body/eval_jaxpr/reduce_sum | solution.py:61
  114.9 3.2 %multiply_reduce_fusion.53 = (f32[3,8,128]{2,1,0:T(8,128)S(1)}, f32[3,8,128]{2,1,0:T(8,128)S(1)}, f32[3,8,128]{2,1,0:T(8,128)S(1)}, f32[3,8,128]{2,1,0:T(8,128)S(1)}, f32[3,8,128]{2,1,0:T(8,128)S(1)}) fusion(f32[8,128,128]{2,1,0:T(8,128)S(1)} %multiply_multiply_fusion.42, f32[8,128,128]{2,1,0:T(8,128)S(1)} %add_sqrt_fusion.47, ...), kind=kLoop, calls=%fused_computation.77.clone.1 | loop fusion | flops 7848960 | bytes 5378048 | tf_op jit(solution)/shard_map/while/body/eval_jaxpr/reduce_sum | solution.py:61
  120.1 5.1 %all-to-all-start.3 = ((f32[8,32,7,128]{3,1,2,0:T(8,128)}), f32[8,32,7,128]{3,1,2,0:T(8,128)S(1)}, u32[]{:S(2)}, u32[]{:S(2)}) async-start(f32[8,32,7,128]{3,1,2,0:T(8,128)} %fusion.46), calls=%async_computation.3 | async-start | bytes 1835008 | tf_op jit(solution)/shard_map/all_to_all | solution.py:135
  125.2 3.5 %collective-permute-start.4 = (f32[7,1,8,128]{3,2,1,0:T(8,128)S(1)}, f32[7,1,8,128]{3,2,1,0:T(8,128)S(1)}, u32[]{:S(2)}, u32[]{:S(2)}) collective-permute-start(f32[7,1,8,128]{3,2,1,0:T(8,128)S(1)} %get-tuple-element.1000), channel_id=1, source_target_pairs={{0,4},{4,8},{8,12},{12,16},{16,20},{20,24},{24,28},{1,5},{5,9},{9,... | collective-permute-start | bytes 86024 | tf_op jit(solution)/shard_map/ppermute | solution.py:20
  130.7 4.4 %collective-permute-done.5 = f32[7,1,8,128]{3,2,1,0:T(8,128)S(1)} collective-permute-done((f32[7,1,8,128]{3,2,1,0:T(8,128)S(1)}, f32[7,1,8,128]{3,2,1,0:T(8,128)S(1)}, u32[]{:S(2)}, u32[]{:S(2)}) %collective-permute-start.5) | collective-permute-done | bytes 28704 | tf_op jit(solution)/shard_map/ppermute | solution.py:23
  140.7 5.1 %collective-permute-done.6 = f32[7,4,1,128]{3,2,1,0:T(1,128)S(1)} collective-permute-done((f32[7,4,1,128]{3,2,1,0:T(1,128)S(1)}, f32[7,4,1,128]{3,2,1,0:T(1,128)S(1)}, u32[]{:S(2)}, u32[]{:S(2)}) %collective-permute-start.6) | collective-permute-done | bytes 14368 | tf_op jit(solution)/shard_map/ppermute | solution.py:20
  147.6 25.4 %while.57 = (s32[]{:T(128)}, f32[4,3,16,128]{3,2,0,1:T(8,128)S(1)}, f32[4,3,16,128]{3,2,1,0:T(8,128)S(1)}, f32[4,7,16,128]{3,2,1,0:T(8,128)S(1)}, f32[4,3,16,128...) while((s32[]{:T(128)}, f32[4,3,16,128]{3,2,0,1:T(8,128)S(1)}, ...), condition=%wide.region_71.72_spmd, body=%wide.region_66.0_spmd.sunk | while | flops 12314628 | bytes 11051161 | solution.py:148
  174.1 5.6 %all-to-all-start.4 = ((f32[8,32,3,128]{3,1,2,0:T(8,128)}), f32[8,32,3,128]{3,1,2,0:T(8,128)S(1)}, u32[]{:S(2)}, u32[]{:S(2)}) async-start(f32[8,32,3,128]{3,1,2,0:T(8,128)} %fusion.36), calls=%async_computation.4 | async-start | bytes 786432 | tf_op jit(solution)/shard_map/all_to_all | solution.py:152
  179.7 42.7 %while.59 = (s32[]{:T(128)}, f32[2,3,8,128]{3,2,0,1:T(8,128)S(1)}, s32[2]{0:T(128)S(1)}, f32[7,2,8,128]{3,2,1,0:T(8,128)S(1)}, f32[7,4,10,128]{3,2,0,1:T(8,128)S...) while((s32[]{:T(128)}, f32[2,3,8,128]{3,2,0,1:T(8,128)S(1)}, ...), condition=%wide.region_65.66_spmd.clone.clone, body=%wide.region_37.65_spmd.sunk.clone.clone.sunk | while | flops 50012176 | bytes 48908780 | solution.py:64
  191.0 3.1 %multiply_reduce_fusion.55 = (f32[3,8,128]{2,1,0:T(8,128)S(1)}, f32[8,128,128]{2,1,0:T(8,128)S(1)}, f32[8,128,128]{2,1,0:T(8,128)S(1)}, f32[8,128,128]{2,1,0:T(8...) fusion(f32[8,128,128]{2,1,0:T(8,128)S(1)} %multiply_multiply_fu, ...), kind=kLoop, calls=%fused_computation.165.clone.1 | loop fusion | flops 10866688 | bytes 6516736 | tf_op jit(solution)/shard_map/while/body/eval_jaxpr/reduce_sum | solution.py:61
  197.8 3.2 %multiply_reduce_fusion.57 = (f32[3,8,128]{2,1,0:T(8,128)S(1)}, f32[3,8,128]{2,1,0:T(8,128)S(1)}, f32[3,8,128]{2,1,0:T(8,128)S(1)}, f32[3,8,128]{2,1,0:T(8,128)S(1)}, f32[3,8,128]{2,1,0:T(8,128)S(1)}) fusion(f32[8,128,128]{2,1,0:T(8,128)S(1)} %multiply_multiply_fusion.51, f32[8,128,128]{2,1,0:T(8,128)S(1)} %add_sqrt_fusion.56, ...), kind=kLoop, calls=%fused_computation.167.clone.1 | loop fusion | flops 7848960 | bytes 5378048 | tf_op jit(solution)/shard_map/while/body/eval_jaxpr/reduce_sum | solution.py:61
  212.4 3.1 %multiply_reduce_fusion.55 = (f32[3,8,128]{2,1,0:T(8,128)S(1)}, f32[8,128,128]{2,1,0:T(8,128)S(1)}, f32[8,128,128]{2,1,0:T(8,128)S(1)}, f32[8,128,128]{2,1,0:T(8...) fusion(f32[8,128,128]{2,1,0:T(8,128)S(1)} %multiply_multiply_fu, ...), kind=kLoop, calls=%fused_computation.165.clone.1 | loop fusion | flops 10866688 | bytes 6516736 | tf_op jit(solution)/shard_map/while/body/eval_jaxpr/reduce_sum | solution.py:61
  219.2 3.2 %multiply_reduce_fusion.57 = (f32[3,8,128]{2,1,0:T(8,128)S(1)}, f32[3,8,128]{2,1,0:T(8,128)S(1)}, f32[3,8,128]{2,1,0:T(8,128)S(1)}, f32[3,8,128]{2,1,0:T(8,128)S(1)}, f32[3,8,128]{2,1,0:T(8,128)S(1)}) fusion(f32[8,128,128]{2,1,0:T(8,128)S(1)} %multiply_multiply_fusion.51, f32[8,128,128]{2,1,0:T(8,128)S(1)} %add_sqrt_fusion.56, ...), kind=kLoop, calls=%fused_computation.167.clone.1 | loop fusion | flops 7848960 | bytes 5378048 | tf_op jit(solution)/shard_map/while/body/eval_jaxpr/reduce_sum | solution.py:61
  (302 shorter events, 120.1 us)
Async XLA Ops:
  3.6 9.4 %all-to-all-start = ((s32[8,1,32]{2,1,0:T(1,128)}), s32[8,1,32]{2,1,0:T(1,128)S(1)}, u32[]{:S(2)}, u32[]{:S(2)}) async-start(s32[8,1,32]{2,1,0:T(1,128)} %all_to_all.18), calls=%async_computation | async-start | bytes 8192 | tf_op jit(solution)/shard_map/all_to_all | solution.py:119
  15.4 10.8 %copy-start.2 = (f32[64,3,128]{2,0,1:T(8,128)S(1)}, f32[64,3,128]{2,0,1:T(8,128)}, u32[]{:S(2)}) copy-start(f32[64,3,128]{2,0,1:T(8,128)} %param.39) | copy-start | bytes 294916
  15.4 10.8 %copy-start.5 = (f32[64,3,128]{2,0,1:T(8,128)S(1)}, f32[64,3,128]{2,0,1:T(8,128)}, u32[]{:S(2)}) copy-start(f32[64,3,128]{2,0,1:T(8,128)} %param.38) | copy-start | bytes 294916
  15.4 27.2 %all-to-all-start.1 = ((f32[8,32,7,128]{3,1,2,0:T(8,128)}), f32[8,32,7,128]{3,1,2,0:T(8,128)S(1)}, u32[]{:S(2)}, u32[]{:S(2)}) async-start(f32[8,32,7,128]{3,1,2,0:T(8,128)} %fusion.48), calls=%async_computation.1 | async-start | bytes 1835008 | tf_op jit(solution)/shard_map/all_to_all | solution.py:135
  20.9 5.5 %collective-permute-start = (f32[7,1,8,128]{3,2,0,1:T(8,128)S(1)}, f32[7,1,8,128]{3,2,0,1:T(8,128)S(1)}, u32[]{:S(2)}, u32[]{:S(2)}) collective-permute-start(f32[7,1,8,128]{3,2,0,1:T(8,128)S(1)} %copy.90), channel_id=1, source_target_pairs={{0,4},{4,8},{8,12},{12,16},{16,20},{20,24},{24,28},{1,5},{5,9},{9,... | collective-permute-start | bytes 86024 | tf_op jit(solution)/shard_map/ppermute | solution.py:20
  24.3 6.4 %collective-permute-start.1 = (f32[7,1,8,128]{3,2,0,1:T(8,128)S(1)}, f32[7,1,8,128]{3,2,0,1:T(8,128)S(1)}, u32[]{:S(2)}, u32[]{:S(2)}) collective-permute-start(f32[7,1,8,128]{3,2,0,1:T(8,128)S(1)} %copy.91), channel_id=1, source_target_pairs={{4,0},{8,4},{12,8},{16,12},{20,16},{24,20},{28,24},{5,1},{9,5},{13... | collective-permute-start | bytes 86024 | tf_op jit(solution)/shard_map/ppermute | solution.py:23
  30.7 10.6 %collective-permute-start.2 = (f32[7,4,1,128]{3,2,0,1:T(1,128)S(1)}, f32[7,4,1,128]{3,2,0,1:T(1,128)S(1)}, u32[]{:S(2)}, u32[]{:S(2)}) collective-permute-start(f32[7,4,1,128]{3,2,0,1:T(1,128)S(1)} %get-tuple-element.998), channel_id=1, source_target_pairs={{0,1},{1,2},{2,3},{4,5},{5,6},{6,7},{8,9},{9,10},{10,11},{12,13},{... | collective-permute-start | bytes 43016 | tf_op jit(solution)/shard_map/ppermute | solution.py:20
  33.8 8.8 %collective-permute-start.3 = (f32[7,4,1,128]{3,2,0,1:T(1,128)S(1)}, f32[7,4,1,128]{3,2,0,1:T(1,128)S(1)}, u32[]{:S(2)}, u32[]{:S(2)}) collective-permute-start(f32[7,4,1,128]{3,2,0,1:T(1,128)S(1)} %get-tuple-element.999), channel_id=1, source_target_pairs={{1,0},{2,1},{3,2},{5,4},{6,5},{7,6},{9,8},{10,9},{11,10},{13,12},{... | collective-permute-start | bytes 43016 | tf_op jit(solution)/shard_map/ppermute | solution.py:23
  68.6 6.9 %copy-start.3 = (f32[4,3,16,128]{3,2,1,0:T(8,128)}, f32[4,3,16,128]{3,2,1,0:T(8,128)S(1)}, u32[]{:S(2)}) copy-start(f32[4,3,16,128]{3,2,1,0:T(8,128)S(1)} %get-tuple-element.663) | copy-start | bytes 294916
  68.6 6.8 %copy-start.6 = (f32[3]{0:T(128)S(1)}, f32[3]{0:T(128)}, u32[]{:S(2)}) copy-start(f32[3]{0:T(128)} %constant.274.clone..sunk.6) | copy-start | bytes 40
  68.6 6.8 %copy-start.7 = (f32[3]{0:T(128)S(1)}, f32[3]{0:T(128)}, u32[]{:S(2)}) copy-start(f32[3]{0:T(128)} %constant.275.clone..sunk.6) | copy-start | bytes 40
  68.6 6.7 %copy-start.8 = (f32[3]{0:T(128)S(1)}, f32[3]{0:T(128)}, u32[]{:S(2)}) copy-start(f32[3]{0:T(128)} %constant.276.clone..sunk.6) | copy-start | bytes 40
  68.6 6.7 %copy-start.9 = (f32[3]{0:T(128)S(1)}, f32[3]{0:T(128)}, u32[]{:S(2)}) copy-start(f32[3]{0:T(128)} %constant.277.clone..sunk.6) | copy-start | bytes 40
  68.6 6.7 %copy-start.10 = (f32[3]{0:T(128)S(1)}, f32[3]{0:T(128)}, u32[]{:S(2)}) copy-start(f32[3]{0:T(128)} %constant.279.clone..sunk.6) | copy-start | bytes 40
  68.7 6.7 %copy-start.11 = (f32[3]{0:T(128)S(1)}, f32[3]{0:T(128)}, u32[]{:S(2)}) copy-start(f32[3]{0:T(128)} %constant.280.clone..sunk.6) | copy-start | bytes 40
  69.8 48.4 %all-to-all-start.2 = ((f32[8,32,3,128]{3,1,2,0:T(8,128)}), f32[8,32,3,128]{3,1,2,0:T(8,128)S(1)}, u32[]{:S(2)}, u32[]{:S(2)}) async-start(f32[8,32,3,128]{3,1,2,0:T(8,128)} %fusion.38), calls=%async_computation.2 | async-start | bytes 786432 | tf_op jit(solution)/shard_map/all_to_all | solution.py:152
  75.4 42.8 %copy-start.14 = (f32[3]{0:T(128)S(1)}, f32[3]{0:T(128)}, u32[]{:S(2)}) copy-start(f32[3]{0:T(128)} %constant.283.clone) | copy-start | bytes 40
  120.1 26.9 %all-to-all-start.3 = ((f32[8,32,7,128]{3,1,2,0:T(8,128)}), f32[8,32,7,128]{3,1,2,0:T(8,128)S(1)}, u32[]{:S(2)}, u32[]{:S(2)}) async-start(f32[8,32,7,128]{3,1,2,0:T(8,128)} %fusion.46), calls=%async_computation.3 | async-start | bytes 1835008 | tf_op jit(solution)/shard_map/all_to_all | solution.py:135
  125.2 5.4 %collective-permute-start.4 = (f32[7,1,8,128]{3,2,1,0:T(8,128)S(1)}, f32[7,1,8,128]{3,2,1,0:T(8,128)S(1)}, u32[]{:S(2)}, u32[]{:S(2)}) collective-permute-start(f32[7,1,8,128]{3,2,1,0:T(8,128)S(1)} %get-tuple-element.1000), channel_id=1, source_target_pairs={{0,4},{4,8},{8,12},{12,16},{16,20},{20,24},{24,28},{1,5},{5,9},{9,... | collective-permute-start | bytes 86024 | tf_op jit(solution)/shard_map/ppermute | solution.py:20
  128.7 6.4 %collective-permute-start.5 = (f32[7,1,8,128]{3,2,1,0:T(8,128)S(1)}, f32[7,1,8,128]{3,2,1,0:T(8,128)S(1)}, u32[]{:S(2)}, u32[]{:S(2)}) collective-permute-start(f32[7,1,8,128]{3,2,1,0:T(8,128)S(1)} %get-tuple-element.1001), channel_id=1, source_target_pairs={{4,0},{8,4},{12,8},{16,12},{20,16},{24,20},{28,24},{5,1},{9,5},{13... | collective-permute-start | bytes 86024 | tf_op jit(solution)/shard_map/ppermute | solution.py:23
  135.1 10.6 %collective-permute-start.6 = (f32[7,4,1,128]{3,2,1,0:T(1,128)S(1)}, f32[7,4,1,128]{3,2,1,0:T(1,128)S(1)}, u32[]{:S(2)}, u32[]{:S(2)}) collective-permute-start(f32[7,4,1,128]{3,2,1,0:T(1,128)S(1)} %get-tuple-element.996), channel_id=1, source_target_pairs={{0,1},{1,2},{2,3},{4,5},{5,6},{6,7},{8,9},{9,10},{10,11},{12,13},{... | collective-permute-start | bytes 43016 | tf_op jit(solution)/shard_map/ppermute | solution.py:20
  138.2 8.7 %collective-permute-start.7 = (f32[7,4,1,128]{3,2,1,0:T(1,128)S(1)}, f32[7,4,1,128]{3,2,1,0:T(1,128)S(1)}, u32[]{:S(2)}, u32[]{:S(2)}) collective-permute-start(f32[7,4,1,128]{3,2,1,0:T(1,128)S(1)} %get-tuple-element.997), channel_id=1, source_target_pairs={{1,0},{2,1},{3,2},{5,4},{6,5},{7,6},{9,8},{10,9},{11,10},{13,12},{... | collective-permute-start | bytes 43016 | tf_op jit(solution)/shard_map/ppermute | solution.py:23
  174.1 49.0 %all-to-all-start.4 = ((f32[8,32,3,128]{3,1,2,0:T(8,128)}), f32[8,32,3,128]{3,1,2,0:T(8,128)S(1)}, u32[]{:S(2)}, u32[]{:S(2)}) async-start(f32[8,32,3,128]{3,1,2,0:T(8,128)} %fusion.36), calls=%async_computation.4 | async-start | bytes 786432 | tf_op jit(solution)/shard_map/all_to_all | solution.py:152
  179.7 42.8 %copy-start.4 = (f32[4,3,16,128]{3,2,1,0:T(8,128)S(1)}, f32[4,3,16,128]{3,2,1,0:T(8,128)}, u32[]{:S(2)}) copy-start(f32[4,3,16,128]{3,2,1,0:T(8,128)} %copy-done.3) | copy-start | bytes 294916
  (5 other events, 29.9 us)
where the time goes:
time: 226 us; the launch traced here: 224 us
  other arithmetic  114 us (50%)
  starting transfers between devices  48.7 us (22%)
  waiting for transfers between devices  23.3 us (10%)
  loops' own time  22.3 us (10%)
  matrix products  8.22 us (4%)
  local copies, waits for them, and re-layouts  6.05 us (3%)
    reduce_sum x16, other arithmetic, contact(): jnp.sum((own_vel[:, :, :, None] - other_vel[:, :, None, :]) * normal, axi...  32.2 us
    reduce_sum x8, other arithmetic, row_force(): total_force = total_force + jnp.sum(pushes, axis=3)  25.4 us
    another operation x2, loops' own time, particle_forces(): forces = lax.map(row_force, jnp.arange(stacked.shape[1], dtype=jnp.int32))  21.6 us
    reduce_sum x8, other arithmetic, tire_contact(): return (jnp.sum(pushes, axis=3), -jnp.sum(pushes, axis=2))  19.3 us
    reduce_sum x12, other arithmetic, contact(): distance = jnp.sqrt(jnp.sum(apart * apart, axis=0) + soften * soften)  13.4 us
    ppermute x4, starting transfers between devices, with_halo(): lax.ppermute(lax.slice_in_dim(block, block.shape[dim] - width, None, axis...  13.1 us
    mul x44, other arithmetic, contact(): intersection * (stiffness - damping * closing) * other_live[:, None, :]  12.5 us
    ppermute x4, waiting for transfers between devices, with_halo(): lax.ppermute(lax.slice_in_dim(block, 0, width, axis=dim), axis, backward)  11.2 us
  transfers between devices with their start and end apart: 13, of which 7 were waited for; matrix products, arithmetic and copies ran while one was open for 30% of the time, Pallas kernels for 0%

commit v1 on v0

v1 whole, which is shorter than its diff:
```python
import functools

import jax
import jax.numpy as jnp
from jax import lax
from jax.experimental import pallas as pl
from jax.experimental.pallas import tpu as pltpu
from jax.sharding import PartitionSpec as P

radius = 0.1
face_radius = 0.15
stiffness = 100.0
damping = 40.0
soften = 0.05
time_step = 0.02
gravity = 9.81

far = 1000.0
f32 = jnp.float32
bf16 = jnp.bfloat16
falls = (0.0, 0.0, -gravity)
VMEM = pltpu.VMEM
SMEM = pltpu.SMEM


def split3(a):
    high = a.astype(bf16).astype(f32)
    rest = a - high
    mid = rest.astype(bf16).astype(f32)
    return high, mid, rest - mid


def features(state, eps):
    row = lax.broadcasted_iota(jnp.int32, state.shape, 0)
    turned = pltpu.roll(state, 5, 0)
    square = jnp.sum(jnp.where(row < 3, state * state, 0.0), axis=0, keepdims=True) + eps
    cross = jnp.sum(jnp.where(row < 3, state * turned, 0.0), axis=0, keepdims=True)
    full = jnp.where(row == 6, square, jnp.where(row == 7, cross, state))
    return split3(full), row


def left_side(pieces, row):
    p1, p2, p3 = pieces
    ones = jnp.where(row >= 6, 1.0, 0.0)
    zero = jnp.zeros_like(p1)
    stack = jnp.concatenate([p1, p1, p2, p1, p3, p2, ones, ones, ones, zero], axis=0)
    return jnp.transpose(stack).astype(bf16)


def right_side(pieces, row):
    def for_square(p, first):
        return jnp.where(row < 3, -2.0 * p, jnp.where(row == 6, 1.0 if first else 0.0, 0.0))

    def for_closing(p, first):
        swapped = jnp.where(row < 3, pltpu.roll(p, 5, 0), pltpu.roll(p, 3, 0))
        return jnp.where(row < 6, -swapped, jnp.where(row == 7, 1.0 if first else 0.0, 0.0))

    halves = []
    for side, keep in ((for_square, 6), (for_closing, 7)):
        b1, b2, b3 = [side(p, k == 0) for k, p in enumerate(pieces)]
        q = [jnp.where(row == keep, p, 0.0) for p in pieces]
        halves.append(jnp.concatenate([b1, b2, b1, b3, b1, b2] + q + [jnp.zeros_like(b1)], axis=0))
    return jnp.concatenate(halves, axis=1).astype(bf16)


def sum_side(pieces):
    p1, p2, p3 = pieces
    stack = jnp.concatenate([p1, p2, p3, jnp.ones_like(p1)], axis=0).astype(bf16)
    return jnp.concatenate([stack, stack], axis=1)


def pair_weights(product, reach):
    n = product.shape[1] // 2
    square = jnp.maximum(product[:, :n], soften * soften * 0.5)
    inverse = lax.rsqrt(square)
    weight = jnp.maximum(reach * inverse - 1.0, 0.0) * (
        stiffness / damping - product[:, n:] * inverse
    )
    high = weight.astype(bf16)
    low = (weight - high.astype(f32)).astype(bf16)
    return high, low


def dot(a, b, contract=((1,), (0,))):
    return lax.dot_general(a, b, (contract, ((), ())), preferred_element_type=f32)


def moment(state, sums):
    total = sums[0:8] + sums[8:16] + sums[16:24]
    return state * sums[24:25] - total


def advanced(x, v, force, axis):
    v = v + time_step * (force + falls[axis])
    return x + time_step * v, v


def put_own(state_ref, x_ref, v_ref, ct, cc):
    cells = lax.broadcasted_iota(jnp.int32, (cc, 128), 0).astype(f32)
    for r in range(ct):
        base = ((r + 1) * (cc + 2) + 1) * 8
        for axis in range(3):
            x = x_ref[axis, pl.ds(r * cc, cc), :]
            if axis == 0:
                x = x + (r + 1 - (ct + 1) / 2)
            if axis == 1:
                x = x + (cells + (1 - (cc + 1) / 2))
            state_ref[pl.ds(base + axis, cc, stride=8), :] = x
            state_ref[pl.ds(base + 3 + axis, cc, stride=8), :] = v_ref[axis, pl.ds(r * cc, cc), :]


def put_dead(state_ref, slot):
    row = lax.broadcasted_iota(jnp.int32, (8, 128), 0)
    state_ref[pl.ds(slot * 8, 8), :] = jnp.where(row == 0, far, 0.0)


def build_left(state_ref, left_ref, sum_ref, slots):
    for slot in slots:
        pieces, row = features(state_ref[pl.ds(slot * 8, 8), :], 0.0)
        left_ref[slot] = left_side(pieces, row)
        sum_ref[slot] = sum_side(pieces)


def build_right(state_ref, right_ref, slots):
    for k, slot in enumerate(slots):
        pieces, row = features(state_ref[pl.ds(slot * 8, 8), :], soften * soften)
        right_ref[k] = right_side(pieces, row)


def pushes(left_ref, sum_ref, right, others):
    total = None
    for slot in others:
        high, low = pair_weights(dot(left_ref[slot], right), 2.0 * radius)
        part = dot(sum_ref[slot], jnp.concatenate([high, low], axis=0))
        total = part if total is None else total + part
    return total


def store_rows(out_ref, values, index, add):
    for axis in range(3):
        line = damping * values[axis : axis + 1]
        if add:
            line = line + out_ref[axis, pl.ds(index, 1), :]
        out_ref[axis, pl.ds(index, 1), :] = line


def inner_kernel(ct, cc, x_ref, v_ref, out_ref, state_ref, left_ref, sum_ref, right_ref):
    wide = cc + 2
    own = [(r + 1) * wide + c + 1 for r in range(ct) for c in range(cc)]
    ends = [(r + 1) * wide + c for r in range(ct) for c in (0, cc + 1)]
    put_own(state_ref, x_ref, v_ref, ct, cc)
    for slot in ends:
        put_dead(state_ref, slot)
    build_left(state_ref, left_ref, sum_ref, own + ends)
    build_right(state_ref, right_ref, own)

    def column(c, carry):
        for r in range(ct):
            others = [
                (q + 1) * wide + c + d
                for q in range(max(r - 1, 0), min(r + 2, ct))
                for d in range(3)
            ]
            sums = pushes(left_ref, sum_ref, right_ref[r * cc + c], others)
            state = state_ref[pl.ds(pl.multiple_of(((r + 1) * wide + c + 1) * 8, 8), 8), :]
            store_rows(out_ref, moment(state, sums), r * cc + c, False)
        return carry

    lax.fori_loop(0, cc, column, 0)


def outer_kernel(ct, cc, crosses, second, s_ref, x_ref, v_ref, all_ref, halo_ref, *rest):
    if second:
        force_ref, halo_force_ref, *rest = rest
    out_ref, state_ref, left_ref, sum_ref, right_ref = rest
    wide = cc + 2
    c_index = s_ref[0]
    own_track = s_ref[1]
    has_low = c_index > 0
    has_high = c_index < crosses - 1
    put_own(state_ref, x_ref, v_ref, ct, cc)

    def place(slot, rr, p, load, ok):
        for axis in range(3):
            x, v = load(axis, 6, 0), load(axis + 3, 6, 0)
            if second:
                x, v = advanced(x, v, load(axis, 3, 1), axis)
            if axis == 0:
                x = x + (rr - (ct + 1) / 2)
                x = jnp.where(ok, x, far)
            if axis == 1:
                x = jnp.where(ok, x + (p - (cc + 1) / 2), 0.0)
            state_ref[pl.ds(slot * 8 + axis, 1), :] = x
            state_ref[pl.ds(slot * 8 + 3 + axis, 1), :] = jnp.where(ok, v, 0.0)

    def from_all(track, row, p):
        shift = -1 if p == 0 else (1 if p == cc + 1 else 0)
        device = track * crosses + jnp.clip(c_index + shift, 0, crosses - 1)
        cell = row * cc + (p - 1) % cc
        refs = (all_ref, force_ref) if second else (all_ref,)
        return lambda f, n, k: refs[k][device, f, pl.ds(cell, 1), :]

    def from_halo(p):
        refs = (halo_ref, halo_force_ref) if second else (halo_ref,)
        return lambda f, n, k: refs[k][pl.ds(p * n + f, 1), :]

    for rr, row, at in ((0, ct - 1, 2), (ct + 1, 0, 5)):
        inside, track, exists = s_ref[at] > 0, s_ref[at + 1], s_ref[at + 2] > 0
        for p in range(wide):
            a, b = from_all(track, row, p), from_halo(p)

            def load(f, n, k, a=a, b=b):
                return jnp.where(inside, a(f, n, k), b(f, n, k))

            ok = exists
            if p == 0:
                ok = jnp.logical_and(ok, has_low)
            if p == cc + 1:
                ok = jnp.logical_and(ok, has_high)
            place(rr * wide + p, rr, p, load, ok)
    for r in range(ct):
        place((r + 1) * wide, r + 1, 0, from_all(own_track, r, 0), has_low)
        place((r + 1) * wide + cc + 1, r + 1, cc + 1, from_all(own_track, r, cc + 1), has_high)
    ring = [rr * wide + p for rr in (0, ct + 1) for p in range(wide)]
    ring += [(r + 1) * wide + p for r in range(ct) for p in (0, cc + 1)]
    build_left(state_ref, left_ref, sum_ref, ring)
    build_right(state_ref, right_ref, [(r + 1) * wide + c + 1 for r in range(ct) for c in range(cc)])

    def one(r, c, others, add):
        sums = pushes(left_ref, sum_ref, right_ref[r * cc + c], others)
        start = ((r + 1) * wide + c + 1) * 8
        state = state_ref[pl.ds(start if add else pl.multiple_of(start, 8), 8), :]
        store_rows(out_ref, moment(state, sums), r * cc + c, add)

    if ct > 2:
        out_ref[...] = jnp.zeros_like(out_ref)

    def column(c, carry):
        one(0, c, [c + d for d in range(3)], False)
        one(ct - 1, c, [(ct + 1) * wide + c + d for d in range(3)], ct == 1)
        return carry

    lax.fori_loop(0, cc, column, 0)
    for r in range(ct):
        near = range(max(r - 1, 0), min(r + 2, ct))
        one(r, 0, [(q + 1) * wide for q in near], True)
        one(r, cc - 1, [(q + 1) * wide + cc + 1 for q in near], True)


def face_kernel(second, index_ref, offset_ref, velocity_ref, all_ref, *rest):
    if second:
        force_ref, *rest = rest
    part_ref, react_ref, state_ref, face_ref = rest
    devices, _, cells, _ = all_ref.shape
    count = offset_ref.shape[0]

    def spread(device, carry):
        base = pl.multiple_of(device * cells * 8, 8)
        for axis in range(3):
            x, v = all_ref[device, axis], all_ref[device, axis + 3]
            if second:
                x, v = advanced(x, v, force_ref[device, axis], axis)
            state_ref[pl.ds(base + axis, cells, stride=8), :] = x
            state_ref[pl.ds(base + 3 + axis, cells, stride=8), :] = v
            part_ref[device, axis] = jnp.zeros_like(x)
        return carry

    lax.fori_loop(0, devices, spread, 0)
    for axis in range(3):
        y, w = offset_ref[:, axis, :], velocity_ref[:, axis, :]
        if second:
            y = y + time_step * w
        face_ref[pl.ds(axis, count, stride=8), :] = y
        face_ref[pl.ds(3 + axis, count, stride=8), :] = w

    def one(f):
        block = index_ref[f]
        state = state_ref[pl.ds(pl.multiple_of(block * 8, 8), 8), :]
        face = face_ref[pl.ds(pl.multiple_of(f * 8, 8), 8), :]
        pieces, row = features(state, soften * soften)
        face_pieces, _ = features(face, 0.0)
        product = dot(left_side(face_pieces, row), right_side(pieces, row))
        high, low = pair_weights(product, radius + face_radius)
        onto = moment(state, dot(sum_side(face_pieces), jnp.concatenate([high, low], axis=0)))
        back = moment(
            face, dot(sum_side(pieces), jnp.concatenate([high, low], axis=1), ((1,), (1,)))
        )
        react_ref[f] = (time_step * damping * back)[0:3]
        return block, onto

    group = 4 if count % 4 == 0 else 1

    def several(g, carry):
        done = [one(g * group + k) for k in range(group)]
        for block, onto in done:
            device, cell = block // cells, block % cells
            for axis in range(3):
                line = part_ref[device, axis, pl.ds(cell, 1), :]
                part_ref[device, axis, pl.ds(cell, 1), :] = line + damping * onto[axis : axis + 1]
        return carry

    lax.fori_loop(0, count // group, several, 0)


def pack_kernel(cc, s_ref, mine_ref, out_ref):
    crosses, fields, _, _ = mine_ref.shape
    c_index, row = s_ref[0], s_ref[8]
    for p in range(cc + 2):
        shift = -1 if p == 0 else (1 if p == cc + 1 else 0)
        device = jnp.clip(c_index + shift, 0, crosses - 1)
        cell = row * cc + (p - 1) % cc
        for f in range(fields):
            out_ref[pl.ds(p * fields + f, 1), :] = mine_ref[device, f, pl.ds(cell, 1), :]


def call(kernel, name, args, scalars, outs, scratch, flops):
    specs = [pl.BlockSpec(memory_space=SMEM)] * scalars
    specs += [pl.BlockSpec(memory_space=VMEM)] * (len(args) - scalars)
    return pl.pallas_call(
        kernel,
        name=name,
        out_shape=[jax.ShapeDtypeStruct(s, f32) for s in outs],
        in_specs=specs,
        out_specs=[pl.BlockSpec(memory_space=VMEM)] * len(outs),
        scratch_shapes=scratch,
        cost_estimate=pl.CostEstimate(flops=flops, transcendentals=0, bytes_accessed=0),
    )(*args)


def body(
    particle_offset,
    particle_velocity,
    cell_count,
    face_offset,
    face_velocity,
    face_route,
    face_cell,
):
    _, ct, cc, slots = particle_offset.shape
    cells = ct * cc
    own_faces, _, faces = face_offset.shape
    vehicles, tracks, crosses = [lax.axis_size(a) for a in ("vehicle", "track", "cross")]
    vehicle, track, cross = [lax.axis_index(a) for a in ("vehicle", "track", "cross")]
    pair = tracks == 2
    wide = cc + 2
    grid_slots = (ct + 2) * wide
    ring_slots = [
        VMEM((grid_slots * 8, slots), f32),
        VMEM((grid_slots, slots, 80), bf16),
        VMEM((grid_slots, 32, 2 * slots), bf16),
        VMEM((cells, 80, 2 * slots), bf16),
    ]

    x = particle_offset.reshape(3, cells, slots)
    v = particle_velocity.reshape(3, cells, slots)
    live = (
        lax.broadcasted_iota(jnp.int32, (cells, slots), 1) < cell_count.reshape(cells)[:, None]
    )
    first = lax.broadcasted_iota(jnp.int32, (3, 1, 1), 0) == 0

    def marked(x):
        return jnp.where(first & ~live[None], far, x)

    def place(t):
        return jnp.bitwise_xor(t, track) if pair else t

    low, high = track > 0, track < tracks - 1
    target = face_route[:, 0]
    index = (place(target // crosses) * crosses + target % crosses) * cells + face_cell
    scalars = jnp.stack(
        [
            cross,
            place(track),
            low,
            place(jnp.maximum(track - 1, 0)),
            low | (vehicle > 0),
            high,
            place(jnp.minimum(track + 1, tracks - 1)),
            high | (vehicle < vehicles - 1),
            jnp.where(high, 0, ct - 1),
        ]
    ).astype(jnp.int32)
    swap = [(0, 1), (1, 0)]
    travel = []
    for e in range(vehicles - 1):
        last, following = e * tracks + tracks - 1, (e + 1) * tracks
        travel += [(last, following), (following, last)]

    def gather_cross(a):
        spread = jnp.broadcast_to(a[None], (crosses,) + a.shape)
        return lax.all_to_all(spread, "cross", split_axis=0, concat_axis=0, tiled=True)

    def gather_track(a):
        if pair:
            return jnp.concatenate([a, lax.ppermute(a, "track", swap)], axis=0)
        return lax.all_gather(a, "track", axis=0, tiled=True)

    def halo(a):
        packed = call(
            functools.partial(pack_kernel, cc),
            "pack",
            [scalars, a],
            1,
            [(wide * a.shape[1], slots)],
            [],
            1000,
        )[0]
        return lax.ppermute(packed, ("vehicle", "track"), travel)

    def scatter_force(part):
        part = part.reshape(tracks, crosses, 3, cells, slots)
        if pair:
            part = part[0] + lax.ppermute(part[1], "track", swap)
        else:
            part = jnp.sum(lax.all_to_all(part, "track", 0, 0, tiled=True), axis=0)
        return jnp.sum(lax.all_to_all(part, "cross", 0, 0, tiled=True), axis=0)

    fall = jnp.array(falls, f32)[:, None, None]
    reaction = None
    everyone = beyond = None
    force = None
    for substep in range(2):
        second = substep == 1
        own = marked(x)
        mine = gather_cross(force if second else jnp.concatenate([own, v], axis=0))
        inner = call(
            functools.partial(inner_kernel, ct, cc),
            "inner",
            [own, v],
            0,
            [(3, cells, slots)],
            ring_slots,
            4 * 10**9,
        )[0]
        group, across = gather_track(mine), halo(mine)
        if second:
            extra, halo_extra = [group], [across]
        else:
            everyone, beyond, extra, halo_extra = group, across, [], []
        part, react = call(
            functools.partial(face_kernel, second),
            "faces",
            [index, face_offset, face_velocity, everyone] + extra,
            1,
            [(tracks * crosses, 3, cells, slots), (own_faces, 3, faces)],
            [
                VMEM((tracks * crosses * cells * 8, slots), f32),
                VMEM((own_faces * 8, faces), f32),
            ],
            4 * 10**9,
        )
        outer = call(
            functools.partial(outer_kernel, ct, cc, crosses, second),
            "outer",
            [scalars, own, v, everyone, beyond] + extra + halo_extra,
            1,
            [(3, cells, slots)],
            ring_slots,
            4 * 10**9,
        )[0]
        force = jnp.where(live[None], inner + outer, 0.0) + scatter_force(part)
        v = v + time_step * (force + fall)
        x = x + time_step * v
        reaction = react if reaction is None else reaction + react
    shape = particle_offset.shape
    return (x.reshape(shape), v.reshape(shape), reaction)


def solution(mesh):
    in_specs = (
        P(None, ("vehicle", "track"), "cross", None),
        P(None, ("vehicle", "track"), "cross", None),
        P(("vehicle", "track"), "cross"),
        P(("vehicle", "track", "cross"), None, None),
        P(("vehicle", "track", "cross"), None, None),
        P(("vehicle", "track", "cross"), None),
        P(("vehicle", "track", "cross")),
    )
    out_specs = (
        P(None, ("vehicle", "track"), "cross", None),
        P(None, ("vehicle", "track"), "cross", None),
        P(("vehicle", "track", "cross"), None, None),
    )
    return jax.shard_map(body, mesh=mesh, in_specs=in_specs, out_specs=out_specs, check_vma=False)
```

time: 226 us -> 141 us (0.62)
  other arithmetic: 114 us -> 4.25 us
  Pallas kernels: 0 us -> 85.8 us
  starting transfers between devices: 48.7 us -> 23.4 us
  loops' own time: 22.3 us -> 0 us
  waiting for transfers between devices: 23.3 us -> 5.82 us
  blocking collectives: 0 us -> 9.32 us
  matrix products: 8.22 us -> 0 us
  local copies, waits for them, and re-layouts: 6.05 us -> 11 us
    reduce_sum x46 -> x2, other arithmetic: 91.3 us -> 0.02 us  [scatter_force(): return jnp.sum(lax.all_to_all(part, 'cross', 0, 0, tiled=True), axis=0)]
    pallas_call x0 -> x8, Pallas kernels: none -> 85.8 us  [call(): pl.pallas_call(kernel, name=name, out_shape=[jax.ShapeDtypeStruct(s, f32)...]
    another operation x4 -> x0, loops' own time: 22.3 us -> none  [the longest x2 21.6 us: particle_forces(): forces = lax.map(row_force, jnp.arange(stacked.shape[1], dtype=jnp.int32))]
    ppermute x8 -> x6, waiting for transfers between devices: 20.4 us -> 0.84 us  [the longest x2 0.83 us: gather_track(): return jnp.concatenate([a, lax.ppermute(a, 'track', swap)], axis=0)]
    all_to_all x5 -> x3, starting transfers between devices: 27.2 us -> 13.4 us  [the longest x2 8.49 us: scatter_force(): return jnp.sum(lax.all_to_all(part, 'cross', 0, 0, tiled=True), axis=0)]
    mul x45 -> x0, other arithmetic: 12.5 us -> none  [the longest x44 12.5 us: contact(): intersection * (stiffness - damping * closing) * other_live[:, None, :]]
    ppermute x8 -> x6, starting transfers between devices: 21.5 us -> 9.98 us  [the longest x2 6.84 us: halo(): return lax.ppermute(packed, ('vehicle', 'track'), travel)]
    all_to_all x0 -> x1, blocking collectives: none -> 9.32 us  [gather_cross(): lax.all_to_all(spread, 'cross', split_axis=0, concat_axis=0, tiled=True)]
  transfers between devices with their start and end apart: 13 -> 9, of which waited for: 7 -> 2; matrix products, arithmetic and copies ran while one was open for 30% -> 3% of each run, Pallas kernels for 0% -> 37%
where the time goes in v1:
time: 141 us; the launch traced here: 140 us
  Pallas kernels  85.8 us (61%)
  starting transfers between devices  23.4 us (17%)
  local copies, waits for them, and re-layouts  11 us (8%)
  blocking collectives  9.32 us (7%)
  waiting for transfers between devices  5.82 us (4%)
  other arithmetic  4.25 us (3%)
    pallas_call x8, Pallas kernels, call(): pl.pallas_call(kernel, name=name, out_shape=[jax.ShapeDtypeStruct(s, f32)...  85.8 us
    all_to_all x1, blocking collectives, gather_cross(): lax.all_to_all(spread, 'cross', split_axis=0, concat_axis=0, tiled=True)  9.32 us
    all_to_all x2, starting transfers between devices, scatter_force(): return jnp.sum(lax.all_to_all(part, 'cross', 0, 0, tiled=True), axis=0)  8.49 us
    unnamed x55, local copies, waits for them, and re-layouts  7.79 us
    ppermute x2, starting transfers between devices, halo(): return lax.ppermute(packed, ('vehicle', 'track'), travel)  6.84 us
    all_to_all x1, waiting for transfers between devices, gather_cross(): lax.all_to_all(spread, 'cross', split_axis=0, concat_axis=0, tiled=True)  4.98 us
    all_to_all x1, starting transfers between devices, gather_cross(): lax.all_to_all(spread, 'cross', split_axis=0, concat_axis=0, tiled=True)  4.89 us
  transfers between devices with their start and end apart: 9, of which 2 were waited for; matrix products, arithmetic and copies ran while one was open for 3% of the time, Pallas kernels for 37%

profile of v1, /device:TPU:11, one launch (start us, length us, event | category | flops | bytes accessed | tf_op | source)
XLA Modules:
  0.0 140.4 jit_solution(13364930279952616726)
XLA Ops:
  1.5 0.8 and_select_fusion.1.x_ref
  3.6 4.9 %all-to-all-start = ((f32[4,6,16,128]{3,2,1,0:T(8,128)}), f32[4,6,16,128]{3,2,1,0:T(8,128)S(1)}, u32[]{:S(2)}, u32[]{:S(2)}) async-start(f32[4,6,16,128]{3,2,1,0:T(8,128)} %broadcast_in_dim.40), calls=%async_computation | async-start | bytes 393216 | tf_op jit(solution)/shard_map/all_to_all | solution.py:391
  8.5 5.0 %all-to-all-done.mine_ref = f32[4,6,16,128]{3,2,1,0:T(8,128)S(1)} async-done(((f32[4,6,16,128]{3,2,1,0:T(8,128)}), f32[4,6,16,128]{3,2,1,0:T(8,128)S(1)}, u32[]{:S(2)}, u32[]{:S(2)}) %all-to-all-start) | async-done | bytes 196640 | tf_op jit(solution)/shard_map/all_to_all | solution.py:391
  13.5 2.2 %collective-permute-start = (f32[4,6,16,128]{3,2,1,0:T(8,128)S(1)}, f32[4,6,16,128]{3,2,1,0:T(8,128)S(1)}, u32[]{:S(2)}, u32[]{:S(2)}) collective-permute-start(f32[4,6,16,128]{3,2,1,0:T(8,128)S(1)} %all-to-all-done.mine_ref), channel_id=1, source_target_pairs={{0,4},{4,0},{1,5},{5,1},{2,6},{6,2},{3,7},{7,3},{8,12},{12,8},{9,1... | collective-permute-start | bytes 589832 | tf_op jit(solution)/shard_map/ppermute | solution.py:395
  16.3 0.7 copy.11.offset_ref
  17.2 0.7 copy.12.velocity_ref
  18.6 0.7 copy-done.9
  19.3 16.8 %faces.2 = (f32[8,3,16,128]{3,2,1,0:T(8,128)}, f32[64,3,128]{2,1,0:T(4,128)}) custom-call(s32[64]{0:T(128)} %multiply_add_fusion.2.index_ref, f32[64,3,128]{2,1,0:T(4,128)} %copy.11.offset_ref, f32[64,3,128]{2,1,0:T(4,128)} %copy.12.velocity_ref, f32[8,6,16,128]{3,2,1,0:T(8,128)} %copy-done.9), custom_call_target="tpu_custom_call" | custom-call | flops 4000000000 | tf_op jit(solution)/shard_map/faces/pallas_call | solution.py:319
  36.1 0.9 slice.17
  37.1 15.7 %inner.2 = f32[3,16,128]{2,1,0:T(8,128)} custom-call(f32[3,16,128]{2,1,0:T(8,128)} %copy-done.12, f32[3,16,128]{2,1,0:T(8,128)} %bitcast.34), custom_call_target="tpu_custom_call" | custom-call | flops 4000000000 | tf_op jit(solution)/shard_map/inner/pallas_call | solution.py:319
  52.8 1.6 %pack.2 = f32[60,128]{1,0:T(8,128)} custom-call(s32[9]{0:T(128)} %stack.51.s_ref, f32[4,6,16,128]{3,2,1,0:T(8,128)} %copy-done), custom_call_target="tpu_custom_call" | custom-call | flops 1000 | tf_op jit(solution)/shard_map/pack/pallas_call | solution.py:319
  54.4 3.4 %collective-permute-start.1 = (f32[60,128]{1,0:T(8,128)}, f32[60,128]{1,0:T(8,128)S(1)}, u32[]{:S(2)}, u32[]{:S(2)}) collective-permute-start(f32[60,128]{1,0:T(8,128)} %pack.2), channel_id=1, source_target_pairs={{4,8},{8,4},{12,16},{16,12},{20,24},{24,20},{5,9},{9,5},{13,17},{1... | collective-permute-start | bytes 92168 | tf_op jit(solution)/shard_map/ppermute | solution.py:408
  58.5 4.5 %all-to-all-start.1 = ((f32[4,3,16,128]{3,2,1,0:T(8,128)}), f32[4,3,16,128]{3,2,1,0:T(8,128)S(1)}, u32[]{:S(2)}, u32[]{:S(2)}) async-start(f32[4,3,16,128]{3,2,1,0:T(8,128)} %slice_add_fusion.1), calls=%async_computation.1 | async-start | bytes 196608 | tf_op jit(solution)/shard_map/all_to_all | solution.py:416
  63.7 8.7 %outer.2 = f32[3,16,128]{2,1,0:T(8,128)} custom-call(s32[9]{0:T(128)} %stack.51.s_ref, f32[3,16,128]{2,1,0:T(8,128)} %copy-done.12, f32[3,16,128]{2,1,0:T(8,128)} %bitcast.35, f32[8,6,16,128]{3,2,1,0:T(8,128)} %copy-done.9, f32[60,128]{1,0:T(8,128)} %copy-done.22), custom_call_target="tpu_custom_call" | custom-call | flops 4000000000 | tf_op jit(solution)/shard_map/outer/pallas_call | solution.py:319
  73.9 9.3 %all_to_all.20.mine_ref = f32[4,3,16,128]{3,2,1,0:T(8,128)S(1)} all-to-all(f32[4,3,16,128]{3,2,1,0:T(8,128)S(1)} %broadcast_in_dim.42), channel_id=1, replica_groups=mesh['vehicle'=4,'track'=2,'cross'=4] {'cross'}, dimensions={0} | all-to-all | bytes 196608 | tf_op jit(solution)/shard_map/all_to_all | solution.py:391
  83.8 0.8 collective-permute-done.3
  85.3 16.9 %faces.3 = (f32[8,3,16,128]{3,2,1,0:T(8,128)}, f32[64,3,128]{2,1,0:T(4,128)}) custom-call(s32[64]{0:T(128)} %multiply_add_fusion.2.index_ref, f32[64,3,128]{2,1,0:T(4,128)} %copy.11.offset_ref, f32[64,3,128]{2,1,0:T(4,128)} %copy.12.velocity_ref, f32[8,6,16,128]{3,2,1,0:T(8,128)} %copy-done.9, f32[8,3,16,128]{3,2,1,0:T(8,128)} %copy-done.14), custom_call_target="tpu_custom_call" | custom-call | flops 4000000000 | tf_op jit(solution)/shard_map/faces/pallas_call | solution.py:319
  102.3 0.9 slice.19
  103.5 15.7 %inner.3 = f32[3,16,128]{2,1,0:T(8,128)} custom-call(f32[3,16,128]{2,1,0:T(8,128)} %get-tuple-element.16.x_ref, f32[3,16,128]{2,1,0:T(8,128)} %get-tuple-element.17.v_ref), custom_call_target="tpu_custom_call" | custom-call | flops 4000000000 | tf_op jit(solution)/shard_map/inner/pallas_call | solution.py:319
  119.3 1.5 %pack.3 = f32[30,128]{1,0:T(8,128)} custom-call(s32[9]{0:T(128)} %stack.51.s_ref, f32[4,3,16,128]{3,2,1,0:T(8,128)} %copy-done.1), custom_call_target="tpu_custom_call" | custom-call | flops 1000 | tf_op jit(solution)/shard_map/pack/pallas_call | solution.py:319
  120.8 3.4 %collective-permute-start.4 = (f32[30,128]{1,0:T(8,128)}, f32[30,128]{1,0:T(8,128)S(1)}, u32[]{:S(2)}, u32[]{:S(2)}) collective-permute-start(f32[30,128]{1,0:T(8,128)} %pack.3), channel_id=1, source_target_pairs={{4,8},{8,4},{12,16},{16,12},{20,24},{24,20},{5,9},{9,5},{13,17},{1... | collective-permute-start | bytes 46088 | tf_op jit(solution)/shard_map/ppermute | solution.py:408
  124.9 3.9 %all-to-all-start.3 = ((f32[4,3,16,128]{3,2,1,0:T(8,128)}), f32[4,3,16,128]{3,2,1,0:T(8,128)S(1)}, u32[]{:S(2)}, u32[]{:S(2)}) async-start(f32[4,3,16,128]{3,2,1,0:T(8,128)} %slice_add_fusion), calls=%async_computation.3 | async-start | bytes 196608 | tf_op jit(solution)/shard_map/all_to_all | solution.py:416
  129.4 8.8 %outer.3 = f32[3,16,128]{2,1,0:T(8,128)} custom-call(s32[9]{0:T(128)} %stack.51.s_ref, f32[3,16,128]{2,1,0:T(8,128)} %get-tuple-element.16.x_ref, f32[3,16,128]{2,1,0:T(8,128)} %get-tuple-element.17.v_ref, f32[8,6,16,128]{3,2,1,0:T(8,128)} %copy-done.9, f32[60,128]{1,0:T(8,128)} %copy-done.22, f32[8,3,16,128]{3,2,1,0:T(8,128)} %copy-done.14, ...), custom_call_target="tpu_custom_call" | custom-call | flops 4000000000 | tf_op jit(solution)/shard_map/outer/pallas_call | solution.py:319
  138.9 0.7 copy-done.13
  (78 shorter events, 10.7 us)
Async XLA Ops:
  1.5 0.8 copy-start.10
  3.6 12.7 %copy-start.7 = (f32[64,3,128]{2,0,1:T(8,128)S(1)}, f32[64,3,128]{2,0,1:T(8,128)}, u32[]{:S(2)}) copy-start(f32[64,3,128]{2,0,1:T(8,128)} %param.11) | copy-start | bytes 294916
  3.6 9.9 %all-to-all-start = ((f32[4,6,16,128]{3,2,1,0:T(8,128)}), f32[4,6,16,128]{3,2,1,0:T(8,128)S(1)}, u32[]{:S(2)}, u32[]{:S(2)}) async-start(f32[4,6,16,128]{3,2,1,0:T(8,128)} %broadcast_in_dim.40), calls=%async_computation | async-start | bytes 393216 | tf_op jit(solution)/shard_map/all_to_all | solution.py:391
  8.5 7.2 %copy-start.20 = (s32[64]{0:T(128)S(1)}, s32[64]{0:T(128)}, u32[]{:S(2)}) copy-start(s32[64]{0:T(128)} %param.14) | copy-start | bytes 772
  8.5 7.2 %copy-start.21 = (s32[64,1]{0,1:T(1,128)S(1)}, s32[64,1]{0,1:T(1,128)}, u32[]{:S(2)}) copy-start(s32[64,1]{0,1:T(1,128)} %param.13) | copy-start | bytes 772
  13.5 5.1 %copy-start = (f32[4,6,16,128]{3,2,1,0:T(8,128)}, f32[4,6,16,128]{3,2,1,0:T(8,128)S(1)}, u32[]{:S(2)}) copy-start(f32[4,6,16,128]{3,2,1,0:T(8,128)S(1)} %all-to-all-done.mine_ref) | copy-start | bytes 589828
  13.5 5.1 %collective-permute-start = (f32[4,6,16,128]{3,2,1,0:T(8,128)S(1)}, f32[4,6,16,128]{3,2,1,0:T(8,128)S(1)}, u32[]{:S(2)}, u32[]{:S(2)}) collective-permute-start(f32[4,6,16,128]{3,2,1,0:T(8,128)S(1)} %all-to-all-done.mine_ref), channel_id=1, source_target_pairs={{0,4},{4,0},{1,5},{5,1},{2,6},{6,2},{3,7},{7,3},{8,12},{12,8},{9,1... | collective-permute-start | bytes 589832 | tf_op jit(solution)/shard_map/ppermute | solution.py:395
  16.3 0.9 copy-start.8
  37.0 20.8 %collective-permute-start.2 = (f32[4,3,16,128]{3,2,1,0:T(8,128)S(1)}, f32[4,3,16,128]{3,2,1,0:T(8,128)S(1)}, u32[]{:S(2)}, u32[]{:S(2)}) collective-permute-start(f32[4,3,16,128]{3,2,1,0:T(8,128)S(1)} %slice.17), channel_id=1, source_target_pairs={{0,4},{4,0},{1,5},{5,1},{2,6},{6,2},{3,7},{7,3},{8,12},{12,8},{9,1... | collective-permute-start | bytes 294920 | tf_op jit(solution)/shard_map/ppermute | solution.py:413
  52.8 5.1 %copy-start.4 = (f32[8,3,16,128]{3,2,1,0:T(8,128)S(1)}, f32[8,3,16,128]{3,2,1,0:T(8,128)}, u32[]{:S(2)}) copy-start(f32[8,3,16,128]{3,2,1,0:T(8,128)} %get-tuple-element.7) | copy-start | bytes 589828
  54.4 8.7 %collective-permute-start.1 = (f32[60,128]{1,0:T(8,128)}, f32[60,128]{1,0:T(8,128)S(1)}, u32[]{:S(2)}, u32[]{:S(2)}) collective-permute-start(f32[60,128]{1,0:T(8,128)} %pack.2), channel_id=1, source_target_pairs={{4,8},{8,4},{12,16},{16,12},{20,24},{24,20},{5,9},{9,5},{13,17},{1... | collective-permute-start | bytes 92168 | tf_op jit(solution)/shard_map/ppermute | solution.py:408
  58.5 13.9 %all-to-all-start.1 = ((f32[4,3,16,128]{3,2,1,0:T(8,128)}), f32[4,3,16,128]{3,2,1,0:T(8,128)S(1)}, u32[]{:S(2)}, u32[]{:S(2)}) async-start(f32[4,3,16,128]{3,2,1,0:T(8,128)} %slice_add_fusion.1), calls=%async_computation.1 | async-start | bytes 196608 | tf_op jit(solution)/shard_map/all_to_all | solution.py:416
  72.4 0.8 copy-start.11
  72.4 0.8 copy-start.15
  72.4 0.8 copy-start.16
  83.2 1.5 %collective-permute-start.3 = (f32[4,3,16,128]{3,2,1,0:T(8,128)S(1)}, f32[4,3,16,128]{3,2,1,0:T(8,128)S(1)}, u32[]{:S(2)}, u32[]{:S(2)}) collective-permute-start(f32[4,3,16,128]{3,2,1,0:T(8,128)S(1)} %all_to_all.20.mine_ref), channel_id=1, source_target_pairs={{0,4},{4,0},{1,5},{5,1},{2,6},{6,2},{3,7},{7,3},{8,12},{12,8},{9,1... | collective-permute-start | bytes 294920 | tf_op jit(solution)/shard_map/ppermute | solution.py:395
  103.2 21.0 %collective-permute-start.5 = (f32[4,3,16,128]{3,2,1,0:T(8,128)S(1)}, f32[4,3,16,128]{3,2,1,0:T(8,128)S(1)}, u32[]{:S(2)}, u32[]{:S(2)}) collective-permute-start(f32[4,3,16,128]{3,2,1,0:T(8,128)S(1)} %slice.19), channel_id=1, source_target_pairs={{0,4},{4,0},{1,5},{5,1},{2,6},{6,2},{3,7},{7,3},{8,12},{12,8},{9,1... | collective-permute-start | bytes 294920 | tf_op jit(solution)/shard_map/ppermute | solution.py:413
  103.5 20.7 %copy-start.3 = (f32[8,3,16,128]{3,2,1,0:T(8,128)S(1)}, f32[8,3,16,128]{3,2,1,0:T(8,128)}, u32[]{:S(2)}) copy-start(f32[8,3,16,128]{3,2,1,0:T(8,128)} %get-tuple-element.8) | copy-start | bytes 589828
  120.8 8.0 %collective-permute-start.4 = (f32[30,128]{1,0:T(8,128)}, f32[30,128]{1,0:T(8,128)S(1)}, u32[]{:S(2)}, u32[]{:S(2)}) collective-permute-start(f32[30,128]{1,0:T(8,128)} %pack.3), channel_id=1, source_target_pairs={{4,8},{8,4},{12,16},{16,12},{20,24},{24,20},{5,9},{9,5},{13,17},{1... | collective-permute-start | bytes 46088 | tf_op jit(solution)/shard_map/ppermute | solution.py:408
  124.9 14.1 %all-to-all-start.3 = ((f32[4,3,16,128]{3,2,1,0:T(8,128)}), f32[4,3,16,128]{3,2,1,0:T(8,128)S(1)}, u32[]{:S(2)}, u32[]{:S(2)}) async-start(f32[4,3,16,128]{3,2,1,0:T(8,128)} %slice_add_fusion), calls=%async_computation.3 | async-start | bytes 196608 | tf_op jit(solution)/shard_map/all_to_all | solution.py:416
  128.8 9.4 %copy-start.5 = (f32[64,3,128]{2,1,0:T(4,128)S(1)}, f32[64,3,128]{2,1,0:T(4,128)}, u32[]{:S(2)}) copy-start(f32[64,3,128]{2,1,0:T(4,128)} %get-tuple-element.9) | copy-start | bytes 294916
  128.8 9.4 %copy-start.6 = (f32[64,3,128]{2,1,0:T(4,128)S(1)}, f32[64,3,128]{2,1,0:T(4,128)}, u32[]{:S(2)}) copy-start(f32[64,3,128]{2,1,0:T(4,128)} %get-tuple-element.10) | copy-start | bytes 294916
  138.9 0.8 copy-start.17
  138.9 0.8 copy-start.18
  (10 other events, 6.8 us)

commit v2 on v1

--- a/solution.py
+++ b/solution.py
@@ -16,6 +16,9 @@
 gravity = 9.81
 
 far = 1000.0
+ahead = 8
+columns = 4
+faces_at_once = 16
 f32 = jnp.float32
 bf16 = jnp.bfloat16
 falls = (0.0, 0.0, -gravity)
@@ -127,13 +130,20 @@
         right_ref[k] = right_side(pieces, row)
 
 
-def pushes(left_ref, sum_ref, right, others):
-    total = None
-    for slot in others:
-        high, low = pair_weights(dot(left_ref[slot], right), 2.0 * radius)
-        part = dot(sum_ref[slot], jnp.concatenate([high, low], axis=0))
-        total = part if total is None else total + part
-    return total
+def pushes(left_ref, sum_ref, right_ref, jobs):
+    todo = [(k, block, slot) for k, (block, others) in enumerate(jobs) for slot in others]
+    totals = [None] * len(jobs)
+    waiting = []
+    for n in range(len(todo) + ahead):
+        if n < len(todo):
+            k, block, slot = todo[n]
+            waiting.append((k, slot, dot(left_ref[slot], right_ref[block])))
+        if n >= ahead:
+            k, slot, product = waiting.pop(0)
+            high, low = pair_weights(product, 2.0 * radius)
+            part = dot(sum_ref[slot], jnp.concatenate([high, low], axis=0))
+            totals[k] = part if totals[k] is None else totals[k] + part
+    return totals
 
 
 def store_rows(out_ref, values, index, add):
@@ -154,19 +164,20 @@
     build_left(state_ref, left_ref, sum_ref, own + ends)
     build_right(state_ref, right_ref, own)
 
-    def column(c, carry):
-        for r in range(ct):
-            others = [
-                (q + 1) * wide + c + d
-                for q in range(max(r - 1, 0), min(r + 2, ct))
-                for d in range(3)
-            ]
-            sums = pushes(left_ref, sum_ref, right_ref[r * cc + c], others)
-            state = state_ref[pl.ds(pl.multiple_of(((r + 1) * wide + c + 1) * 8, 8), 8), :]
-            store_rows(out_ref, moment(state, sums), r * cc + c, False)
+    def several(step, carry):
+        jobs, places = [], []
+        for k in range(columns):
+            c = step * columns + k
+            for r in range(ct):
+                near = range(max(r - 1, 0), min(r + 2, ct))
+                jobs.append((r * cc + c, [(q + 1) * wide + c + d for q in near for d in range(3)]))
+                places.append(((r + 1) * wide + c + 1, r * cc + c))
+        for sums, (slot, index) in zip(pushes(left_ref, sum_ref, right_ref, jobs), places):
+            state = state_ref[pl.ds(pl.multiple_of(slot * 8, 8), 8), :]
+            store_rows(out_ref, moment(state, sums), index, False)
         return carry
 
-    lax.fori_loop(0, cc, column, 0)
+    lax.fori_loop(0, cc // columns, several, 0)
 
 
 def outer_kernel(ct, cc, crosses, second, s_ref, x_ref, v_ref, all_ref, halo_ref, *rest):
@@ -226,33 +237,41 @@
     build_left(state_ref, left_ref, sum_ref, ring)
     build_right(state_ref, right_ref, [(r + 1) * wide + c + 1 for r in range(ct) for c in range(cc)])
 
-    def one(r, c, others, add):
-        sums = pushes(left_ref, sum_ref, right_ref[r * cc + c], others)
-        start = ((r + 1) * wide + c + 1) * 8
-        state = state_ref[pl.ds(start if add else pl.multiple_of(start, 8), 8), :]
-        store_rows(out_ref, moment(state, sums), r * cc + c, add)
-
-    if ct > 2:
+    def finish(jobs, places, add):
+        for sums, (slot, index) in zip(pushes(left_ref, sum_ref, right_ref, jobs), places):
+            start = slot * 8 if isinstance(slot, int) else pl.multiple_of(slot * 8, 8)
+            store_rows(out_ref, moment(state_ref[pl.ds(start, 8), :], sums), index, add)
+
+    if ct != 2:
         out_ref[...] = jnp.zeros_like(out_ref)
 
-    def column(c, carry):
-        one(0, c, [c + d for d in range(3)], False)
-        one(ct - 1, c, [(ct + 1) * wide + c + d for d in range(3)], ct == 1)
+    def several(step, carry):
+        jobs, places = [], []
+        for k in range(columns):
+            c = step * columns + k
+            for r, rr in ((0, 0), (ct - 1, ct + 1)):
+                jobs.append((r * cc + c, [rr * wide + c + d for d in range(3)]))
+                places.append(((r + 1) * wide + c + 1, r * cc + c))
+        finish(jobs, places, ct != 2)
         return carry
 
-    lax.fori_loop(0, cc, column, 0)
+    lax.fori_loop(0, cc // columns, several, 0)
+    jobs, places = [], []
     for r in range(ct):
         near = range(max(r - 1, 0), min(r + 2, ct))
-        one(r, 0, [(q + 1) * wide for q in near], True)
-        one(r, cc - 1, [(q + 1) * wide + cc + 1 for q in near], True)
-
-
-def face_kernel(second, index_ref, offset_ref, velocity_ref, all_ref, *rest):
+        for c, p in ((0, 0), (cc - 1, cc + 1)):
+            jobs.append((r * cc + c, [(q + 1) * wide + p for q in near]))
+            places.append(((r + 1) * wide + c + 1, r * cc + c))
+    finish(jobs, places, True)
+
+
+def face_kernel(second, cc, crosses, s_ref, index_ref, offset_ref, velocity_ref, all_ref, *rest):
     if second:
-        force_ref, *rest = rest
-    part_ref, react_ref, state_ref, face_ref = rest
+        force_ref, before_ref, *rest = rest
+    part_ref, react_ref, halo_ref, state_ref, face_ref = rest
     devices, _, cells, _ = all_ref.shape
     count = offset_ref.shape[0]
+    pack(cc, crosses, s_ref, force_ref if second else all_ref, halo_ref)
 
     def spread(device, carry):
         base = pl.multiple_of(device * cells * 8, 8)
@@ -273,27 +292,42 @@
         face_ref[pl.ds(axis, count, stride=8), :] = y
         face_ref[pl.ds(3 + axis, count, stride=8), :] = w
 
-    def one(f):
-        block = index_ref[f]
-        state = state_ref[pl.ds(pl.multiple_of(block * 8, 8), 8), :]
-        face = face_ref[pl.ds(pl.multiple_of(f * 8, 8), 8), :]
-        pieces, row = features(state, soften * soften)
-        face_pieces, _ = features(face, 0.0)
-        product = dot(left_side(face_pieces, row), right_side(pieces, row))
-        high, low = pair_weights(product, radius + face_radius)
-        onto = moment(state, dot(sum_side(face_pieces), jnp.concatenate([high, low], axis=0)))
-        back = moment(
-            face, dot(sum_side(pieces), jnp.concatenate([high, low], axis=1), ((1,), (1,)))
-        )
-        react_ref[f] = (time_step * damping * back)[0:3]
-        return block, onto
-
-    group = 4 if count % 4 == 0 else 1
+    group = next(n for n in (faces_at_once, 4, 2, 1) if count % n == 0)
 
     def several(g, carry):
-        done = [one(g * group + k) for k in range(group)]
-        for block, onto in done:
-            device, cell = block // cells, block % cells
+        blocks, states, faces, rights, lefts, sums, back_sums = [], [], [], [], [], [], []
+        for k in range(group):
+            f = g * group + k
+            block = index_ref[f]
+            state = state_ref[pl.ds(pl.multiple_of(block * 8, 8), 8), :]
+            face = face_ref[pl.ds(pl.multiple_of(f * 8, 8), 8), :]
+            pieces, row = features(state, soften * soften)
+            face_pieces, _ = features(face, 0.0)
+            blocks.append(block)
+            states.append(state)
+            faces.append(face)
+            lefts.append(left_side(face_pieces, row))
+            rights.append(right_side(pieces, row))
+            sums.append(sum_side(face_pieces))
+            back_sums.append(sum_side(pieces))
+        waiting, done = [], []
+        for n in range(group + ahead):
+            if n < group:
+                waiting.append(dot(lefts[n], rights[n]))
+            if n >= ahead and n - ahead < group:
+                k = n - ahead
+                high, low = pair_weights(waiting[k], radius + face_radius)
+                done.append(
+                    (
+                        dot(sums[k], jnp.concatenate([high, low], axis=0)),
+                        dot(back_sums[k], jnp.concatenate([high, low], axis=1), ((1,), (1,))),
+                    )
+                )
+        for k in range(group):
+            onto, back = moment(states[k], done[k][0]), moment(faces[k], done[k][1])
+            back = (time_step * damping * back)[0:3]
+            react_ref[g * group + k] = before_ref[g * group + k] + back if second else back
+            device, cell = blocks[k] // cells, blocks[k] % cells
             for axis in range(3):
                 line = part_ref[device, axis, pl.ds(cell, 1), :]
                 part_ref[device, axis, pl.ds(cell, 1), :] = line + damping * onto[axis : axis + 1]
@@ -302,15 +336,15 @@
     lax.fori_loop(0, count // group, several, 0)
 
 
-def pack_kernel(cc, s_ref, mine_ref, out_ref):
-    crosses, fields, _, _ = mine_ref.shape
-    c_index, row = s_ref[0], s_ref[8]
+def pack(cc, crosses, s_ref, all_ref, out_ref):
+    fields = all_ref.shape[1]
+    c_index, first, row = s_ref[0], s_ref[1] * crosses, s_ref[8]
     for p in range(cc + 2):
         shift = -1 if p == 0 else (1 if p == cc + 1 else 0)
-        device = jnp.clip(c_index + shift, 0, crosses - 1)
+        device = first + jnp.clip(c_index + shift, 0, crosses - 1)
         cell = row * cc + (p - 1) % cc
         for f in range(fields):
-            out_ref[pl.ds(p * fields + f, 1), :] = mine_ref[device, f, pl.ds(cell, 1), :]
+            out_ref[pl.ds(p * fields + f, 1), :] = all_ref[device, f, pl.ds(cell, 1), :]
 
 
 def call(kernel, name, args, scalars, outs, scratch, flops):
@@ -395,25 +429,13 @@
             return jnp.concatenate([a, lax.ppermute(a, "track", swap)], axis=0)
         return lax.all_gather(a, "track", axis=0, tiled=True)
 
-    def halo(a):
-        packed = call(
-            functools.partial(pack_kernel, cc),
-            "pack",
-            [scalars, a],
-            1,
-            [(wide * a.shape[1], slots)],
-            [],
-            1000,
-        )[0]
-        return lax.ppermute(packed, ("vehicle", "track"), travel)
-
     def scatter_force(part):
         part = part.reshape(tracks, crosses, 3, cells, slots)
         if pair:
             part = part[0] + lax.ppermute(part[1], "track", swap)
         else:
             part = jnp.sum(lax.all_to_all(part, "track", 0, 0, tiled=True), axis=0)
-        return jnp.sum(lax.all_to_all(part, "cross", 0, 0, tiled=True), axis=0)
+        return lax.all_to_all(part, "cross", 0, 0, tiled=True)
 
     fall = jnp.array(falls, f32)[:, None, None]
     reaction = None
@@ -432,23 +454,33 @@
             ring_slots,
             4 * 10**9,
         )[0]
-        group, across = gather_track(mine), halo(mine)
+        mine, inner = lax.optimization_barrier((mine, inner))
+        group = gather_track(mine)
         if second:
-            extra, halo_extra = [group], [across]
+            extra, before = [group], [reaction]
         else:
-            everyone, beyond, extra, halo_extra = group, across, [], []
-        part, react = call(
-            functools.partial(face_kernel, second),
+            everyone, extra, before = group, [], []
+        part, reaction, packed = call(
+            functools.partial(face_kernel, second, cc, crosses),
             "faces",
-            [index, face_offset, face_velocity, everyone] + extra,
-            1,
-            [(tracks * crosses, 3, cells, slots), (own_faces, 3, faces)],
+            [scalars, index, face_offset, face_velocity, everyone] + extra + before,
+            2,
+            [
+                (tracks * crosses, 3, cells, slots),
+                (own_faces, 3, faces),
+                (wide * group.shape[1], slots),
+            ],
             [
                 VMEM((tracks * crosses * cells * 8, slots), f32),
                 VMEM((own_faces * 8, faces), f32),
             ],
             4 * 10**9,
         )
+        across = lax.ppermute(packed, ("vehicle", "track"), travel)
+        if second:
+            halo_extra = [across]
+        else:
+            beyond, halo_extra = across, []
         outer = call(
             functools.partial(outer_kernel, ct, cc, crosses, second),
             "outer",
@@ -458,10 +490,10 @@
             ring_slots,
             4 * 10**9,
         )[0]
-        force = jnp.where(live[None], inner + outer, 0.0) + scatter_force(part)
+        returned, outer = lax.optimization_barrier((scatter_force(part), outer))
+        force = jnp.where(live[None], inner + outer, 0.0) + jnp.sum(returned, axis=0)
         v = v + time_step * (force + fall)
         x = x + time_step * v
-        reaction = react if reaction is None else reaction + react
     shape = particle_offset.shape
     return (x.reshape(shape), v.reshape(shape), reaction)
 

time: 141 us -> 77.9 us (0.55)
  Pallas kernels: 85.8 us -> 30.5 us
  blocking collectives: 9.32 us -> 0 us
  starting transfers between devices: 23.4 us -> 28.1 us
  waiting for transfers between devices: 5.82 us -> 1.45 us
    pallas_call x8 -> x6, Pallas kernels: 85.8 us -> 30.5 us  [call(): pl.pallas_call(kernel, name=name, out_shape=[jax.ShapeDtypeStruct(s, f32)...]
    all_to_all x1 -> x0, blocking collectives: 9.32 us -> none  [gather_cross(): lax.all_to_all(spread, 'cross', split_axis=0, concat_axis=0, tiled=True)]
    all_to_all x1 -> x2, waiting for transfers between devices: 4.98 us -> 0.5 us  [gather_cross(): lax.all_to_all(spread, 'cross', split_axis=0, concat_axis=0, tiled=True)]
    all_to_all x1 -> x2, starting transfers between devices: 4.89 us -> 9.29 us  [gather_cross(): lax.all_to_all(spread, 'cross', split_axis=0, concat_axis=0, tiled=True)]
    unnamed x55 -> x49, local copies, waits for them, and re-layouts: 7.79 us -> 7.63 us
  transfers between devices with their start and end apart: 9 -> 10, of which waited for: 2 -> 3; matrix products, arithmetic and copies ran while one was open for 3% -> 6% of each run, Pallas kernels for 37% -> 24%
where the time goes in v2:
time: 77.9 us; the launch traced here: 76.7 us
  Pallas kernels  30.5 us (39%)
  starting transfers between devices  28.1 us (36%)
  local copies, waits for them, and re-layouts  11.7 us (15%)
  other arithmetic  4.17 us (5%)
  waiting for transfers between devices  1.45 us (2%)
  between operations  0.82 us (1%)
    pallas_call x6, Pallas kernels, call(): pl.pallas_call(kernel, name=name, out_shape=[jax.ShapeDtypeStruct(s, f32)...  30.5 us
    all_to_all x2, starting transfers between devices, gather_cross(): lax.all_to_all(spread, 'cross', split_axis=0, concat_axis=0, tiled=True)  9.29 us
    all_to_all x2, starting transfers between devices, scatter_force(): return lax.all_to_all(part, 'cross', 0, 0, tiled=True)  8.92 us
    unnamed x49, local copies, waits for them, and re-layouts  7.63 us
    ppermute x2, starting transfers between devices, body(): across = lax.ppermute(packed, ('vehicle', 'track'), travel)  6.84 us
    ppermute x2, starting transfers between devices, gather_track(): return jnp.concatenate([a, lax.ppermute(a, 'track', swap)], axis=0)  2.68 us
    slice x2, local copies, waits for them, and re-layouts, scatter_force(): part = part[0] + lax.ppermute(part[1], 'track', swap)  1.94 us
  transfers between devices with their start and end apart: 10, of which 3 were waited for; matrix products, arithmetic and copies ran while one was open for 6% of the time, Pallas kernels for 24%

profile of v2, /device:TPU:11, one launch (start us, length us, event | category | flops | bytes accessed | tf_op | source)
XLA Modules:
  0.0 76.7 jit_solution(2070175485241118825)
XLA Ops:
  1.5 0.8 %and_select_fusion.1.x_ref = f32[3,16,128]{2,1,0:T(8,128)S(1)} fusion(f32[3,2,8,128]{3,2,1,0:T(8,128)} %param.8, pred[16,128]{1,0:T(8,128)(4,1)S(1)} %get-tuple-element.40, pred[3]{0:T(512)(128)(4,1)S(1)} %iota_compare_fusion.1), kind=kLoop, calls=%fused_computation.4 | loop fusion | flops 12288 | bytes 51203 | tf_op jit(solution)/shard_map/jit(_where)/select_n | solution.py:396
  2.9 0.7 broadcast_in_dim.40
  3.6 4.8 %all-to-all-start = ((f32[4,6,16,128]{3,2,1,0:T(8,128)}), f32[4,6,16,128]{3,2,1,0:T(8,128)S(1)}, u32[]{:S(2)}, u32[]{:S(2)}) async-start(f32[4,6,16,128]{3,2,1,0:T(8,128)} %broadcast_in_dim.40), calls=%async_computation | async-start | bytes 393216 | tf_op jit(solution)/shard_map/all_to_all | solution.py:425
  8.4 4.8 %inner.2 = f32[3,16,128]{2,1,0:T(8,128)} custom-call(f32[3,16,128]{2,1,0:T(8,128)} %copy-done.9, f32[3,16,128]{2,1,0:T(8,128)} %bitcast.34), custom_call_target="tpu_custom_call" | custom-call | flops 4000000000 | tf_op jit(solution)/shard_map/inner/pallas_call | solution.py:353
  13.3 2.2 %collective-permute-start = (f32[4,6,16,128]{3,2,1,0:T(8,128)S(1)}, f32[4,6,16,128]{3,2,1,0:T(8,128)S(1)}, u32[]{:S(2)}, u32[]{:S(2)}) collective-permute-start(f32[4,6,16,128]{3,2,1,0:T(8,128)S(1)} %all-to-all-done), channel_id=1, source_target_pairs={{0,4},{4,0},{1,5},{5,1},{2,6},{6,2},{3,7},{7,3},{8,12},{12,8},{9,1... | collective-permute-start | bytes 589832 | tf_op jit(solution)/shard_map/ppermute | solution.py:429
  16.1 0.7 copy.11.offset_ref
  17.0 0.7 copy.12.velocity_ref
  18.4 0.7 copy-done.6
  19.2 5.9 %faces.2 = (f32[8,3,16,128]{3,2,1,0:T(8,128)}, f32[64,3,128]{2,1,0:T(4,128)}, f32[60,128]{1,0:T(8,128)}) custom-call(s32[9]{0:T(128)} %stack.51.s_ref, s32[64]{0:T(128)} %multiply_add_fusion.2.index_ref, f32[64,3,128]{2,1,0:T(4,128)} %copy.11.offset_ref, f32[64,3,128]{2,1,0:T(4,128)} %copy.12.velocity_ref, f32[8,6,16,128]{3,2,1,0:T(8,128)} %copy-done.6), custom_call_target="tpu_custom_call" | custom-call | flops 4000000000 | tf_op jit(solution)/shard_map/faces/pallas_call | solution.py:353
  25.1 1.0 %slice.17 = f32[4,3,16,128]{3,2,1,0:T(8,128)S(1)} slice(f32[8,3,16,128]{3,2,1,0:T(8,128)} %get-tuple-element.19), slice={[4:8], [0:3], [0:16], [0:128]} | slice | bytes 196608 | tf_op jit(solution)/shard_map/slice | solution.py:435
  26.1 3.5 %collective-permute-start.2 = (f32[60,128]{1,0:T(8,128)}, f32[60,128]{1,0:T(8,128)S(1)}, u32[]{:S(2)}, u32[]{:S(2)}) collective-permute-start(f32[60,128]{1,0:T(8,128)} %get-tuple-element.20), channel_id=1, source_target_pairs={{4,8},{8,4},{12,16},{16,12},{20,24},{24,20},{5,9},{9,5},{13,17},{1... | collective-permute-start | bytes 92168 | tf_op jit(solution)/shard_map/ppermute | solution.py:479
  30.3 4.5 %all-to-all-start.1 = ((f32[4,3,16,128]{3,2,1,0:T(8,128)}), f32[4,3,16,128]{3,2,1,0:T(8,128)S(1)}, u32[]{:S(2)}, u32[]{:S(2)}) async-start(f32[4,3,16,128]{3,2,1,0:T(8,128)} %slice_add_fusion.1), calls=%async_computation.1 | async-start | bytes 196608 | tf_op jit(solution)/shard_map/all_to_all | solution.py:438
  35.4 4.4 %outer.2 = f32[3,16,128]{2,1,0:T(8,128)} custom-call(s32[9]{0:T(128)} %stack.51.s_ref, f32[3,16,128]{2,1,0:T(8,128)} %copy-done.9, f32[3,16,128]{2,1,0:T(8,128)} %bitcast.35, f32[8,6,16,128]{3,2,1,0:T(8,128)} %copy-done.6, f32[60,128]{1,0:T(8,128)} %copy-done.19), custom_call_target="tpu_custom_call" | custom-call | flops 4000000000 | tf_op jit(solution)/shard_map/outer/pallas_call | solution.py:353
  40.6 0.7 and_select_fusion
  41.9 4.5 %all-to-all-start.2 = ((f32[4,3,16,128]{3,2,1,0:T(8,128)}), f32[4,3,16,128]{3,2,1,0:T(8,128)S(1)}, u32[]{:S(2)}, u32[]{:S(2)}) async-start(f32[4,3,16,128]{3,2,1,0:T(8,128)} %broadcast_in_dim.42), calls=%async_computation.2 | async-start | bytes 196608 | tf_op jit(solution)/shard_map/all_to_all | solution.py:425
  46.5 4.7 %inner.3 = f32[3,16,128]{2,1,0:T(8,128)} custom-call(f32[3,16,128]{2,1,0:T(8,128)} %get-tuple-element.36.x_ref, f32[3,16,128]{2,1,0:T(8,128)} %get-tuple-element.37.v_ref), custom_call_target="tpu_custom_call" | custom-call | flops 4000000000 | tf_op jit(solution)/shard_map/inner/pallas_call | solution.py:353
  52.0 0.9 %collective-permute-done.3 = f32[4,3,16,128]{3,2,1,0:T(8,128)S(1)} collective-permute-done((f32[4,3,16,128]{3,2,1,0:T(8,128)S(1)}, f32[4,3,16,128]{3,2,1,0:T(8,128)S(1)}, u32[]{:S(2)}, u32[]{:S(2)}) %collective-permute-start.3) | collective-permute-done | bytes 98336 | tf_op jit(solution)/shard_map/ppermute | solution.py:429
  53.6 6.2 %faces.3 = (f32[8,3,16,128]{3,2,1,0:T(8,128)}, f32[64,3,128]{2,1,0:T(4,128)}, f32[30,128]{1,0:T(8,128)}) custom-call(s32[9]{0:T(128)} %stack.51.s_ref, s32[64]{0:T(128)} %multiply_add_fusion.2.index_ref, f32[64,3,128]{2,1,0:T(4,128)} %copy.11.offset_ref, f32[64,3,128]{2,1,0:T(4,128)} %copy.12.velocity_ref, f32[8,6,16,128]{3,2,1,0:T(8,128)} %copy-done.6, ...), custom_call_target="tpu_custom_call" | custom-call | flops 4000000000 | tf_op jit(solution)/shard_map/faces/pallas_call | solution.py:353
  59.8 1.0 %slice.19 = f32[4,3,16,128]{3,2,1,0:T(8,128)S(1)} slice(f32[8,3,16,128]{3,2,1,0:T(8,128)} %get-tuple-element.26), slice={[4:8], [0:3], [0:16], [0:128]} | slice | bytes 196608 | tf_op jit(solution)/shard_map/slice | solution.py:435
  61.1 3.4 %collective-permute-start.5 = (f32[30,128]{1,0:T(8,128)}, f32[30,128]{1,0:T(8,128)S(1)}, u32[]{:S(2)}, u32[]{:S(2)}) collective-permute-start(f32[30,128]{1,0:T(8,128)} %get-tuple-element.27), channel_id=1, source_target_pairs={{4,8},{8,4},{12,16},{16,12},{20,24},{24,20},{5,9},{9,5},{13,17},{1... | collective-permute-start | bytes 46088 | tf_op jit(solution)/shard_map/ppermute | solution.py:479
  65.8 4.4 %all-to-all-start.3 = ((f32[4,3,16,128]{3,2,1,0:T(8,128)}), f32[4,3,16,128]{3,2,1,0:T(8,128)S(1)}, u32[]{:S(2)}, u32[]{:S(2)}) async-start(f32[4,3,16,128]{3,2,1,0:T(8,128)} %slice_add_fusion), calls=%async_computation.3 | async-start | bytes 196608 | tf_op jit(solution)/shard_map/all_to_all | solution.py:438
  70.7 4.5 %outer.3 = f32[3,16,128]{2,1,0:T(8,128)} custom-call(s32[9]{0:T(128)} %stack.51.s_ref, f32[3,16,128]{2,1,0:T(8,128)} %get-tuple-element.36.x_ref, f32[3,16,128]{2,1,0:T(8,128)} %get-tuple-element.37.v_ref, f32[8,6,16,128]{3,2,1,0:T(8,128)} %copy-done.6, f32[60,128]{1,0:T(8,128)} %copy-done.19, f32[8,3,16,128]{3,2,1,0:T(8,128)} %copy-done.11, ...), custom_call_target="tpu_custom_call" | custom-call | flops 4000000000 | tf_op jit(solution)/shard_map/outer/pallas_call | solution.py:353
  75.3 0.7 copy-done.10
  76.0 0.7 add_bitcast_fusion
  (70 shorter events, 9.5 us)
Async XLA Ops:
  1.5 0.8 %copy-start.7 = (f32[3,2,8,128]{3,2,1,0:T(8,128)S(1)}, f32[3,2,8,128]{3,2,1,0:T(8,128)}, u32[]{:S(2)}) copy-start(f32[3,2,8,128]{3,2,1,0:T(8,128)} %param.9) | copy-start | bytes 73732
  3.6 9.7 %all-to-all-start = ((f32[4,6,16,128]{3,2,1,0:T(8,128)}), f32[4,6,16,128]{3,2,1,0:T(8,128)S(1)}, u32[]{:S(2)}, u32[]{:S(2)}) async-start(f32[4,6,16,128]{3,2,1,0:T(8,128)} %broadcast_in_dim.40), calls=%async_computation | async-start | bytes 393216 | tf_op jit(solution)/shard_map/all_to_all | solution.py:425
  8.3 7.2 %copy-start.17 = (s32[64]{0:T(128)S(1)}, s32[64]{0:T(128)}, u32[]{:S(2)}) copy-start(s32[64]{0:T(128)} %param.14) | copy-start | bytes 772
  8.3 7.2 %copy-start.18 = (s32[64,1]{0,1:T(1,128)S(1)}, s32[64,1]{0,1:T(1,128)}, u32[]{:S(2)}) copy-start(s32[64,1]{0,1:T(1,128)} %param.13) | copy-start | bytes 772
  8.4 7.8 %copy-start.4 = (f32[64,3,128]{2,0,1:T(8,128)S(1)}, f32[64,3,128]{2,0,1:T(8,128)}, u32[]{:S(2)}) copy-start(f32[64,3,128]{2,0,1:T(8,128)} %param.11) | copy-start | bytes 294916
  13.3 5.1 %collective-permute-start = (f32[4,6,16,128]{3,2,1,0:T(8,128)S(1)}, f32[4,6,16,128]{3,2,1,0:T(8,128)S(1)}, u32[]{:S(2)}, u32[]{:S(2)}) collective-permute-start(f32[4,6,16,128]{3,2,1,0:T(8,128)S(1)} %all-to-all-done), channel_id=1, source_target_pairs={{0,4},{4,0},{1,5},{5,1},{2,6},{6,2},{3,7},{7,3},{8,12},{12,8},{9,1... | collective-permute-start | bytes 589832 | tf_op jit(solution)/shard_map/ppermute | solution.py:429
  16.1 0.9 %copy-start.5 = (f32[64,3,128]{2,0,1:T(8,128)S(1)}, f32[64,3,128]{2,0,1:T(8,128)}, u32[]{:S(2)}) copy-start(f32[64,3,128]{2,0,1:T(8,128)} %param.12) | copy-start | bytes 294916
  18.4 0.7 copy-start.6
  25.1 4.5 %copy-start.2 = (f32[8,3,16,128]{3,2,1,0:T(8,128)S(1)}, f32[8,3,16,128]{3,2,1,0:T(8,128)}, u32[]{:S(2)}) copy-start(f32[8,3,16,128]{3,2,1,0:T(8,128)} %get-tuple-element.19) | copy-start | bytes 589828
  26.1 3.5 %collective-permute-start.1 = (f32[4,3,16,128]{3,2,1,0:T(8,128)S(1)}, f32[4,3,16,128]{3,2,1,0:T(8,128)S(1)}, u32[]{:S(2)}, u32[]{:S(2)}) collective-permute-start(f32[4,3,16,128]{3,2,1,0:T(8,128)S(1)} %slice.17), channel_id=1, source_target_pairs={{0,4},{4,0},{1,5},{5,1},{2,6},{6,2},{3,7},{7,3},{8,12},{12,8},{9,1... | collective-permute-start | bytes 294920 | tf_op jit(solution)/shard_map/ppermute | solution.py:435
  26.1 8.7 %collective-permute-start.2 = (f32[60,128]{1,0:T(8,128)}, f32[60,128]{1,0:T(8,128)S(1)}, u32[]{:S(2)}, u32[]{:S(2)}) collective-permute-start(f32[60,128]{1,0:T(8,128)} %get-tuple-element.20), channel_id=1, source_target_pairs={{4,8},{8,4},{12,16},{16,12},{20,24},{24,20},{5,9},{9,5},{13,17},{1... | collective-permute-start | bytes 92168 | tf_op jit(solution)/shard_map/ppermute | solution.py:479
  30.3 9.5 %all-to-all-start.1 = ((f32[4,3,16,128]{3,2,1,0:T(8,128)}), f32[4,3,16,128]{3,2,1,0:T(8,128)S(1)}, u32[]{:S(2)}, u32[]{:S(2)}) async-start(f32[4,3,16,128]{3,2,1,0:T(8,128)} %slice_add_fusion.1), calls=%async_computation.1 | async-start | bytes 196608 | tf_op jit(solution)/shard_map/all_to_all | solution.py:438
  39.8 0.8 copy-start.8
  39.8 0.8 %copy-start.12 = (f32[3,16,128]{2,1,0:T(8,128)S(1)}, f32[3,16,128]{2,1,0:T(8,128)}, u32[]{:S(2)}) copy-start(f32[3,16,128]{2,1,0:T(8,128)} %inner.2) | copy-start | bytes 73732
  39.8 0.8 %copy-start.13 = (f32[3,16,128]{2,1,0:T(8,128)S(1)}, f32[3,16,128]{2,1,0:T(8,128)}, u32[]{:S(2)}) copy-start(f32[3,16,128]{2,1,0:T(8,128)} %outer.2) | copy-start | bytes 73732
  41.9 9.6 %all-to-all-start.2 = ((f32[4,3,16,128]{3,2,1,0:T(8,128)}), f32[4,3,16,128]{3,2,1,0:T(8,128)S(1)}, u32[]{:S(2)}, u32[]{:S(2)}) async-start(f32[4,3,16,128]{3,2,1,0:T(8,128)} %broadcast_in_dim.42), calls=%async_computation.2 | async-start | bytes 196608 | tf_op jit(solution)/shard_map/all_to_all | solution.py:425
  51.5 1.4 %collective-permute-start.3 = (f32[4,3,16,128]{3,2,1,0:T(8,128)S(1)}, f32[4,3,16,128]{3,2,1,0:T(8,128)S(1)}, u32[]{:S(2)}, u32[]{:S(2)}) collective-permute-start(f32[4,3,16,128]{3,2,1,0:T(8,128)S(1)} %all-to-all-done.2), channel_id=1, source_target_pairs={{0,4},{4,0},{1,5},{5,1},{2,6},{6,2},{3,7},{7,3},{8,12},{12,8},{9,1... | collective-permute-start | bytes 294920 | tf_op jit(solution)/shard_map/ppermute | solution.py:429
  59.8 4.7 %copy-start.3 = (f32[64,3,128]{2,1,0:T(4,128)S(1)}, f32[64,3,128]{2,1,0:T(4,128)}, u32[]{:S(2)}) copy-start(f32[64,3,128]{2,1,0:T(4,128)} %get-tuple-element.33) | copy-start | bytes 294916
  59.8 5.4 %copy-start.1 = (f32[8,3,16,128]{3,2,1,0:T(8,128)S(1)}, f32[8,3,16,128]{3,2,1,0:T(8,128)}, u32[]{:S(2)}) copy-start(f32[8,3,16,128]{3,2,1,0:T(8,128)} %get-tuple-element.26) | copy-start | bytes 589828
  60.7 4.4 %collective-permute-start.4 = (f32[4,3,16,128]{3,2,1,0:T(8,128)S(1)}, f32[4,3,16,128]{3,2,1,0:T(8,128)S(1)}, u32[]{:S(2)}, u32[]{:S(2)}) collective-permute-start(f32[4,3,16,128]{3,2,1,0:T(8,128)S(1)} %slice.19), channel_id=1, source_target_pairs={{0,4},{4,0},{1,5},{5,1},{2,6},{6,2},{3,7},{7,3},{8,12},{12,8},{9,1... | collective-permute-start | bytes 294920 | tf_op jit(solution)/shard_map/ppermute | solution.py:435
  61.1 9.0 %collective-permute-start.5 = (f32[30,128]{1,0:T(8,128)}, f32[30,128]{1,0:T(8,128)S(1)}, u32[]{:S(2)}, u32[]{:S(2)}) collective-permute-start(f32[30,128]{1,0:T(8,128)} %get-tuple-element.27), channel_id=1, source_target_pairs={{4,8},{8,4},{12,16},{16,12},{20,24},{24,20},{5,9},{9,5},{13,17},{1... | collective-permute-start | bytes 46088 | tf_op jit(solution)/shard_map/ppermute | solution.py:479
  65.8 9.5 %all-to-all-start.3 = ((f32[4,3,16,128]{3,2,1,0:T(8,128)}), f32[4,3,16,128]{3,2,1,0:T(8,128)S(1)}, u32[]{:S(2)}, u32[]{:S(2)}) async-start(f32[4,3,16,128]{3,2,1,0:T(8,128)} %slice_add_fusion), calls=%async_computation.3 | async-start | bytes 196608 | tf_op jit(solution)/shard_map/all_to_all | solution.py:438
  75.2 0.8 copy-start.14
  75.2 0.8 %copy-start.15 = (f32[3,16,128]{2,1,0:T(8,128)S(1)}, f32[3,16,128]{2,1,0:T(8,128)}, u32[]{:S(2)}) copy-start(f32[3,16,128]{2,1,0:T(8,128)} %outer.3) | copy-start | bytes 73732
  (8 other events, 5.4 us)

commit v3 on v2

--- a/solution.py
+++ b/solution.py
@@ -19,11 +19,13 @@
 ahead = 8
 columns = 4
 faces_at_once = 16
+scratch_bytes = 20 * 2**20
 f32 = jnp.float32
 bf16 = jnp.bfloat16
 falls = (0.0, 0.0, -gravity)
 VMEM = pltpu.VMEM
 SMEM = pltpu.SMEM
+VMEM_SPACE = pltpu.MemorySpace.VMEM
 
 
 def split3(a):
@@ -180,13 +182,31 @@
     lax.fori_loop(0, cc // columns, several, 0)
 
 
-def outer_kernel(ct, cc, crosses, second, s_ref, x_ref, v_ref, all_ref, halo_ref, *rest):
+class Gathered:
+    def __init__(self, refs, crosses, track):
+        self.refs, self.crosses, self.track = refs, crosses, track
+
+    def line(self, shift, device, field, cell):
+        if len(self.refs) == 2:
+            return self.refs[0 if shift == 0 else 1][device, field, pl.ds(cell, 1), :]
+        tracks = self.refs[0].shape[0] // self.crosses
+        track = jnp.clip(self.track + shift, 0, tracks - 1)
+        return self.refs[0][track * self.crosses + device, field, pl.ds(cell, 1), :]
+
+
+def outer_kernel(ct, cc, crosses, nrefs, second, x_ref, v_ref, *rest):
+    track, c_index = lax.axis_index("track"), lax.axis_index("cross")
+    vehicle = lax.axis_index("vehicle")
+    vehicles, tracks = lax.axis_size("vehicle"), lax.axis_size("track")
+    gathered = [Gathered(rest[:nrefs], crosses, track)]
+    halos = [rest[nrefs]]
+    rest = rest[nrefs + 1 :]
     if second:
-        force_ref, halo_force_ref, *rest = rest
+        gathered.append(Gathered(rest[:nrefs], crosses, track))
+        halos.append(rest[nrefs])
+        rest = rest[nrefs + 1 :]
     out_ref, state_ref, left_ref, sum_ref, right_ref = rest
     wide = cc + 2
-    c_index = s_ref[0]
-    own_track = s_ref[1]
     has_low = c_index > 0
     has_high = c_index < crosses - 1
     put_own(state_ref, x_ref, v_ref, ct, cc)
@@ -204,21 +224,23 @@
             state_ref[pl.ds(slot * 8 + axis, 1), :] = x
             state_ref[pl.ds(slot * 8 + 3 + axis, 1), :] = jnp.where(ok, v, 0.0)
 
-    def from_all(track, row, p):
-        shift = -1 if p == 0 else (1 if p == cc + 1 else 0)
-        device = track * crosses + jnp.clip(c_index + shift, 0, crosses - 1)
+    def from_all(shift, row, p):
+        step = -1 if p == 0 else (1 if p == cc + 1 else 0)
+        device = jnp.clip(c_index + step, 0, crosses - 1)
         cell = row * cc + (p - 1) % cc
-        refs = (all_ref, force_ref) if second else (all_ref,)
-        return lambda f, n, k: refs[k][device, f, pl.ds(cell, 1), :]
+        return lambda f, n, k: gathered[k].line(shift, device, f, cell)
 
     def from_halo(p):
-        refs = (halo_ref, halo_force_ref) if second else (halo_ref,)
-        return lambda f, n, k: refs[k][pl.ds(p * n + f, 1), :]
-
-    for rr, row, at in ((0, ct - 1, 2), (ct + 1, 0, 5)):
-        inside, track, exists = s_ref[at] > 0, s_ref[at + 1], s_ref[at + 2] > 0
+        return lambda f, n, k: halos[k][pl.ds(p * n + f, 1), :]
+
+    for rr, shift, row in ((0, -1, ct - 1), (ct + 1, 1, 0)):
+        if shift < 0:
+            inside, exists = track > 0, (track > 0) | (vehicle > 0)
+        else:
+            inside = track < tracks - 1
+            exists = inside | (vehicle < vehicles - 1)
         for p in range(wide):
-            a, b = from_all(track, row, p), from_halo(p)
+            a, b = from_all(shift, row, p), from_halo(p)
 
             def load(f, n, k, a=a, b=b):
                 return jnp.where(inside, a(f, n, k), b(f, n, k))
@@ -230,8 +252,8 @@
                 ok = jnp.logical_and(ok, has_high)
             place(rr * wide + p, rr, p, load, ok)
     for r in range(ct):
-        place((r + 1) * wide, r + 1, 0, from_all(own_track, r, 0), has_low)
-        place((r + 1) * wide + cc + 1, r + 1, cc + 1, from_all(own_track, r, cc + 1), has_high)
+        place((r + 1) * wide, r + 1, 0, from_all(0, r, 0), has_low)
+        place((r + 1) * wide + cc + 1, r + 1, cc + 1, from_all(0, r, cc + 1), has_high)
     ring = [rr * wide + p for rr in (0, ct + 1) for p in range(wide)]
     ring += [(r + 1) * wide + p for r in range(ct) for p in (0, cc + 1)]
     build_left(state_ref, left_ref, sum_ref, ring)
@@ -265,41 +287,53 @@
     finish(jobs, places, True)
 
 
-def face_kernel(second, cc, crosses, s_ref, index_ref, offset_ref, velocity_ref, all_ref, *rest):
+def face_kernel(second, ct, cc, crosses, nrefs, route_ref, cell_ref, offset_ref, velocity_ref, *rest):
+    all_refs, rest = rest[:nrefs], rest[nrefs:]
     if second:
-        force_ref, before_ref, *rest = rest
-    part_ref, react_ref, halo_ref, state_ref, face_ref = rest
-    devices, _, cells, _ = all_ref.shape
-    count = offset_ref.shape[0]
-    pack(cc, crosses, s_ref, force_ref if second else all_ref, halo_ref)
-
-    def spread(device, carry):
-        base = pl.multiple_of(device * cells * 8, 8)
-        for axis in range(3):
-            x, v = all_ref[device, axis], all_ref[device, axis + 3]
-            if second:
-                x, v = advanced(x, v, force_ref[device, axis], axis)
-            state_ref[pl.ds(base + axis, cells, stride=8), :] = x
-            state_ref[pl.ds(base + 3 + axis, cells, stride=8), :] = v
-            part_ref[device, axis] = jnp.zeros_like(x)
-        return carry
-
-    lax.fori_loop(0, devices, spread, 0)
+        force_refs, before_ref, rest = rest[:nrefs], rest[nrefs], rest[nrefs + 1 :]
+    part_refs, (react_ref, halo_ref, state_ref, face_ref, part_ref) = rest[:nrefs], rest[nrefs:]
+    devices, _, cells, _ = all_refs[0].shape
+    count = offset_ref.shape[1]
+    track = lax.axis_index("track")
+    pack(ct, cc, crosses, track, force_refs if second else all_refs, halo_ref)
+
+    for k in range(nrefs):
+
+        def spread(device, carry, k=k):
+            base = pl.multiple_of((k * devices + device) * cells * 8, 8)
+            for axis in range(3):
+                x, v = all_refs[k][device, axis], all_refs[k][device, axis + 3]
+                if second:
+                    x, v = advanced(x, v, force_refs[k][device, axis], axis)
+                state_ref[pl.ds(base + axis, cells, stride=8), :] = x
+                state_ref[pl.ds(base + 3 + axis, cells, stride=8), :] = v
+                part_ref[k * devices + device, axis] = jnp.zeros_like(x)
+            return carry
+
+        lax.fori_loop(0, devices, spread, 0, unroll=min(devices, 4))
     for axis in range(3):
-        y, w = offset_ref[:, axis, :], velocity_ref[:, axis, :]
+        y, w = offset_ref[axis], velocity_ref[axis]
         if second:
             y = y + time_step * w
         face_ref[pl.ds(axis, count, stride=8), :] = y
         face_ref[pl.ds(3 + axis, count, stride=8), :] = w
 
+    def block_of(f):
+        target = route_ref[f]
+        where, across = lax.div(target, crosses), lax.rem(target, crosses)
+        if nrefs == 2:
+            where = jnp.bitwise_xor(where, track)
+        return where * crosses + across, cell_ref[f]
+
     group = next(n for n in (faces_at_once, 4, 2, 1) if count % n == 0)
 
     def several(g, carry):
         blocks, states, faces, rights, lefts, sums, back_sums = [], [], [], [], [], [], []
         for k in range(group):
             f = g * group + k
-            block = index_ref[f]
-            state = state_ref[pl.ds(pl.multiple_of(block * 8, 8), 8), :]
+            block = block_of(f)
+            place = (block[0] * cells + block[1]) * 8
+            state = state_ref[pl.ds(pl.multiple_of(place, 8), 8), :]
             face = face_ref[pl.ds(pl.multiple_of(f * 8, 8), 8), :]
             pieces, row = features(state, soften * soften)
             face_pieces, _ = features(face, 0.0)
@@ -325,40 +359,84 @@
                 )
         for k in range(group):
             onto, back = moment(states[k], done[k][0]), moment(faces[k], done[k][1])
-            back = (time_step * damping * back)[0:3]
-            react_ref[g * group + k] = before_ref[g * group + k] + back if second else back
-            device, cell = blocks[k] // cells, blocks[k] % cells
+            device, cell = blocks[k]
             for axis in range(3):
+                line = time_step * damping * back[axis : axis + 1]
+                at = pl.ds(g * group + k, 1)
+                if second:
+                    line = line + before_ref[axis, at, :]
+                react_ref[axis, at, :] = line
                 line = part_ref[device, axis, pl.ds(cell, 1), :]
                 part_ref[device, axis, pl.ds(cell, 1), :] = line + damping * onto[axis : axis + 1]
         return carry
 
     lax.fori_loop(0, count // group, several, 0)
-
-
-def pack(cc, crosses, s_ref, all_ref, out_ref):
-    fields = all_ref.shape[1]
-    c_index, first, row = s_ref[0], s_ref[1] * crosses, s_ref[8]
+    for k in range(nrefs):
+        part_refs[k][...] = part_ref[pl.ds(k * devices, devices)]
+
+
+def pack(ct, cc, crosses, track, refs, out_ref):
+    gathered = Gathered(refs, crosses, track)
+    fields = refs[0].shape[1]
+    c_index = lax.axis_index("cross")
+    row = jnp.where(track < lax.axis_size("track") - 1, 0, ct - 1)
     for p in range(cc + 2):
-        shift = -1 if p == 0 else (1 if p == cc + 1 else 0)
-        device = first + jnp.clip(c_index + shift, 0, crosses - 1)
+        step = -1 if p == 0 else (1 if p == cc + 1 else 0)
+        device = jnp.clip(c_index + step, 0, crosses - 1)
         cell = row * cc + (p - 1) % cc
         for f in range(fields):
-            out_ref[pl.ds(p * fields + f, 1), :] = all_ref[device, f, pl.ds(cell, 1), :]
-
-
-def call(kernel, name, args, scalars, outs, scratch, flops):
-    specs = [pl.BlockSpec(memory_space=SMEM)] * scalars
-    specs += [pl.BlockSpec(memory_space=VMEM)] * (len(args) - scalars)
+            out_ref[pl.ds(p * fields + f, 1), :] = gathered.line(0, device, f, cell)
+
+
+def first_kernel(count_ref, x_ref, v_ref, own_ref, live_ref, spread_ref):
+    ct, cc = count_ref.shape
+    shape = live_ref.shape
+    row = lax.broadcasted_iota(jnp.int32, shape, 0)
+    lane = lax.broadcasted_iota(jnp.int32, shape, 1)
+    count = jnp.zeros(shape, jnp.int32)
+    for cell in range(ct * cc):
+        count = jnp.where(row == cell, count_ref[cell // cc, cell % cc], count)
+    live = lane < count
+    live_ref[...] = jnp.where(live, 1.0, 0.0)
+    for axis in range(3):
+        x, v = x_ref[axis], v_ref[axis]
+        if axis == 0:
+            x = jnp.where(live, x, far)
+        own_ref[axis] = x
+        for k in range(spread_ref.shape[0]):
+            spread_ref[k, axis] = x
+            spread_ref[k, axis + 3] = v
+
+
+def update_kernel(second, live_ref, x_ref, v_ref, inner_ref, outer_ref, back_ref, *outs):
+    live = live_ref[...] > 0.5
+    for axis in range(3):
+        force = jnp.where(live, inner_ref[axis] + outer_ref[axis], 0.0)
+        for k in range(back_ref.shape[0]):
+            force = force + back_ref[k, axis]
+        x, v = advanced(x_ref[axis], v_ref[axis], force, axis)
+        outs[0][axis] = x
+        outs[1][axis] = v
+        if not second:
+            outs[2][axis] = jnp.where(live, x, far) if axis == 0 else x
+            for k in range(back_ref.shape[0]):
+                outs[3][k, axis] = force
+
+
+def call(kernel, name, scalars, args, outs, scratch, flops, keep=True):
+    specs = [pl.BlockSpec(memory_space=SMEM)] * len(scalars)
+    specs += [pl.BlockSpec(memory_space=VMEM)] * len(args)
+    shapes = [VMEM(s, f32) if keep else jax.ShapeDtypeStruct(s, f32) for s in outs]
     return pl.pallas_call(
         kernel,
         name=name,
-        out_shape=[jax.ShapeDtypeStruct(s, f32) for s in outs],
+        out_shape=shapes,
         in_specs=specs,
         out_specs=[pl.BlockSpec(memory_space=VMEM)] * len(outs),
         scratch_shapes=scratch,
+        compiler_params=pltpu.CompilerParams(vmem_limit_bytes=scratch_bytes),
         cost_estimate=pl.CostEstimate(flops=flops, transcendentals=0, bytes_accessed=0),
-    )(*args)
+    )(*scalars, *[pltpu.with_memory_space_constraint(a, VMEM_SPACE) for a in args])
 
 
 def body(
@@ -374,8 +452,9 @@
     cells = ct * cc
     own_faces, _, faces = face_offset.shape
     vehicles, tracks, crosses = [lax.axis_size(a) for a in ("vehicle", "track", "cross")]
-    vehicle, track, cross = [lax.axis_index(a) for a in ("vehicle", "track", "cross")]
     pair = tracks == 2
+    nrefs = 2 if pair else 1
+    devices = tracks * crosses
     wide = cc + 2
     grid_slots = (ct + 2) * wide
     ring_slots = [
@@ -384,95 +463,64 @@
         VMEM((grid_slots, 32, 2 * slots), bf16),
         VMEM((cells, 80, 2 * slots), bf16),
     ]
-
-    x = particle_offset.reshape(3, cells, slots)
-    v = particle_velocity.reshape(3, cells, slots)
-    live = (
-        lax.broadcasted_iota(jnp.int32, (cells, slots), 1) < cell_count.reshape(cells)[:, None]
-    )
-    first = lax.broadcasted_iota(jnp.int32, (3, 1, 1), 0) == 0
-
-    def marked(x):
-        return jnp.where(first & ~live[None], far, x)
-
-    def place(t):
-        return jnp.bitwise_xor(t, track) if pair else t
-
-    low, high = track > 0, track < tracks - 1
-    target = face_route[:, 0]
-    index = (place(target // crosses) * crosses + target % crosses) * cells + face_cell
-    scalars = jnp.stack(
-        [
-            cross,
-            place(track),
-            low,
-            place(jnp.maximum(track - 1, 0)),
-            low | (vehicle > 0),
-            high,
-            place(jnp.minimum(track + 1, tracks - 1)),
-            high | (vehicle < vehicles - 1),
-            jnp.where(high, 0, ct - 1),
-        ]
-    ).astype(jnp.int32)
+    block = (3, cells, slots)
     swap = [(0, 1), (1, 0)]
     travel = []
     for e in range(vehicles - 1):
         last, following = e * tracks + tracks - 1, (e + 1) * tracks
         travel += [(last, following), (following, last)]
 
-    def gather_cross(a):
-        spread = jnp.broadcast_to(a[None], (crosses,) + a.shape)
-        return lax.all_to_all(spread, "cross", split_axis=0, concat_axis=0, tiled=True)
+    def exchange(a):
+        return lax.all_to_all(a, "cross", split_axis=0, concat_axis=0, tiled=True)
 
     def gather_track(a):
         if pair:
-            return jnp.concatenate([a, lax.ppermute(a, "track", swap)], axis=0)
-        return lax.all_gather(a, "track", axis=0, tiled=True)
-
-    def scatter_force(part):
-        part = part.reshape(tracks, crosses, 3, cells, slots)
+            return [a, lax.ppermute(a, "track", swap)]
+        return [lax.all_gather(a, "track", axis=0, tiled=True)]
+
+    def sum_track(parts):
         if pair:
-            part = part[0] + lax.ppermute(part[1], "track", swap)
-        else:
-            part = jnp.sum(lax.all_to_all(part, "track", 0, 0, tiled=True), axis=0)
-        return lax.all_to_all(part, "cross", 0, 0, tiled=True)
-
-    fall = jnp.array(falls, f32)[:, None, None]
-    reaction = None
-    everyone = beyond = None
-    force = None
+            return parts[0] + lax.ppermute(parts[1], "track", swap)
+        part = parts[0].reshape(tracks, crosses, 3, cells, slots)
+        return jnp.sum(lax.all_to_all(part, "track", 0, 0, tiled=True), axis=0)
+
+    x = particle_offset.reshape(block)
+    v = particle_velocity.reshape(block)
+    offset_rows = jnp.transpose(face_offset, (1, 0, 2))
+    velocity_rows = jnp.transpose(face_velocity, (1, 0, 2))
+    own, live, spread = call(
+        first_kernel,
+        "first",
+        [cell_count],
+        [x, v],
+        [block, (cells, slots), (crosses, 6, cells, slots)],
+        [],
+        10**6,
+    )
+    reaction = everyone = beyond = None
     for substep in range(2):
         second = substep == 1
-        own = marked(x)
-        mine = gather_cross(force if second else jnp.concatenate([own, v], axis=0))
+        mine = exchange(spread)
         inner = call(
-            functools.partial(inner_kernel, ct, cc),
-            "inner",
-            [own, v],
-            0,
-            [(3, cells, slots)],
-            ring_slots,
-            4 * 10**9,
+            functools.partial(inner_kernel, ct, cc), "inner", [], [own, v], [block], ring_slots, 10**9
         )[0]
         mine, inner = lax.optimization_barrier((mine, inner))
         group = gather_track(mine)
         if second:
-            extra, before = [group], [reaction]
+            extra, before = group, [reaction]
         else:
             everyone, extra, before = group, [], []
-        part, reaction, packed = call(
-            functools.partial(face_kernel, second, cc, crosses),
+        *parts, reaction, packed = call(
+            functools.partial(face_kernel, second, ct, cc, crosses, nrefs),
             "faces",
-            [scalars, index, face_offset, face_velocity, everyone] + extra + before,
-            2,
+            [face_route.reshape(own_faces), face_cell],
+            [offset_rows, velocity_rows] + everyone + extra + before,
+            [(devices // nrefs, 3, cells, slots)] * nrefs
+            + [(3, own_faces, faces), (wide * group[0].shape[1], slots)],
             [
-                (tracks * crosses, 3, cells, slots),
-                (own_faces, 3, faces),
-                (wide * group.shape[1], slots),
-            ],
-            [
-                VMEM((tracks * crosses * cells * 8, slots), f32),
+                VMEM((devices * cells * 8, slots), f32),
                 VMEM((own_faces * 8, faces), f32),
+                VMEM((devices, 3, cells, slots), f32),
             ],
             4 * 10**9,
         )
@@ -482,20 +530,30 @@
         else:
             beyond, halo_extra = across, []
         outer = call(
-            functools.partial(outer_kernel, ct, cc, crosses, second),
+            functools.partial(outer_kernel, ct, cc, crosses, nrefs, second),
             "outer",
-            [scalars, own, v, everyone, beyond] + extra + halo_extra,
-            1,
-            [(3, cells, slots)],
+            [],
+            [own, v] + everyone + [beyond] + extra + halo_extra,
+            [block],
             ring_slots,
-            4 * 10**9,
+            10**9,
         )[0]
-        returned, outer = lax.optimization_barrier((scatter_force(part), outer))
-        force = jnp.where(live[None], inner + outer, 0.0) + jnp.sum(returned, axis=0)
-        v = v + time_step * (force + fall)
-        x = x + time_step * v
+        returned, outer = lax.optimization_barrier((exchange(sum_track(parts)), outer))
+        new = call(
+            functools.partial(update_kernel, second),
+            "update",
+            [],
+            [live, x, v, inner, outer, returned],
+            [block, block] if second else [block, block, block, (crosses, 3, cells, slots)],
+            [],
+            10**6,
+            not second,
+        )
+        x, v = new[:2]
+        if not second:
+            own, spread = new[2:]
     shape = particle_offset.shape
-    return (x.reshape(shape), v.reshape(shape), reaction)
+    return (x.reshape(shape), v.reshape(shape), jnp.transpose(reaction, (1, 0, 2)))
 
 
 def solution(mesh):

time: 77.9 us -> 70.7 us (0.908)
  waiting for transfers between devices: 1.45 us -> 11.1 us
  local copies, waits for them, and re-layouts: 11.7 us -> 3.47 us
  Pallas kernels: 30.5 us -> 23.8 us
  other arithmetic: 4.17 us -> 1.29 us
  starting transfers between devices: 28.1 us -> 29.1 us
    pallas_call x6 -> x9, Pallas kernels: 30.5 us -> 23.8 us  [call(): pl.pallas_call(kernel, name=name, out_shape=shapes, in_specs=specs, out_s...]
    unnamed x49 -> x19, local copies, waits for them, and re-layouts: 7.63 us -> 3.47 us
    ppermute x2, waiting for transfers between devices: 0.01 us -> 3.99 us  [body(): across = lax.ppermute(packed, ('vehicle', 'track'), travel)]
    ppermute x4, waiting for transfers between devices: 0.94 us -> 3.91 us  [the longest x2 2.01 us: gather_track(): return [a, lax.ppermute(a, 'track', swap)]]
    all_to_all x4, waiting for transfers between devices: 0.5 us -> 3.2 us  [exchange(): return lax.all_to_all(a, 'cross', split_axis=0, concat_axis=0, tiled=True)]
    slice x2 -> x0, local copies, waits for them, and re-layouts: 1.94 us -> none  [scatter_force(): part = part[0] + lax.ppermute(part[1], 'track', swap)]
    select_n x2 -> x0, other arithmetic: 1.51 us -> none  [marked(): return jnp.where(first & ~live[None], far, x)]
    broadcast_in_dim x2 -> x0, local copies, waits for them, and re-layouts: 1.33 us -> none  [gather_cross(): spread = jnp.broadcast_to(a[None], (crosses,) + a.shape)]
  transfers between devices with their start and end apart: 10 -> 10, of which waited for: 3 -> 8; matrix products, arithmetic and copies ran while one was open for 6% -> 1% of each run, Pallas kernels for 24% -> 18%
where the time goes in v3:
time: 70.7 us; the launch traced here: 69.5 us
  starting transfers between devices  29.1 us (41%)
  Pallas kernels  23.8 us (34%)
  waiting for transfers between devices  11.1 us (16%)
  local copies, waits for them, and re-layouts  3.47 us (5%)
  other arithmetic  1.29 us (2%)
  between operations  0.74 us (1%)
    pallas_call x9, Pallas kernels, call(): pl.pallas_call(kernel, name=name, out_shape=shapes, in_specs=specs, out_s...  23.8 us
    all_to_all x4, starting transfers between devices, exchange(): return lax.all_to_all(a, 'cross', split_axis=0, concat_axis=0, tiled=True)  17.5 us
    ppermute x2, starting transfers between devices, body(): across = lax.ppermute(packed, ('vehicle', 'track'), travel)  8 us
    ppermute x2, waiting for transfers between devices, body(): across = lax.ppermute(packed, ('vehicle', 'track'), travel)  3.99 us
    unnamed x19, local copies, waits for them, and re-layouts  3.47 us
    all_to_all x4, waiting for transfers between devices, exchange(): return lax.all_to_all(a, 'cross', split_axis=0, concat_axis=0, tiled=True)  3.2 us
    ppermute x2, starting transfers between devices, gather_track(): return [a, lax.ppermute(a, 'track', swap)]  2.74 us
    ppermute x2, waiting for transfers between devices, gather_track(): return [a, lax.ppermute(a, 'track', swap)]  2.01 us
  transfers between devices with their start and end apart: 10, of which 8 were waited for; matrix products, arithmetic and copies ran while one was open for 1% of the time, Pallas kernels for 18%

profile of v3, /device:TPU:11, one launch (start us, length us, event | category | flops | bytes accessed | tf_op | source)
XLA Modules:
  0.0 69.5 jit_solution(4346322833067217379)
XLA Ops:
  1.3 0.7 %copy-done = f32[3,2,8,128]{3,2,1,0:T(8,128)S(1)} copy-done((f32[3,2,8,128]{3,2,1,0:T(8,128)S(1)}, f32[3,2,8,128]{3,2,1,0:T(8,128)}, u32[]{:S(2)}) %copy-start) | copy-done | bytes 24600
  2.0 0.7 %copy-done.2 = f32[3,2,8,128]{3,2,1,0:T(8,128)S(1)} copy-done((f32[3,2,8,128]{3,2,1,0:T(8,128)S(1)}, f32[3,2,8,128]{3,2,1,0:T(8,128)}, u32[]{:S(2)}) %copy-start.2) | copy-done | bytes 24600
  2.8 1.2 %first.1 = (f32[3,16,128]{2,1,0:T(8,128)S(1)}, f32[16,128]{1,0:T(8,128)S(1)}, f32[4,6,16,128]{3,2,1,0:T(8,128)}) custom-call(s32[2,8]{1,0:T(2,128)S(1)} %copy-done.4, f32[3,16,128]{2,1,0:T(8,128)S(1)} %bitcast.9, f32[3,16,128]{2,1,0:T(8,128)S(1)} %bitcast.11), custom_call_target="tpu_custom_call" | custom-call | flops 1000000 | tf_op jit(solution)/shard_map/first/pallas_call | solution.py:430
  4.0 4.9 %all-to-all-start = ((f32[4,6,16,128]{3,2,1,0:T(8,128)}), f32[4,6,16,128]{3,2,1,0:T(8,128)S(1)}, u32[]{:S(2)}, u32[]{:S(2)}) async-start(f32[4,6,16,128]{3,2,1,0:T(8,128)} %get-tuple-element.29), calls=%async_computation | async-start | bytes 393216 | tf_op jit(solution)/shard_map/all_to_all | solution.py:474
  8.9 3.4 %inner.2.inner_ref = f32[3,16,128]{2,1,0:T(8,128)S(1)} custom-call(f32[3,16,128]{2,1,0:T(8,128)S(1)} %get-tuple-element.30.x_ref, f32[3,16,128]{2,1,0:T(8,128)S(1)} %bitcast.12), custom_call_target="tpu_custom_call" | custom-call | flops 1000000000 | tf_op jit(solution)/shard_map/inner/pallas_call | solution.py:430
  12.3 1.6 %all-to-all-done.rest_0_ = f32[4,6,16,128]{3,2,1,0:T(8,128)S(1)} async-done(((f32[4,6,16,128]{3,2,1,0:T(8,128)}), f32[4,6,16,128]{3,2,1,0:T(8,128)S(1)}, u32[]{:S(2)}, u32[]{:S(2)}) %all-to-all-start) | async-done | bytes 196640 | tf_op jit(solution)/shard_map/all_to_all | solution.py:474
  13.9 2.2 %collective-permute-start = (f32[4,6,16,128]{3,2,1,0:T(8,128)S(1)}, f32[4,6,16,128]{3,2,1,0:T(8,128)S(1)}, u32[]{:S(2)}, u32[]{:S(2)}) collective-permute-start(f32[4,6,16,128]{3,2,1,0:T(8,128)S(1)} %all-to-all-done.rest_0_), channel_id=1, source_target_pairs={{0,4},{4,0},{1,5},{5,1},{2,6},{6,2},{3,7},{7,3},{8,12},{12,8},{9,1... | collective-permute-start | bytes 589832 | tf_op jit(solution)/shard_map/ppermute | solution.py:478
  16.1 1.1 %collective-permute-done.rest_1_ = f32[4,6,16,128]{3,2,1,0:T(8,128)S(1)} collective-permute-done((f32[4,6,16,128]{3,2,1,0:T(8,128)S(1)}, f32[4,6,16,128]{3,2,1,0:T(8,128)S(1)}, u32[]{:S(2)}, u32[]{:S(2)}) %collective-permute-start) | collective-permute-done | bytes 196640 | tf_op jit(solution)/shard_map/ppermute | solution.py:478
  17.8 4.5 %faces.2 = (f32[4,3,16,128]{3,2,1,0:T(8,128)S(1)}, f32[4,3,16,128]{3,2,1,0:T(8,128)S(1)}, f32[3,64,128]{2,1,0:T(8,128)S(1)}, f32[60,128]{1,0:T(8,128)S(1)}) custom-call(s32[64]{0:T(128)S(1)} %bitcast.19, s32[64]{0:T(128)S(1)} %copy-done.8, f32[3,64,128]{2,1,0:T(8,128)S(1)} %bitcast.15, f32[3,64,128]{2,1,0:T(8,128)S(1)} %bitcast.17, ...), custom_call_target="tpu_custom_call" | custom-call | flops 4000000000 | tf_op jit(solution)/shard_map/faces/pallas_call | solution.py:430
  22.8 0.9 %collective-permute-done.1 = f32[4,3,16,128]{3,2,1,0:T(8,128)S(1)} collective-permute-done((f32[4,3,16,128]{3,2,1,0:T(8,128)S(1)}, f32[4,3,16,128]{3,2,1,0:T(8,128)S(1)}, u32[]{:S(2)}, u32[]{:S(2)}) %collective-permute-start.1) | collective-permute-done | bytes 98336 | tf_op jit(solution)/shard_map/ppermute | solution.py:483
  24.4 4.6 %all-to-all-start.1 = ((f32[4,3,16,128]{3,2,1,0:T(8,128)}), f32[4,3,16,128]{3,2,1,0:T(8,128)S(1)}, u32[]{:S(2)}, u32[]{:S(2)}) async-start(f32[4,3,16,128]{3,2,1,0:T(8,128)} %add.6), calls=%async_computation.1 | async-start | bytes 196608 | tf_op jit(solution)/shard_map/all_to_all | solution.py:474
  28.9 3.8 %collective-permute-start.2 = (f32[60,128]{1,0:T(8,128)S(1)}, f32[60,128]{1,0:T(8,128)S(1)}, u32[]{:S(2)}, u32[]{:S(2)}) collective-permute-start(f32[60,128]{1,0:T(8,128)S(1)} %get-tuple-element.35), channel_id=1, source_target_pairs={{4,8},{8,4},{12,16},{16,12},{20,24},{24,20},{5,9},{9,5},{13,17},{1... | collective-permute-start | bytes 92168 | tf_op jit(solution)/shard_map/ppermute | solution.py:527
  32.7 2.8 %collective-permute-done.2.rest_2_ = f32[60,128]{1,0:T(8,128)S(1)} collective-permute-done((f32[60,128]{1,0:T(8,128)S(1)}, f32[60,128]{1,0:T(8,128)S(1)}, u32[]{:S(2)}, u32[]{:S(2)}) %collective-permute-start.2) | collective-permute-done | bytes 30752 | tf_op jit(solution)/shard_map/ppermute | solution.py:527
  35.5 2.7 %outer.2.outer_ref = f32[3,16,128]{2,1,0:T(8,128)S(1)} custom-call(f32[3,16,128]{2,1,0:T(8,128)S(1)} %get-tuple-element.30.x_ref, f32[3,16,128]{2,1,0:T(8,128)S(1)} %bitcast.13, f32[4,6,16,128]{3,2,1,0:T(8,128)S(1)} %all-to-all-done.rest_0_, f32[4,6,16,128]{3,2,1,0:T(8,128)S(1)} %collective-permute-done.rest_1_, f32[60,128]{1,0:T(8,128)S(1)} %collective-permute-done.2.rest_2_), custom_call_target="tpu_custom_call" | custom-call | flops 1000000000 | tf_op jit(solution)/shard_map/outer/pallas_call | solution.py:430
  38.9 4.5 %all-to-all-start.2 = ((f32[4,3,16,128]{3,2,1,0:T(8,128)}), f32[4,3,16,128]{3,2,1,0:T(8,128)S(1)}, u32[]{:S(2)}, u32[]{:S(2)}) async-start(f32[4,3,16,128]{3,2,1,0:T(8,128)} %get-tuple-element.40), calls=%async_computation.2 | async-start | bytes 196608 | tf_op jit(solution)/shard_map/all_to_all | solution.py:474
  43.5 3.4 %inner.3.inner_ref = f32[3,16,128]{2,1,0:T(8,128)S(1)} custom-call(f32[3,16,128]{2,1,0:T(8,128)S(1)} %get-tuple-element.41.x_ref, f32[3,16,128]{2,1,0:T(8,128)S(1)} %get-tuple-element.39.v_ref), custom_call_target="tpu_custom_call" | custom-call | flops 1000000000 | tf_op jit(solution)/shard_map/inner/pallas_call | solution.py:430
  46.9 1.6 %all-to-all-done.2.rest_2_.rest_3_ = f32[4,3,16,128]{3,2,1,0:T(8,128)S(1)} async-done(((f32[4,3,16,128]{3,2,1,0:T(8,128)}), f32[4,3,16,128]{3,2,1,0:T(8,128)S(1)}, u32[]{:S(2)}, u32[]{:S(2)}) %all-to-all-start.2) | async-done | bytes 98336 | tf_op jit(solution)/shard_map/all_to_all | solution.py:474
  49.0 0.9 %collective-permute-done.3.rest_3_.rest_4_ = f32[4,3,16,128]{3,2,1,0:T(8,128)S(1)} collective-permute-done((f32[4,3,16,128]{3,2,1,0:T(8,128)S(1)}, f32[4,3,16,128]{3,2,1,0:T(8,128)S(1)}, u32[]{:S(2)}, u32[]{:S(2)}) %collective-permute-start.3) | collective-permute-done | bytes 98336 | tf_op jit(solution)/shard_map/ppermute | solution.py:478
  49.9 4.5 %faces.3 = (f32[4,3,16,128]{3,2,1,0:T(8,128)S(1)}, f32[4,3,16,128]{3,2,1,0:T(8,128)S(1)}, f32[3,64,128]{2,1,0:T(8,128)S(1)}, f32[30,128]{1,0:T(8,128)S(1)}) custom-call(s32[64]{0:T(128)S(1)} %bitcast.20, s32[64]{0:T(128)S(1)} %copy-done.8, f32[3,64,128]{2,1,0:T(8,128)S(1)} %bitcast.16, f32[3,64,128]{2,1,0:T(8,128)S(1)} %bitcast.18, ...), custom_call_target="tpu_custom_call" | custom-call | flops 4000000000 | tf_op jit(solution)/shard_map/faces/pallas_call | solution.py:430
  54.9 0.9 %collective-permute-done.4 = f32[4,3,16,128]{3,2,1,0:T(8,128)S(1)} collective-permute-done((f32[4,3,16,128]{3,2,1,0:T(8,128)S(1)}, f32[4,3,16,128]{3,2,1,0:T(8,128)S(1)}, u32[]{:S(2)}, u32[]{:S(2)}) %collective-permute-start.4) | collective-permute-done | bytes 98336 | tf_op jit(solution)/shard_map/ppermute | solution.py:483
  56.5 3.6 %all-to-all-start.3 = ((f32[4,3,16,128]{3,2,1,0:T(8,128)}), f32[4,3,16,128]{3,2,1,0:T(8,128)S(1)}, u32[]{:S(2)}, u32[]{:S(2)}) async-start(f32[4,3,16,128]{3,2,1,0:T(8,128)} %add.7), calls=%async_computation.3 | async-start | bytes 196608 | tf_op jit(solution)/shard_map/all_to_all | solution.py:474
  60.0 4.2 %collective-permute-start.5 = (f32[30,128]{1,0:T(8,128)S(1)}, f32[30,128]{1,0:T(8,128)S(1)}, u32[]{:S(2)}, u32[]{:S(2)}) collective-permute-start(f32[30,128]{1,0:T(8,128)S(1)} %get-tuple-element.47), channel_id=1, source_target_pairs={{4,8},{8,4},{12,16},{16,12},{20,24},{24,20},{5,9},{9,5},{13,17},{1... | collective-permute-start | bytes 46088 | tf_op jit(solution)/shard_map/ppermute | solution.py:527
  64.9 1.2 %collective-permute-done.5.rest_5_ = f32[30,128]{1,0:T(8,128)S(1)} collective-permute-done((f32[30,128]{1,0:T(8,128)S(1)}, f32[30,128]{1,0:T(8,128)S(1)}, u32[]{:S(2)}, u32[]{:S(2)}) %collective-permute-start.5) | collective-permute-done | bytes 15392 | tf_op jit(solution)/shard_map/ppermute | solution.py:527
  66.1 2.8 %outer.3.outer_ref = f32[3,16,128]{2,1,0:T(8,128)S(1)} custom-call(f32[3,16,128]{2,1,0:T(8,128)S(1)} %get-tuple-element.41.x_ref, f32[3,16,128]{2,1,0:T(8,128)S(1)} %get-tuple-element.39.v_ref, f32[4,6,16,128]{3,2,1,0:T(8,128)S(1)} %all-to-all-done.rest_0_, f32[4,6,16,128]{3,2,1,0:T(8,128)S(1)} %collective-permute-done.rest_1_, ...), custom_call_target="tpu_custom_call" | custom-call | flops 1000000000 | tf_op jit(solution)/shard_map/outer/pallas_call | solution.py:430
  (26 shorter events, 6.0 us)
Async XLA Ops:
  0.6 0.7 copy-start.4
  1.3 0.7 %copy-start = (f32[3,2,8,128]{3,2,1,0:T(8,128)S(1)}, f32[3,2,8,128]{3,2,1,0:T(8,128)}, u32[]{:S(2)}) copy-start(f32[3,2,8,128]{3,2,1,0:T(8,128)} %param.7) | copy-start | bytes 73732
  2.0 0.7 %copy-start.2 = (f32[3,2,8,128]{3,2,1,0:T(8,128)S(1)}, f32[3,2,8,128]{3,2,1,0:T(8,128)}, u32[]{:S(2)}) copy-start(f32[3,2,8,128]{3,2,1,0:T(8,128)} %param.8) | copy-start | bytes 73732
  4.0 4.9 %copy-start.3 = (f32[3,2,8,128]{3,2,1,0:T(8,128)S(1)}, f32[3,2,8,128]{3,2,1,0:T(8,128)}, u32[]{:S(2)}) copy-start(f32[3,2,8,128]{3,2,1,0:T(8,128)} %param.8) | copy-start | bytes 73732
  4.0 9.9 %all-to-all-start = ((f32[4,6,16,128]{3,2,1,0:T(8,128)}), f32[4,6,16,128]{3,2,1,0:T(8,128)S(1)}, u32[]{:S(2)}, u32[]{:S(2)}) async-start(f32[4,6,16,128]{3,2,1,0:T(8,128)} %get-tuple-element.29), calls=%async_computation | async-start | bytes 393216 | tf_op jit(solution)/shard_map/all_to_all | solution.py:474
  8.9 8.3 %copy-start.5 = (f32[64,3,128]{2,0,1:T(8,128)S(1)}, f32[64,3,128]{2,0,1:T(8,128)}, u32[]{:S(2)}) copy-start(f32[64,3,128]{2,0,1:T(8,128)} %param.10) | copy-start | bytes 294916
  8.9 8.3 %copy-start.6 = (f32[64,3,128]{2,0,1:T(8,128)S(1)}, f32[64,3,128]{2,0,1:T(8,128)}, u32[]{:S(2)}) copy-start(f32[64,3,128]{2,0,1:T(8,128)} %param.11) | copy-start | bytes 294916
  13.9 3.3 %collective-permute-start = (f32[4,6,16,128]{3,2,1,0:T(8,128)S(1)}, f32[4,6,16,128]{3,2,1,0:T(8,128)S(1)}, u32[]{:S(2)}, u32[]{:S(2)}) collective-permute-start(f32[4,6,16,128]{3,2,1,0:T(8,128)S(1)} %all-to-all-done.rest_0_), channel_id=1, source_target_pairs={{0,4},{4,0},{1,5},{5,1},{2,6},{6,2},{3,7},{7,3},{8,12},{12,8},{9,1... | collective-permute-start | bytes 589832 | tf_op jit(solution)/shard_map/ppermute | solution.py:478
  17.2 0.7 copy-start.7
  17.2 0.7 copy-start.8
  22.4 1.4 %collective-permute-start.1 = (f32[4,3,16,128]{3,2,1,0:T(8,128)S(1)}, f32[4,3,16,128]{3,2,1,0:T(8,128)S(1)}, u32[]{:S(2)}, u32[]{:S(2)}) collective-permute-start(f32[4,3,16,128]{3,2,1,0:T(8,128)S(1)} %get-tuple-element.34), channel_id=1, source_target_pairs={{0,4},{4,0},{1,5},{5,1},{2,6},{6,2},{3,7},{7,3},{8,12},{12,8},{9,1... | collective-permute-start | bytes 294920 | tf_op jit(solution)/shard_map/ppermute | solution.py:483
  24.4 13.9 %all-to-all-start.1 = ((f32[4,3,16,128]{3,2,1,0:T(8,128)}), f32[4,3,16,128]{3,2,1,0:T(8,128)S(1)}, u32[]{:S(2)}, u32[]{:S(2)}) async-start(f32[4,3,16,128]{3,2,1,0:T(8,128)} %add.6), calls=%async_computation.1 | async-start | bytes 196608 | tf_op jit(solution)/shard_map/all_to_all | solution.py:474
  28.9 9.3 %copy-start.1 = (f32[3,2,8,128]{3,2,1,0:T(8,128)S(1)}, f32[3,2,8,128]{3,2,1,0:T(8,128)}, u32[]{:S(2)}) copy-start(f32[3,2,8,128]{3,2,1,0:T(8,128)} %param.7) | copy-start | bytes 73732
  28.9 6.6 %collective-permute-start.2 = (f32[60,128]{1,0:T(8,128)S(1)}, f32[60,128]{1,0:T(8,128)S(1)}, u32[]{:S(2)}, u32[]{:S(2)}) collective-permute-start(f32[60,128]{1,0:T(8,128)S(1)} %get-tuple-element.35), channel_id=1, source_target_pairs={{4,8},{8,4},{12,16},{16,12},{20,24},{24,20},{5,9},{9,5},{13,17},{1... | collective-permute-start | bytes 92168 | tf_op jit(solution)/shard_map/ppermute | solution.py:527
  38.9 9.5 %all-to-all-start.2 = ((f32[4,3,16,128]{3,2,1,0:T(8,128)}), f32[4,3,16,128]{3,2,1,0:T(8,128)S(1)}, u32[]{:S(2)}, u32[]{:S(2)}) async-start(f32[4,3,16,128]{3,2,1,0:T(8,128)} %get-tuple-element.40), calls=%async_computation.2 | async-start | bytes 196608 | tf_op jit(solution)/shard_map/all_to_all | solution.py:474
  48.5 1.5 %collective-permute-start.3 = (f32[4,3,16,128]{3,2,1,0:T(8,128)S(1)}, f32[4,3,16,128]{3,2,1,0:T(8,128)S(1)}, u32[]{:S(2)}, u32[]{:S(2)}) collective-permute-start(f32[4,3,16,128]{3,2,1,0:T(8,128)S(1)} %all-to-all-done.2.rest_2_.rest_3_), channel_id=1, source_target_pairs={{0,4},{4,0},{1,5},{5,1},{2,6},{6,2},{3,7},{7,3},{8,12},{12,8},{9,1... | collective-permute-start | bytes 294920 | tf_op jit(solution)/shard_map/ppermute | solution.py:478
  54.5 1.4 %collective-permute-start.4 = (f32[4,3,16,128]{3,2,1,0:T(8,128)S(1)}, f32[4,3,16,128]{3,2,1,0:T(8,128)S(1)}, u32[]{:S(2)}, u32[]{:S(2)}) collective-permute-start(f32[4,3,16,128]{3,2,1,0:T(8,128)S(1)} %get-tuple-element.46), channel_id=1, source_target_pairs={{0,4},{4,0},{1,5},{5,1},{2,6},{6,2},{3,7},{7,3},{8,12},{12,8},{9,1... | collective-permute-start | bytes 294920 | tf_op jit(solution)/shard_map/ppermute | solution.py:483
  56.5 12.4 %all-to-all-start.3 = ((f32[4,3,16,128]{3,2,1,0:T(8,128)}), f32[4,3,16,128]{3,2,1,0:T(8,128)S(1)}, u32[]{:S(2)}, u32[]{:S(2)}) async-start(f32[4,3,16,128]{3,2,1,0:T(8,128)} %add.7), calls=%async_computation.3 | async-start | bytes 196608 | tf_op jit(solution)/shard_map/all_to_all | solution.py:474
  60.0 6.1 %collective-permute-start.5 = (f32[30,128]{1,0:T(8,128)S(1)}, f32[30,128]{1,0:T(8,128)S(1)}, u32[]{:S(2)}, u32[]{:S(2)}) collective-permute-start(f32[30,128]{1,0:T(8,128)S(1)} %get-tuple-element.47), channel_id=1, source_target_pairs={{4,8},{8,4},{12,16},{16,12},{20,24},{24,20},{5,9},{9,5},{13,17},{1... | collective-permute-start | bytes 46088 | tf_op jit(solution)/shard_map/ppermute | solution.py:527

commit v4 on v3

--- a/solution.py
+++ b/solution.py
@@ -112,11 +112,6 @@
                 x = x + (cells + (1 - (cc + 1) / 2))
             state_ref[pl.ds(base + axis, cc, stride=8), :] = x
             state_ref[pl.ds(base + 3 + axis, cc, stride=8), :] = v_ref[axis, pl.ds(r * cc, cc), :]
-
-
-def put_dead(state_ref, slot):
-    row = lax.broadcasted_iota(jnp.int32, (8, 128), 0)
-    state_ref[pl.ds(slot * 8, 8), :] = jnp.where(row == 0, far, 0.0)
 
 
 def build_left(state_ref, left_ref, sum_ref, slots):
@@ -156,30 +151,35 @@
         out_ref[axis, pl.ds(index, 1), :] = line
 
 
-def inner_kernel(ct, cc, x_ref, v_ref, out_ref, state_ref, left_ref, sum_ref, right_ref):
+def inner_kernel(ct, cc, x_ref, v_ref, out_ref, right_ref, state_ref, left_ref, sum_ref):
     wide = cc + 2
     own = [(r + 1) * wide + c + 1 for r in range(ct) for c in range(cc)]
-    ends = [(r + 1) * wide + c for r in range(ct) for c in (0, cc + 1)]
     put_own(state_ref, x_ref, v_ref, ct, cc)
-    for slot in ends:
-        put_dead(state_ref, slot)
-    build_left(state_ref, left_ref, sum_ref, own + ends)
+    build_left(state_ref, left_ref, sum_ref, own)
     build_right(state_ref, right_ref, own)
 
-    def several(step, carry):
+    def finish(cells):
         jobs, places = [], []
-        for k in range(columns):
-            c = step * columns + k
+        for c, steps in cells:
             for r in range(ct):
                 near = range(max(r - 1, 0), min(r + 2, ct))
-                jobs.append((r * cc + c, [(q + 1) * wide + c + d for q in near for d in range(3)]))
+                jobs.append(
+                    (r * cc + c, [(q + 1) * wide + c + 1 + d for q in near for d in steps])
+                )
                 places.append(((r + 1) * wide + c + 1, r * cc + c))
         for sums, (slot, index) in zip(pushes(left_ref, sum_ref, right_ref, jobs), places):
-            state = state_ref[pl.ds(pl.multiple_of(slot * 8, 8), 8), :]
-            store_rows(out_ref, moment(state, sums), index, False)
+            start = slot * 8 if isinstance(slot, int) else pl.multiple_of(slot * 8, 8)
+            store_rows(out_ref, moment(state_ref[pl.ds(start, 8), :], sums), index, False)
+
+    def several(step, carry):
+        finish([(1 + step * columns + k, (-1, 0, 1)) for k in range(columns)])
         return carry
 
-    lax.fori_loop(0, cc // columns, several, 0)
+    assert cc >= 2
+    middle = cc - 2
+    lax.fori_loop(0, middle // columns, several, 0)
+    rest = [(c, (-1, 0, 1)) for c in range(1 + middle // columns * columns, cc - 1)]
+    finish(rest + [(0, (0, 1)), (cc - 1, (-1, 0))])
 
 
 class Gathered:
@@ -194,7 +194,7 @@
         return self.refs[0][track * self.crosses + device, field, pl.ds(cell, 1), :]
 
 
-def outer_kernel(ct, cc, crosses, nrefs, second, x_ref, v_ref, *rest):
+def outer_kernel(ct, cc, crosses, nrefs, second, x_ref, v_ref, right_ref, *rest):
     track, c_index = lax.axis_index("track"), lax.axis_index("cross")
     vehicle = lax.axis_index("vehicle")
     vehicles, tracks = lax.axis_size("vehicle"), lax.axis_size("track")
@@ -202,10 +202,10 @@
     halos = [rest[nrefs]]
     rest = rest[nrefs + 1 :]
     if second:
-        gathered.append(Gathered(rest[:nrefs], crosses, track))
-        halos.append(rest[nrefs])
-        rest = rest[nrefs + 1 :]
-    out_ref, state_ref, left_ref, sum_ref, right_ref = rest
+        gathered.append(Gathered(rest[:1], crosses, track))
+        halos.append(rest[1])
+        rest = rest[2:]
+    out_ref, state_ref, left_ref, sum_ref = rest
     wide = cc + 2
     has_low = c_index > 0
     has_high = c_index < crosses - 1
@@ -257,7 +257,6 @@
     ring = [rr * wide + p for rr in (0, ct + 1) for p in range(wide)]
     ring += [(r + 1) * wide + p for r in range(ct) for p in (0, cc + 1)]
     build_left(state_ref, left_ref, sum_ref, ring)
-    build_right(state_ref, right_ref, [(r + 1) * wide + c + 1 for r in range(ct) for c in range(cc)])
 
     def finish(jobs, places, add):
         for sums, (slot, index) in zip(pushes(left_ref, sum_ref, right_ref, jobs), places):
@@ -287,16 +286,23 @@
     finish(jobs, places, True)
 
 
-def face_kernel(second, ct, cc, crosses, nrefs, route_ref, cell_ref, offset_ref, velocity_ref, *rest):
+def face_kernel(second, ct, cc, crosses, nrefs, route_from, cell_from, offset_ref, velocity_ref, *rest):
     all_refs, rest = rest[:nrefs], rest[nrefs:]
     if second:
-        force_refs, before_ref, rest = rest[:nrefs], rest[nrefs], rest[nrefs + 1 :]
-    part_refs, (react_ref, halo_ref, state_ref, face_ref, part_ref) = rest[:nrefs], rest[nrefs:]
+        force_ref, before_ref, *rest = rest
+    out_ref, react_ref, halo_ref, state_ref, face_ref, part_ref, route_ref, cell_ref, sems = rest
+    copies = [
+        pltpu.make_async_copy(route_from, route_ref, sems.at[0]),
+        pltpu.make_async_copy(cell_from, cell_ref, sems.at[1]),
+    ]
+    for copy in copies:
+        copy.start()
     devices, _, cells, _ = all_refs[0].shape
     count = offset_ref.shape[1]
     track = lax.axis_index("track")
-    pack(ct, cc, crosses, track, force_refs if second else all_refs, halo_ref)
-
+    pack(ct, cc, crosses, track, [force_ref] if second else all_refs, halo_ref)
+
+    starts = [jnp.bitwise_xor(k, track) * devices if nrefs == 2 else 0 for k in range(nrefs)]
     for k in range(nrefs):
 
         def spread(device, carry, k=k):
@@ -304,7 +310,7 @@
             for axis in range(3):
                 x, v = all_refs[k][device, axis], all_refs[k][device, axis + 3]
                 if second:
-                    x, v = advanced(x, v, force_refs[k][device, axis], axis)
+                    x, v = advanced(x, v, force_ref[starts[k] + device, axis], axis)
                 state_ref[pl.ds(base + axis, cells, stride=8), :] = x
                 state_ref[pl.ds(base + 3 + axis, cells, stride=8), :] = v
                 part_ref[k * devices + device, axis] = jnp.zeros_like(x)
@@ -317,6 +323,9 @@
             y = y + time_step * w
         face_ref[pl.ds(axis, count, stride=8), :] = y
         face_ref[pl.ds(3 + axis, count, stride=8), :] = w
+
+    for copy in copies:
+        copy.wait()
 
     def block_of(f):
         target = route_ref[f]
@@ -372,7 +381,7 @@
 
     lax.fori_loop(0, count // group, several, 0)
     for k in range(nrefs):
-        part_refs[k][...] = part_ref[pl.ds(k * devices, devices)]
+        out_ref[pl.ds(starts[k], devices)] = part_ref[pl.ds(k * devices, devices)]
 
 
 def pack(ct, cc, crosses, track, refs, out_ref):
@@ -388,7 +397,19 @@
             out_ref[pl.ds(p * fields + f, 1), :] = gathered.line(0, device, f, cell)
 
 
-def first_kernel(count_ref, x_ref, v_ref, own_ref, live_ref, spread_ref):
+def first_kernel(
+    count_from, x_from, v_from, own_ref, live_ref, spread_ref, count_ref, x_ref, v_ref, sems
+):
+    copies = [
+        pltpu.make_async_copy(source, target, sems.at[k])
+        for k, (source, target) in enumerate(
+            ((count_from, count_ref), (x_from, x_ref), (v_from, v_ref))
+        )
+    ]
+    for copy in copies:
+        copy.start()
+    for copy in copies:
+        copy.wait()
     ct, cc = count_ref.shape
     shape = live_ref.shape
     row = lax.broadcasted_iota(jnp.int32, shape, 0)
@@ -408,7 +429,12 @@
             spread_ref[k, axis + 3] = v
 
 
-def update_kernel(second, live_ref, x_ref, v_ref, inner_ref, outer_ref, back_ref, *outs):
+def update_kernel(second, live_ref, x_ref, v_ref, inner_ref, outer_ref, back_ref, *rest):
+    if second:
+        react_ref, *outs = rest
+        outs[2][...] = react_ref[...]
+    else:
+        outs = rest
     live = live_ref[...] > 0.5
     for axis in range(3):
         force = jnp.where(live, inner_ref[axis] + outer_ref[axis], 0.0)
@@ -423,10 +449,13 @@
                 outs[3][k, axis] = force
 
 
-def call(kernel, name, scalars, args, outs, scratch, flops, keep=True):
-    specs = [pl.BlockSpec(memory_space=SMEM)] * len(scalars)
+def call(kernel, name, there, args, outs, scratch, flops, keep=True):
+    specs = [pl.BlockSpec(memory_space=pltpu.HBM)] * len(there)
     specs += [pl.BlockSpec(memory_space=VMEM)] * len(args)
-    shapes = [VMEM(s, f32) if keep else jax.ShapeDtypeStruct(s, f32) for s in outs]
+    there = [pltpu.with_memory_space_constraint(a, pltpu.HBM) for a in there]
+    args = [pltpu.with_memory_space_constraint(a, VMEM_SPACE) for a in args]
+    outs = [s if isinstance(s[0], tuple) else (s, f32) for s in outs]
+    shapes = [VMEM(s, t) if keep else jax.ShapeDtypeStruct(s, t) for s, t in outs]
     return pl.pallas_call(
         kernel,
         name=name,
@@ -436,7 +465,7 @@
         scratch_shapes=scratch,
         compiler_params=pltpu.CompilerParams(vmem_limit_bytes=scratch_bytes),
         cost_estimate=pl.CostEstimate(flops=flops, transcendentals=0, bytes_accessed=0),
-    )(*scalars, *[pltpu.with_memory_space_constraint(a, VMEM_SPACE) for a in args])
+    )(*there, *args)
 
 
 def body(
@@ -461,8 +490,8 @@
         VMEM((grid_slots * 8, slots), f32),
         VMEM((grid_slots, slots, 80), bf16),
         VMEM((grid_slots, 32, 2 * slots), bf16),
-        VMEM((cells, 80, 2 * slots), bf16),
     ]
+    right = ((cells, 80, 2 * slots), bf16)
     block = (3, cells, slots)
     swap = [(0, 1), (1, 0)]
     travel = []
@@ -470,19 +499,13 @@
         last, following = e * tracks + tracks - 1, (e + 1) * tracks
         travel += [(last, following), (following, last)]
 
-    def exchange(a):
-        return lax.all_to_all(a, "cross", split_axis=0, concat_axis=0, tiled=True)
+    def exchange(a, axes):
+        return lax.all_to_all(a, axes, split_axis=0, concat_axis=0, tiled=True)
 
     def gather_track(a):
         if pair:
             return [a, lax.ppermute(a, "track", swap)]
         return [lax.all_gather(a, "track", axis=0, tiled=True)]
-
-    def sum_track(parts):
-        if pair:
-            return parts[0] + lax.ppermute(parts[1], "track", swap)
-        part = parts[0].reshape(tracks, crosses, 3, cells, slots)
-        return jnp.sum(lax.all_to_all(part, "track", 0, 0, tiled=True), axis=0)
 
     x = particle_offset.reshape(block)
     v = particle_velocity.reshape(block)
@@ -491,36 +514,52 @@
     own, live, spread = call(
         first_kernel,
         "first",
-        [cell_count],
-        [x, v],
+        [cell_count, x, v],
+        [],
         [block, (cells, slots), (crosses, 6, cells, slots)],
-        [],
+        [
+            SMEM((ct, cc), jnp.int32),
+            VMEM(block, f32),
+            VMEM(block, f32),
+            pltpu.SemaphoreType.DMA((3,)),
+        ],
         10**6,
     )
     reaction = everyone = beyond = None
     for substep in range(2):
         second = substep == 1
-        mine = exchange(spread)
-        inner = call(
-            functools.partial(inner_kernel, ct, cc), "inner", [], [own, v], [block], ring_slots, 10**9
-        )[0]
+        mine = exchange(spread, ("track", "cross") if second else "cross")
+        inner, rights = call(
+            functools.partial(inner_kernel, ct, cc),
+            "inner",
+            [],
+            [own, v],
+            [block, right],
+            ring_slots,
+            10**9,
+        )
         mine, inner = lax.optimization_barrier((mine, inner))
-        group = gather_track(mine)
         if second:
-            extra, before = group, [reaction]
+            extra, before = [mine], [reaction]
         else:
-            everyone, extra, before = group, [], []
-        *parts, reaction, packed = call(
+            everyone, extra, before = gather_track(mine), [], []
+        part, reaction, packed = call(
             functools.partial(face_kernel, second, ct, cc, crosses, nrefs),
             "faces",
             [face_route.reshape(own_faces), face_cell],
             [offset_rows, velocity_rows] + everyone + extra + before,
-            [(devices // nrefs, 3, cells, slots)] * nrefs
-            + [(3, own_faces, faces), (wide * group[0].shape[1], slots)],
+            [
+                (devices, 3, cells, slots),
+                (3, own_faces, faces),
+                (wide * (3 if second else 6), slots),
+            ],
             [
                 VMEM((devices * cells * 8, slots), f32),
                 VMEM((own_faces * 8, faces), f32),
                 VMEM((devices, 3, cells, slots), f32),
+                SMEM((own_faces,), jnp.int32),
+                SMEM((own_faces,), jnp.int32),
+                pltpu.SemaphoreType.DMA((2,)),
             ],
             4 * 10**9,
         )
@@ -533,24 +572,29 @@
             functools.partial(outer_kernel, ct, cc, crosses, nrefs, second),
             "outer",
             [],
-            [own, v] + everyone + [beyond] + extra + halo_extra,
+            [own, v, rights] + everyone + [beyond] + extra + halo_extra,
             [block],
             ring_slots,
             10**9,
         )[0]
-        returned, outer = lax.optimization_barrier((exchange(sum_track(parts)), outer))
+        returned, outer = lax.optimization_barrier(
+            (exchange(part, ("track", "cross")), outer)
+        )
         new = call(
             functools.partial(update_kernel, second),
             "update",
             [],
-            [live, x, v, inner, outer, returned],
-            [block, block] if second else [block, block, block, (crosses, 3, cells, slots)],
+            [live, x, v, inner, outer, returned] + ([reaction] if second else []),
+            [block, block]
+            + ([(3, own_faces, faces)] if second else [block, (devices, 3, cells, slots)]),
             [],
             10**6,
             not second,
         )
         x, v = new[:2]
-        if not second:
+        if second:
+            reaction = new[2]
+        else:
             own, spread = new[2:]
     shape = particle_offset.shape
     return (x.reshape(shape), v.reshape(shape), jnp.transpose(reaction, (1, 0, 2)))

time: 70.7 us -> 65.9 us (0.932)
  local copies, waits for them, and re-layouts: 3.47 us -> 0.02 us
  other arithmetic: 1.29 us -> 0 us
  Pallas kernels: 23.8 us -> 24.6 us
    unnamed x19 -> x8, local copies, waits for them, and re-layouts: 3.47 us -> 0.02 us
    all_to_all x4, starting transfers between devices: 17.5 us -> 19.8 us  [exchange(): return lax.all_to_all(a, axes, split_axis=0, concat_axis=0, tiled=True)]
    ppermute x2 -> x0, waiting for transfers between devices: 1.89 us -> none  [sum_track(): return parts[0] + lax.ppermute(parts[1], 'track', swap)]
    all_to_all x4, waiting for transfers between devices: 3.2 us -> 4.66 us  [exchange(): return lax.all_to_all(a, axes, split_axis=0, concat_axis=0, tiled=True)]
    add x2 -> x0, other arithmetic: 1.29 us -> none  [sum_track(): return parts[0] + lax.ppermute(parts[1], 'track', swap)]
    ppermute x2, waiting for transfers between devices: 3.99 us -> 5.23 us  [body(): across = lax.ppermute(packed, ('vehicle', 'track'), travel)]
    ppermute x2, starting transfers between devices: 8 us -> 6.91 us  [body(): across = lax.ppermute(packed, ('vehicle', 'track'), travel)]
    ppermute x2 -> x1, waiting for transfers between devices: 2.01 us -> 1.07 us  [gather_track(): return [a, lax.ppermute(a, 'track', swap)]]
  transfers between devices with their start and end apart: 10 -> 7, of which waited for: 8 -> 5; matrix products, arithmetic and copies ran while one was open for 1% -> 0% of each run, Pallas kernels for 18% -> 18%
where the time goes in v4:
time: 65.9 us; the launch traced here: 65.3 us
  starting transfers between devices  28.9 us (44%)
  Pallas kernels  24.6 us (37%)
  waiting for transfers between devices  11 us (17%)
  between operations  0.74 us (1%)
    pallas_call x9, Pallas kernels, call(): pl.pallas_call(kernel, name=name, out_shape=shapes, in_specs=specs, out_s...  24.6 us
    all_to_all x4, starting transfers between devices, exchange(): return lax.all_to_all(a, axes, split_axis=0, concat_axis=0, tiled=True)  19.8 us
    ppermute x2, starting transfers between devices, body(): across = lax.ppermute(packed, ('vehicle', 'track'), travel)  6.91 us
    ppermute x2, waiting for transfers between devices, body(): across = lax.ppermute(packed, ('vehicle', 'track'), travel)  5.23 us
    all_to_all x4, waiting for transfers between devices, exchange(): return lax.all_to_all(a, axes, split_axis=0, concat_axis=0, tiled=True)  4.66 us
    ppermute x1, starting transfers between devices, gather_track(): return [a, lax.ppermute(a, 'track', swap)]  2.2 us
  transfers between devices with their start and end apart: 7, of which 5 were waited for; matrix products, arithmetic and copies ran while one was open for 0% of the time, Pallas kernels for 18%

profile of v4, /device:TPU:11, one launch (start us, length us, event | category | flops | bytes accessed | tf_op | source)
XLA Modules:
  0.0 65.3 jit_solution(8875246502264903435)
XLA Ops:
  0.6 1.5 %first.1 = (f32[3,16,128]{2,1,0:T(8,128)S(1)}, f32[16,128]{1,0:T(8,128)S(1)}, f32[4,6,16,128]{3,2,1,0:T(8,128)}) custom-call(s32[2,8]{1,0:T(2,128)} %count_from.1, f32[3,16,128]{2,1,0:T(8,128)} %bitcast.8, f32[3,16,128]{2,1,0:T(8,128)} %bitcast.10), custom_call_target="tpu_custom_call" | custom-call | flops 1000000 | tf_op jit(solution)/shard_map/first/pallas_call | solution.py:459
  2.1 0.0 copy-start.1
  2.1 4.8 %all-to-all-start = ((f32[4,6,16,128]{3,2,1,0:T(8,128)}), f32[4,6,16,128]{3,2,1,0:T(8,128)S(1)}, u32[]{:S(2)}, u32[]{:S(2)}) async-start(f32[4,6,16,128]{3,2,1,0:T(8,128)} %get-tuple-element.32), calls=%async_computation | async-start | bytes 393216 | tf_op jit(solution)/shard_map/all_to_all | solution.py:503
  6.9 3.1 %inner.2 = (f32[3,16,128]{2,1,0:T(8,128)S(1)}, bf16[16,80,256]{2,1,0:T(8,128)(2,1)S(1)}) custom-call(f32[3,16,128]{2,1,0:T(8,128)S(1)} %get-tuple-element.33.x_ref, f32[3,16,128]{2,1,0:T(8,128)S(1)} %bitcast.11), custom_call_target="tpu_custom_call" | custom-call | flops 1000000000 | tf_op jit(solution)/shard_map/inner/pallas_call | solution.py:459
  10.0 1.9 %all-to-all-done.rest_0_ = f32[4,6,16,128]{3,2,1,0:T(8,128)S(1)} async-done(((f32[4,6,16,128]{3,2,1,0:T(8,128)}), f32[4,6,16,128]{3,2,1,0:T(8,128)S(1)}, u32[]{:S(2)}, u32[]{:S(2)}) %all-to-all-start) | async-done | bytes 196640 | tf_op jit(solution)/shard_map/all_to_all | solution.py:503
  11.9 2.2 %collective-permute-start = (f32[4,6,16,128]{3,2,1,0:T(8,128)S(1)}, f32[4,6,16,128]{3,2,1,0:T(8,128)S(1)}, u32[]{:S(2)}, u32[]{:S(2)}) collective-permute-start(f32[4,6,16,128]{3,2,1,0:T(8,128)S(1)} %all-to-all-done.rest_0_), channel_id=1, source_target_pairs={{0,4},{4,0},{1,5},{5,1},{2,6},{6,2},{3,7},{7,3},{8,12},{12,8},{9,1... | collective-permute-start | bytes 589832 | tf_op jit(solution)/shard_map/ppermute | solution.py:507
  14.1 1.1 %collective-permute-done.rest_1_ = f32[4,6,16,128]{3,2,1,0:T(8,128)S(1)} collective-permute-done((f32[4,6,16,128]{3,2,1,0:T(8,128)S(1)}, f32[4,6,16,128]{3,2,1,0:T(8,128)S(1)}, u32[]{:S(2)}, u32[]{:S(2)}) %collective-permute-start) | collective-permute-done | bytes 196640 | tf_op jit(solution)/shard_map/ppermute | solution.py:507
  15.1 5.2 %faces.2 = (f32[8,3,16,128]{3,2,1,0:T(8,128)}, f32[3,64,128]{2,1,0:T(8,128)S(1)}, f32[60,128]{1,0:T(8,128)S(1)}) custom-call(s32[64]{0:T(128)} %bitcast.21, s32[64]{0:T(128)} %cell_from.3, f32[3,64,128]{2,1,0:T(8,128)S(1)} %bitcast.14, f32[3,64,128]{2,1,0:T(8,128)S(1)} %bitcast.16, f32[4,6,16,128]{3,2,1,0:T(8,128)S(1)} %all-to-all-done.rest_0_, ...), custom_call_target="tpu_custom_call" | custom-call | flops 4000000000 | tf_op jit(solution)/shard_map/faces/pallas_call | solution.py:459
  20.3 4.9 %all-to-all-start.1 = ((f32[8,3,16,128]{3,2,1,0:T(8,128)}), f32[8,3,16,128]{3,2,1,0:T(8,128)S(1)}, u32[]{:S(2)}, u32[]{:S(2)}) async-start(f32[8,3,16,128]{3,2,1,0:T(8,128)} %get-tuple-element.37), calls=%async_computation.1 | async-start | bytes 393216 | tf_op jit(solution)/shard_map/all_to_all | solution.py:503
  25.2 3.4 %collective-permute-start.1 = (f32[60,128]{1,0:T(8,128)S(1)}, f32[60,128]{1,0:T(8,128)S(1)}, u32[]{:S(2)}, u32[]{:S(2)}) collective-permute-start(f32[60,128]{1,0:T(8,128)S(1)} %get-tuple-element.39), channel_id=1, source_target_pairs={{4,8},{8,4},{12,16},{16,12},{20,24},{24,20},{5,9},{9,5},{13,17},{1... | collective-permute-start | bytes 92168 | tf_op jit(solution)/shard_map/ppermute | solution.py:566
  28.6 2.8 %collective-permute-done.1.rest_2_ = f32[60,128]{1,0:T(8,128)S(1)} collective-permute-done((f32[60,128]{1,0:T(8,128)S(1)}, f32[60,128]{1,0:T(8,128)S(1)}, u32[]{:S(2)}, u32[]{:S(2)}) %collective-permute-start.1) | collective-permute-done | bytes 30752 | tf_op jit(solution)/shard_map/ppermute | solution.py:566
  31.4 2.6 %outer.2.outer_ref = f32[3,16,128]{2,1,0:T(8,128)S(1)} custom-call(f32[3,16,128]{2,1,0:T(8,128)S(1)} %get-tuple-element.33.x_ref, f32[3,16,128]{2,1,0:T(8,128)S(1)} %bitcast.12, bf16[16,80,256]{2,1,0:T(8,128)(2,1)S(1)} %get-tuple-element.38.right_ref, f32[4,6,16,128]{3,2,1,0:T(8,128)S(1)} %all-to-all-done.rest_0_, ...), custom_call_target="tpu_custom_call" | custom-call | flops 1000000000 | tf_op jit(solution)/shard_map/outer/pallas_call | solution.py:459
  34.0 0.0 all-to-all-done.1.back_ref
  34.1 0.7 %update.2 = (f32[3,16,128]{2,1,0:T(8,128)S(1)}, f32[3,16,128]{2,1,0:T(8,128)S(1)}, f32[3,16,128]{2,1,0:T(8,128)S(1)}, f32[8,3,16,128]{3,2,1,0:T(8,128)}) custom-call(f32[16,128]{1,0:T(8,128)S(1)} %get-tuple-element.31.live_ref, f32[3,16,128]{2,1,0:T(8,128)S(1)} %bitcast.9, f32[3,16,128]{2,1,0:T(8,128)S(1)} %bitcast.13, ...), custom_call_target="tpu_custom_call" | custom-call | flops 1000000 | tf_op jit(solution)/shard_map/update/pallas_call | solution.py:459
  34.8 4.8 %all-to-all-start.2 = ((f32[8,3,16,128]{3,2,1,0:T(8,128)}), f32[8,3,16,128]{3,2,1,0:T(8,128)S(1)}, u32[]{:S(2)}, u32[]{:S(2)}) async-start(f32[8,3,16,128]{3,2,1,0:T(8,128)} %get-tuple-element.44), calls=%async_computation.2 | async-start | bytes 393216 | tf_op jit(solution)/shard_map/all_to_all | solution.py:503
  39.6 3.1 %inner.3 = (f32[3,16,128]{2,1,0:T(8,128)S(1)}, bf16[16,80,256]{2,1,0:T(8,128)(2,1)S(1)}) custom-call(f32[3,16,128]{2,1,0:T(8,128)S(1)} %get-tuple-element.45.x_ref, f32[3,16,128]{2,1,0:T(8,128)S(1)} %get-tuple-element.43.v_ref), custom_call_target="tpu_custom_call" | custom-call | flops 1000000000 | tf_op jit(solution)/shard_map/inner/pallas_call | solution.py:459
  42.7 2.8 %all-to-all-done.2.rest_2_.rest_3_ = f32[8,3,16,128]{3,2,1,0:T(8,128)S(1)} async-done(((f32[8,3,16,128]{3,2,1,0:T(8,128)}), f32[8,3,16,128]{3,2,1,0:T(8,128)S(1)}, u32[]{:S(2)}, u32[]{:S(2)}) %all-to-all-start.2) | async-done | bytes 196640 | tf_op jit(solution)/shard_map/all_to_all | solution.py:503
  45.4 5.2 %faces.3 = (f32[8,3,16,128]{3,2,1,0:T(8,128)}, f32[3,64,128]{2,1,0:T(8,128)S(1)}, f32[30,128]{1,0:T(8,128)S(1)}) custom-call(s32[64]{0:T(128)} %bitcast.22, s32[64]{0:T(128)} %cell_from.3, f32[3,64,128]{2,1,0:T(8,128)S(1)} %bitcast.15, f32[3,64,128]{2,1,0:T(8,128)S(1)} %bitcast.17, f32[4,6,16,128]{3,2,1,0:T(8,128)S(1)} %all-to-all-done.rest_0_, ...), custom_call_target="tpu_custom_call" | custom-call | flops 4000000000 | tf_op jit(solution)/shard_map/faces/pallas_call | solution.py:459
  50.6 5.3 %all-to-all-start.3 = ((f32[8,3,16,128]{3,2,1,0:T(8,128)}), f32[8,3,16,128]{3,2,1,0:T(8,128)S(1)}, u32[]{:S(2)}, u32[]{:S(2)}) async-start(f32[8,3,16,128]{3,2,1,0:T(8,128)} %get-tuple-element.50), calls=%async_computation.3 | async-start | bytes 393216 | tf_op jit(solution)/shard_map/all_to_all | solution.py:503
  56.0 3.5 %collective-permute-start.2 = (f32[30,128]{1,0:T(8,128)S(1)}, f32[30,128]{1,0:T(8,128)S(1)}, u32[]{:S(2)}, u32[]{:S(2)}) collective-permute-start(f32[30,128]{1,0:T(8,128)S(1)} %get-tuple-element.52), channel_id=1, source_target_pairs={{4,8},{8,4},{12,16},{16,12},{20,24},{24,20},{5,9},{9,5},{13,17},{1... | collective-permute-start | bytes 46088 | tf_op jit(solution)/shard_map/ppermute | solution.py:566
  59.5 2.4 %collective-permute-done.2.rest_4_ = f32[30,128]{1,0:T(8,128)S(1)} collective-permute-done((f32[30,128]{1,0:T(8,128)S(1)}, f32[30,128]{1,0:T(8,128)S(1)}, u32[]{:S(2)}, u32[]{:S(2)}) %collective-permute-start.2) | collective-permute-done | bytes 15392 | tf_op jit(solution)/shard_map/ppermute | solution.py:566
  61.9 2.6 %outer.3.outer_ref = f32[3,16,128]{2,1,0:T(8,128)S(1)} custom-call(f32[3,16,128]{2,1,0:T(8,128)S(1)} %get-tuple-element.45.x_ref, f32[3,16,128]{2,1,0:T(8,128)S(1)} %get-tuple-element.43.v_ref, bf16[16,80,256]{2,1,0:T(8,128)(2,1)S(1)} %get-tuple-element.51.right_ref, f32[4,6,16,128]{3,2,1,0:T(8,128)S(1)} %all-to-all-done.rest_0_, ...), custom_call_target="tpu_custom_call" | custom-call | flops 1000000000 | tf_op jit(solution)/shard_map/outer/pallas_call | solution.py:459
  64.6 0.0 all-to-all-done.3.back_ref
  64.6 0.7 %update.3 = (f32[3,16,128]{2,1,0:T(8,128)}, f32[3,16,128]{2,1,0:T(8,128)}, f32[3,64,128]{2,1,0:T(8,128)}) custom-call(f32[16,128]{1,0:T(8,128)S(1)} %get-tuple-element.31.live_ref, f32[3,16,128]{2,1,0:T(8,128)S(1)} %get-tuple-element.42.x_ref, f32[3,16,128]{2,1,0:T(8,128)S(1)} %get-tuple-element.43.v_ref, f32[3,16,128]{2,1,0:T(8,128)S(1)} %get-tuple-element.47.inner_ref, ...), custom_call_target="tpu_custom_call" | custom-call | flops 1000000 | tf_op jit(solution)/shard_map/update/pallas_call | solution.py:459
  (7 shorter events, 0.0 us)
Async XLA Ops:
  2.1 4.8 %copy-start.1 = (f32[3,2,8,128]{3,2,1,0:T(8,128)S(1)}, f32[3,2,8,128]{3,2,1,0:T(8,128)}, u32[]{:S(2)}) copy-start(f32[3,2,8,128]{3,2,1,0:T(8,128)} %param.8) | copy-start | bytes 73732
  2.1 9.8 %all-to-all-start = ((f32[4,6,16,128]{3,2,1,0:T(8,128)}), f32[4,6,16,128]{3,2,1,0:T(8,128)S(1)}, u32[]{:S(2)}, u32[]{:S(2)}) async-start(f32[4,6,16,128]{3,2,1,0:T(8,128)} %get-tuple-element.32), calls=%async_computation | async-start | bytes 393216 | tf_op jit(solution)/shard_map/all_to_all | solution.py:503
  6.9 8.3 %copy-start.2 = (f32[64,3,128]{2,0,1:T(8,128)S(1)}, f32[64,3,128]{2,0,1:T(8,128)}, u32[]{:S(2)}) copy-start(f32[64,3,128]{2,0,1:T(8,128)} %param.10) | copy-start | bytes 294916
  6.9 8.3 %copy-start.3 = (f32[64,3,128]{2,0,1:T(8,128)S(1)}, f32[64,3,128]{2,0,1:T(8,128)}, u32[]{:S(2)}) copy-start(f32[64,3,128]{2,0,1:T(8,128)} %param.11) | copy-start | bytes 294916
  11.9 3.3 %collective-permute-start = (f32[4,6,16,128]{3,2,1,0:T(8,128)S(1)}, f32[4,6,16,128]{3,2,1,0:T(8,128)S(1)}, u32[]{:S(2)}, u32[]{:S(2)}) collective-permute-start(f32[4,6,16,128]{3,2,1,0:T(8,128)S(1)} %all-to-all-done.rest_0_), channel_id=1, source_target_pairs={{0,4},{4,0},{1,5},{5,1},{2,6},{6,2},{3,7},{7,3},{8,12},{12,8},{9,1... | collective-permute-start | bytes 589832 | tf_op jit(solution)/shard_map/ppermute | solution.py:507
  20.3 13.7 %all-to-all-start.1 = ((f32[8,3,16,128]{3,2,1,0:T(8,128)}), f32[8,3,16,128]{3,2,1,0:T(8,128)S(1)}, u32[]{:S(2)}, u32[]{:S(2)}) async-start(f32[8,3,16,128]{3,2,1,0:T(8,128)} %get-tuple-element.37), calls=%async_computation.1 | async-start | bytes 393216 | tf_op jit(solution)/shard_map/all_to_all | solution.py:503
  25.2 6.2 %collective-permute-start.1 = (f32[60,128]{1,0:T(8,128)S(1)}, f32[60,128]{1,0:T(8,128)S(1)}, u32[]{:S(2)}, u32[]{:S(2)}) collective-permute-start(f32[60,128]{1,0:T(8,128)S(1)} %get-tuple-element.39), channel_id=1, source_target_pairs={{4,8},{8,4},{12,16},{16,12},{20,24},{24,20},{5,9},{9,5},{13,17},{1... | collective-permute-start | bytes 92168 | tf_op jit(solution)/shard_map/ppermute | solution.py:566
  31.4 2.6 %copy-start = (f32[3,2,8,128]{3,2,1,0:T(8,128)S(1)}, f32[3,2,8,128]{3,2,1,0:T(8,128)}, u32[]{:S(2)}) copy-start(f32[3,2,8,128]{3,2,1,0:T(8,128)} %param.7) | copy-start | bytes 73732
  34.8 10.7 %all-to-all-start.2 = ((f32[8,3,16,128]{3,2,1,0:T(8,128)}), f32[8,3,16,128]{3,2,1,0:T(8,128)S(1)}, u32[]{:S(2)}, u32[]{:S(2)}) async-start(f32[8,3,16,128]{3,2,1,0:T(8,128)} %get-tuple-element.44), calls=%async_computation.2 | async-start | bytes 393216 | tf_op jit(solution)/shard_map/all_to_all | solution.py:503
  50.6 13.9 %all-to-all-start.3 = ((f32[8,3,16,128]{3,2,1,0:T(8,128)}), f32[8,3,16,128]{3,2,1,0:T(8,128)S(1)}, u32[]{:S(2)}, u32[]{:S(2)}) async-start(f32[8,3,16,128]{3,2,1,0:T(8,128)} %get-tuple-element.50), calls=%async_computation.3 | async-start | bytes 393216 | tf_op jit(solution)/shard_map/all_to_all | solution.py:503
  56.0 5.9 %collective-permute-start.2 = (f32[30,128]{1,0:T(8,128)S(1)}, f32[30,128]{1,0:T(8,128)S(1)}, u32[]{:S(2)}, u32[]{:S(2)}) collective-permute-start(f32[30,128]{1,0:T(8,128)S(1)} %get-tuple-element.52), channel_id=1, source_target_pairs={{4,8},{8,4},{12,16},{16,12},{20,24},{24,20},{5,9},{9,5},{13,17},{1... | collective-permute-start | bytes 46088 | tf_op jit(solution)/shard_map/ppermute | solution.py:566

commit v5 on v4

--- a/solution.py
+++ b/solution.py
@@ -18,7 +18,8 @@
 far = 1000.0
 ahead = 8
 columns = 4
-faces_at_once = 16
+faces_at_once = 64
+early, late = 2, 4
 scratch_bytes = 20 * 2**20
 f32 = jnp.float32
 bf16 = jnp.bfloat16
@@ -286,7 +287,9 @@
     finish(jobs, places, True)
 
 
-def face_kernel(second, ct, cc, crosses, nrefs, route_from, cell_from, offset_ref, velocity_ref, *rest):
+def face_kernel(
+    second, ct, cc, crosses, nrefs, route_from, cell_from, offset_ref, velocity_ref, *rest
+):
     all_refs, rest = rest[:nrefs], rest[nrefs:]
     if second:
         force_ref, before_ref, *rest = rest
@@ -301,7 +304,6 @@
     count = offset_ref.shape[1]
     track = lax.axis_index("track")
     pack(ct, cc, crosses, track, [force_ref] if second else all_refs, halo_ref)
-
     starts = [jnp.bitwise_xor(k, track) * devices if nrefs == 2 else 0 for k in range(nrefs)]
     for k in range(nrefs):
 
@@ -323,7 +325,6 @@
             y = y + time_step * w
         face_ref[pl.ds(axis, count, stride=8), :] = y
         face_ref[pl.ds(3 + axis, count, stride=8), :] = w
-
     for copy in copies:
         copy.wait()
 
@@ -334,49 +335,48 @@
             where = jnp.bitwise_xor(where, track)
         return where * crosses + across, cell_ref[f]
 
-    group = next(n for n in (faces_at_once, 4, 2, 1) if count % n == 0)
+    group = next(n for n in (faces_at_once, 16, 4, 2, 1) if count % n == 0)
 
     def several(g, carry):
-        blocks, states, faces, rights, lefts, sums, back_sums = [], [], [], [], [], [], []
-        for k in range(group):
-            f = g * group + k
-            block = block_of(f)
-            place = (block[0] * cells + block[1]) * 8
-            state = state_ref[pl.ds(pl.multiple_of(place, 8), 8), :]
-            face = face_ref[pl.ds(pl.multiple_of(f * 8, 8), 8), :]
-            pieces, row = features(state, soften * soften)
-            face_pieces, _ = features(face, 0.0)
-            blocks.append(block)
-            states.append(state)
-            faces.append(face)
-            lefts.append(left_side(face_pieces, row))
-            rights.append(right_side(pieces, row))
-            sums.append(sum_side(face_pieces))
-            back_sums.append(sum_side(pieces))
-        waiting, done = [], []
-        for n in range(group + ahead):
-            if n < group:
-                waiting.append(dot(lefts[n], rights[n]))
-            if n >= ahead and n - ahead < group:
-                k = n - ahead
-                high, low = pair_weights(waiting[k], radius + face_radius)
-                done.append(
-                    (
-                        dot(sums[k], jnp.concatenate([high, low], axis=0)),
-                        dot(back_sums[k], jnp.concatenate([high, low], axis=1), ((1,), (1,))),
-                    )
+        blocks, states, rights, back_sums, products, done = {}, {}, {}, {}, {}, {}
+        faces, lefts, sums = {}, {}, {}
+        for n in range(group + early + ahead + late):
+            k = n
+            if k < group:
+                blocks[k] = block_of(g * group + k)
+                place = (blocks[k][0] * cells + blocks[k][1]) * 8
+                states[k] = state_ref[pl.ds(pl.multiple_of(place, 8), 8), :]
+                pieces, row = features(states[k], soften * soften)
+                rights[k], back_sums[k] = right_side(pieces, row), sum_side(pieces)
+                faces[k] = face_ref[pl.ds(pl.multiple_of((g * group + k) * 8, 8), 8), :]
+                pieces, _ = features(faces[k], 0.0)
+                lefts[k], sums[k] = left_side(pieces, row), sum_side(pieces)
+            k = n - early
+            if 0 <= k < group:
+                products[k] = dot(lefts.pop(k), rights.pop(k))
+            k = n - early - ahead
+            if 0 <= k < group:
+                high, low = pair_weights(products.pop(k), radius + face_radius)
+                done[k] = (
+                    dot(sums.pop(k), jnp.concatenate([high, low], axis=0)),
+                    dot(
+                        back_sums.pop(k), jnp.concatenate([high, low], axis=1), ((1,), (1,))
+                    ),
                 )
-        for k in range(group):
-            onto, back = moment(states[k], done[k][0]), moment(faces[k], done[k][1])
-            device, cell = blocks[k]
-            for axis in range(3):
-                line = time_step * damping * back[axis : axis + 1]
-                at = pl.ds(g * group + k, 1)
-                if second:
-                    line = line + before_ref[axis, at, :]
-                react_ref[axis, at, :] = line
-                line = part_ref[device, axis, pl.ds(cell, 1), :]
-                part_ref[device, axis, pl.ds(cell, 1), :] = line + damping * onto[axis : axis + 1]
+            k = n - early - ahead - late
+            if 0 <= k < group:
+                f = g * group + k
+                onto, back = done.pop(k)
+                onto, back = moment(states.pop(k), onto), moment(faces.pop(k), back)
+                device, cell = blocks[k]
+                for axis in range(3):
+                    line = time_step * damping * back[axis : axis + 1]
+                    if second:
+                        line = line + before_ref[axis, pl.ds(f, 1), :]
+                    react_ref[axis, pl.ds(f, 1), :] = line
+                    line = part_ref[device, axis, pl.ds(cell, 1), :]
+                    line = line + damping * onto[axis : axis + 1]
+                    part_ref[device, axis, pl.ds(cell, 1), :] = line
         return carry
 
     lax.fori_loop(0, count // group, several, 0)

time: 65.9 us -> 64.4 us (0.977)
  Pallas kernels: 24.6 us -> 23.1 us
    pallas_call x9, Pallas kernels: 24.6 us -> 23.1 us  [call(): pl.pallas_call(kernel, name=name, out_shape=shapes, in_specs=specs, out_s...]
where the time goes in v5:
time: 64.4 us; the launch traced here: 63.8 us
  starting transfers between devices  28.9 us (45%)
  Pallas kernels  23.1 us (36%)
  waiting for transfers between devices  11 us (17%)
  between operations  0.74 us (1%)
    pallas_call x9, Pallas kernels, call(): pl.pallas_call(kernel, name=name, out_shape=shapes, in_specs=specs, out_s...  23.1 us
    all_to_all x4, starting transfers between devices, exchange(): return lax.all_to_all(a, axes, split_axis=0, concat_axis=0, tiled=True)  19.8 us
    ppermute x2, starting transfers between devices, body(): across = lax.ppermute(packed, ('vehicle', 'track'), travel)  6.91 us
    ppermute x2, waiting for transfers between devices, body(): across = lax.ppermute(packed, ('vehicle', 'track'), travel)  5.22 us
    all_to_all x4, waiting for transfers between devices, exchange(): return lax.all_to_all(a, axes, split_axis=0, concat_axis=0, tiled=True)  4.66 us
    ppermute x1, starting transfers between devices, gather_track(): return [a, lax.ppermute(a, 'track', swap)]  2.2 us
  transfers between devices with their start and end apart: 7, of which 5 were waited for; matrix products, arithmetic and copies ran while one was open for 0% of the time, Pallas kernels for 18%

profile of v5, /device:TPU:11, one launch (start us, length us, event | category | flops | bytes accessed | tf_op | source)
XLA Modules:
  0.0 63.8 jit_solution(633676759472458429)
XLA Ops:
  0.6 1.5 %first.1 = (f32[3,16,128]{2,1,0:T(8,128)S(1)}, f32[16,128]{1,0:T(8,128)S(1)}, f32[4,6,16,128]{3,2,1,0:T(8,128)}) custom-call(s32[2,8]{1,0:T(2,128)} %count_from.1, f32[3,16,128]{2,1,0:T(8,128)} %bitcast.8, f32[3,16,128]{2,1,0:T(8,128)} %bitcast.10), custom_call_target="tpu_custom_call" | custom-call | flops 1000000 | tf_op jit(solution)/shard_map/first/pallas_call | solution.py:459
  2.1 0.0 copy-start.1
  2.1 4.8 %all-to-all-start = ((f32[4,6,16,128]{3,2,1,0:T(8,128)}), f32[4,6,16,128]{3,2,1,0:T(8,128)S(1)}, u32[]{:S(2)}, u32[]{:S(2)}) async-start(f32[4,6,16,128]{3,2,1,0:T(8,128)} %get-tuple-element.32), calls=%async_computation | async-start | bytes 393216 | tf_op jit(solution)/shard_map/all_to_all | solution.py:503
  6.9 3.1 %inner.2 = (f32[3,16,128]{2,1,0:T(8,128)S(1)}, bf16[16,80,256]{2,1,0:T(8,128)(2,1)S(1)}) custom-call(f32[3,16,128]{2,1,0:T(8,128)S(1)} %get-tuple-element.33.x_ref, f32[3,16,128]{2,1,0:T(8,128)S(1)} %bitcast.11), custom_call_target="tpu_custom_call" | custom-call | flops 1000000000 | tf_op jit(solution)/shard_map/inner/pallas_call | solution.py:459
  10.0 1.9 %all-to-all-done.rest_0_ = f32[4,6,16,128]{3,2,1,0:T(8,128)S(1)} async-done(((f32[4,6,16,128]{3,2,1,0:T(8,128)}), f32[4,6,16,128]{3,2,1,0:T(8,128)S(1)}, u32[]{:S(2)}, u32[]{:S(2)}) %all-to-all-start) | async-done | bytes 196640 | tf_op jit(solution)/shard_map/all_to_all | solution.py:503
  11.9 2.2 %collective-permute-start = (f32[4,6,16,128]{3,2,1,0:T(8,128)S(1)}, f32[4,6,16,128]{3,2,1,0:T(8,128)S(1)}, u32[]{:S(2)}, u32[]{:S(2)}) collective-permute-start(f32[4,6,16,128]{3,2,1,0:T(8,128)S(1)} %all-to-all-done.rest_0_), channel_id=1, source_target_pairs={{0,4},{4,0},{1,5},{5,1},{2,6},{6,2},{3,7},{7,3},{8,12},{12,8},{9,1... | collective-permute-start | bytes 589832 | tf_op jit(solution)/shard_map/ppermute | solution.py:507
  14.1 1.1 %collective-permute-done.rest_1_ = f32[4,6,16,128]{3,2,1,0:T(8,128)S(1)} collective-permute-done((f32[4,6,16,128]{3,2,1,0:T(8,128)S(1)}, f32[4,6,16,128]{3,2,1,0:T(8,128)S(1)}, u32[]{:S(2)}, u32[]{:S(2)}) %collective-permute-start) | collective-permute-done | bytes 196640 | tf_op jit(solution)/shard_map/ppermute | solution.py:507
  15.1 4.3 %faces.2 = (f32[8,3,16,128]{3,2,1,0:T(8,128)}, f32[3,64,128]{2,1,0:T(8,128)S(1)}, f32[60,128]{1,0:T(8,128)S(1)}) custom-call(s32[64]{0:T(128)} %bitcast.21, s32[64]{0:T(128)} %cell_from.3, f32[3,64,128]{2,1,0:T(8,128)S(1)} %bitcast.14, f32[3,64,128]{2,1,0:T(8,128)S(1)} %bitcast.16, f32[4,6,16,128]{3,2,1,0:T(8,128)S(1)} %all-to-all-done.rest_0_, ...), custom_call_target="tpu_custom_call" | custom-call | flops 4000000000 | tf_op jit(solution)/shard_map/faces/pallas_call | solution.py:459
  19.5 4.9 %all-to-all-start.1 = ((f32[8,3,16,128]{3,2,1,0:T(8,128)}), f32[8,3,16,128]{3,2,1,0:T(8,128)S(1)}, u32[]{:S(2)}, u32[]{:S(2)}) async-start(f32[8,3,16,128]{3,2,1,0:T(8,128)} %get-tuple-element.37), calls=%async_computation.1 | async-start | bytes 393216 | tf_op jit(solution)/shard_map/all_to_all | solution.py:503
  24.4 3.4 %collective-permute-start.1 = (f32[60,128]{1,0:T(8,128)S(1)}, f32[60,128]{1,0:T(8,128)S(1)}, u32[]{:S(2)}, u32[]{:S(2)}) collective-permute-start(f32[60,128]{1,0:T(8,128)S(1)} %get-tuple-element.39), channel_id=1, source_target_pairs={{4,8},{8,4},{12,16},{16,12},{20,24},{24,20},{5,9},{9,5},{13,17},{1... | collective-permute-start | bytes 92168 | tf_op jit(solution)/shard_map/ppermute | solution.py:566
  27.7 2.8 %collective-permute-done.1.rest_2_ = f32[60,128]{1,0:T(8,128)S(1)} collective-permute-done((f32[60,128]{1,0:T(8,128)S(1)}, f32[60,128]{1,0:T(8,128)S(1)}, u32[]{:S(2)}, u32[]{:S(2)}) %collective-permute-start.1) | collective-permute-done | bytes 30752 | tf_op jit(solution)/shard_map/ppermute | solution.py:566
  30.6 2.6 %outer.2.outer_ref = f32[3,16,128]{2,1,0:T(8,128)S(1)} custom-call(f32[3,16,128]{2,1,0:T(8,128)S(1)} %get-tuple-element.33.x_ref, f32[3,16,128]{2,1,0:T(8,128)S(1)} %bitcast.12, bf16[16,80,256]{2,1,0:T(8,128)(2,1)S(1)} %get-tuple-element.38.right_ref, f32[4,6,16,128]{3,2,1,0:T(8,128)S(1)} %all-to-all-done.rest_0_, ...), custom_call_target="tpu_custom_call" | custom-call | flops 1000000000 | tf_op jit(solution)/shard_map/outer/pallas_call | solution.py:459
  33.2 0.0 all-to-all-done.1.back_ref
  33.2 0.7 %update.2 = (f32[3,16,128]{2,1,0:T(8,128)S(1)}, f32[3,16,128]{2,1,0:T(8,128)S(1)}, f32[3,16,128]{2,1,0:T(8,128)S(1)}, f32[8,3,16,128]{3,2,1,0:T(8,128)}) custom-call(f32[16,128]{1,0:T(8,128)S(1)} %get-tuple-element.31.live_ref, f32[3,16,128]{2,1,0:T(8,128)S(1)} %bitcast.9, f32[3,16,128]{2,1,0:T(8,128)S(1)} %bitcast.13, ...), custom_call_target="tpu_custom_call" | custom-call | flops 1000000 | tf_op jit(solution)/shard_map/update/pallas_call | solution.py:459
  33.9 4.8 %all-to-all-start.2 = ((f32[8,3,16,128]{3,2,1,0:T(8,128)}), f32[8,3,16,128]{3,2,1,0:T(8,128)S(1)}, u32[]{:S(2)}, u32[]{:S(2)}) async-start(f32[8,3,16,128]{3,2,1,0:T(8,128)} %get-tuple-element.44), calls=%async_computation.2 | async-start | bytes 393216 | tf_op jit(solution)/shard_map/all_to_all | solution.py:503
  38.7 3.1 %inner.3 = (f32[3,16,128]{2,1,0:T(8,128)S(1)}, bf16[16,80,256]{2,1,0:T(8,128)(2,1)S(1)}) custom-call(f32[3,16,128]{2,1,0:T(8,128)S(1)} %get-tuple-element.45.x_ref, f32[3,16,128]{2,1,0:T(8,128)S(1)} %get-tuple-element.43.v_ref), custom_call_target="tpu_custom_call" | custom-call | flops 1000000000 | tf_op jit(solution)/shard_map/inner/pallas_call | solution.py:459
  41.8 2.8 %all-to-all-done.2.rest_2_.rest_3_ = f32[8,3,16,128]{3,2,1,0:T(8,128)S(1)} async-done(((f32[8,3,16,128]{3,2,1,0:T(8,128)}), f32[8,3,16,128]{3,2,1,0:T(8,128)S(1)}, u32[]{:S(2)}, u32[]{:S(2)}) %all-to-all-start.2) | async-done | bytes 196640 | tf_op jit(solution)/shard_map/all_to_all | solution.py:503
  44.6 4.5 %faces.3 = (f32[8,3,16,128]{3,2,1,0:T(8,128)}, f32[3,64,128]{2,1,0:T(8,128)S(1)}, f32[30,128]{1,0:T(8,128)S(1)}) custom-call(s32[64]{0:T(128)} %bitcast.22, s32[64]{0:T(128)} %cell_from.3, f32[3,64,128]{2,1,0:T(8,128)S(1)} %bitcast.15, f32[3,64,128]{2,1,0:T(8,128)S(1)} %bitcast.17, f32[4,6,16,128]{3,2,1,0:T(8,128)S(1)} %all-to-all-done.rest_0_, ...), custom_call_target="tpu_custom_call" | custom-call | flops 4000000000 | tf_op jit(solution)/shard_map/faces/pallas_call | solution.py:459
  49.1 5.4 %all-to-all-start.3 = ((f32[8,3,16,128]{3,2,1,0:T(8,128)}), f32[8,3,16,128]{3,2,1,0:T(8,128)S(1)}, u32[]{:S(2)}, u32[]{:S(2)}) async-start(f32[8,3,16,128]{3,2,1,0:T(8,128)} %get-tuple-element.50), calls=%async_computation.3 | async-start | bytes 393216 | tf_op jit(solution)/shard_map/all_to_all | solution.py:503
  54.5 3.5 %collective-permute-start.2 = (f32[30,128]{1,0:T(8,128)S(1)}, f32[30,128]{1,0:T(8,128)S(1)}, u32[]{:S(2)}, u32[]{:S(2)}) collective-permute-start(f32[30,128]{1,0:T(8,128)S(1)} %get-tuple-element.52), channel_id=1, source_target_pairs={{4,8},{8,4},{12,16},{16,12},{20,24},{24,20},{5,9},{9,5},{13,17},{1... | collective-permute-start | bytes 46088 | tf_op jit(solution)/shard_map/ppermute | solution.py:566
  58.0 2.4 %collective-permute-done.2.rest_4_ = f32[30,128]{1,0:T(8,128)S(1)} collective-permute-done((f32[30,128]{1,0:T(8,128)S(1)}, f32[30,128]{1,0:T(8,128)S(1)}, u32[]{:S(2)}, u32[]{:S(2)}) %collective-permute-start.2) | collective-permute-done | bytes 15392 | tf_op jit(solution)/shard_map/ppermute | solution.py:566
  60.4 2.6 %outer.3.outer_ref = f32[3,16,128]{2,1,0:T(8,128)S(1)} custom-call(f32[3,16,128]{2,1,0:T(8,128)S(1)} %get-tuple-element.45.x_ref, f32[3,16,128]{2,1,0:T(8,128)S(1)} %get-tuple-element.43.v_ref, bf16[16,80,256]{2,1,0:T(8,128)(2,1)S(1)} %get-tuple-element.51.right_ref, f32[4,6,16,128]{3,2,1,0:T(8,128)S(1)} %all-to-all-done.rest_0_, ...), custom_call_target="tpu_custom_call" | custom-call | flops 1000000000 | tf_op jit(solution)/shard_map/outer/pallas_call | solution.py:459
  63.1 0.0 all-to-all-done.3.back_ref
  63.1 0.7 %update.3 = (f32[3,16,128]{2,1,0:T(8,128)}, f32[3,16,128]{2,1,0:T(8,128)}, f32[3,64,128]{2,1,0:T(8,128)}) custom-call(f32[16,128]{1,0:T(8,128)S(1)} %get-tuple-element.31.live_ref, f32[3,16,128]{2,1,0:T(8,128)S(1)} %get-tuple-element.42.x_ref, f32[3,16,128]{2,1,0:T(8,128)S(1)} %get-tuple-element.43.v_ref, f32[3,16,128]{2,1,0:T(8,128)S(1)} %get-tuple-element.47.inner_ref, ...), custom_call_target="tpu_custom_call" | custom-call | flops 1000000 | tf_op jit(solution)/shard_map/update/pallas_call | solution.py:459
  (7 shorter events, 0.0 us)
Async XLA Ops:
  2.1 4.8 %copy-start.1 = (f32[3,2,8,128]{3,2,1,0:T(8,128)S(1)}, f32[3,2,8,128]{3,2,1,0:T(8,128)}, u32[]{:S(2)}) copy-start(f32[3,2,8,128]{3,2,1,0:T(8,128)} %param.8) | copy-start | bytes 73732
  2.1 9.8 %all-to-all-start = ((f32[4,6,16,128]{3,2,1,0:T(8,128)}), f32[4,6,16,128]{3,2,1,0:T(8,128)S(1)}, u32[]{:S(2)}, u32[]{:S(2)}) async-start(f32[4,6,16,128]{3,2,1,0:T(8,128)} %get-tuple-element.32), calls=%async_computation | async-start | bytes 393216 | tf_op jit(solution)/shard_map/all_to_all | solution.py:503
  6.9 8.3 %copy-start.2 = (f32[64,3,128]{2,0,1:T(8,128)S(1)}, f32[64,3,128]{2,0,1:T(8,128)}, u32[]{:S(2)}) copy-start(f32[64,3,128]{2,0,1:T(8,128)} %param.10) | copy-start | bytes 294916
  6.9 8.3 %copy-start.3 = (f32[64,3,128]{2,0,1:T(8,128)S(1)}, f32[64,3,128]{2,0,1:T(8,128)}, u32[]{:S(2)}) copy-start(f32[64,3,128]{2,0,1:T(8,128)} %param.11) | copy-start | bytes 294916
  11.9 3.3 %collective-permute-start = (f32[4,6,16,128]{3,2,1,0:T(8,128)S(1)}, f32[4,6,16,128]{3,2,1,0:T(8,128)S(1)}, u32[]{:S(2)}, u32[]{:S(2)}) collective-permute-start(f32[4,6,16,128]{3,2,1,0:T(8,128)S(1)} %all-to-all-done.rest_0_), channel_id=1, source_target_pairs={{0,4},{4,0},{1,5},{5,1},{2,6},{6,2},{3,7},{7,3},{8,12},{12,8},{9,1... | collective-permute-start | bytes 589832 | tf_op jit(solution)/shard_map/ppermute | solution.py:507
  19.5 13.7 %all-to-all-start.1 = ((f32[8,3,16,128]{3,2,1,0:T(8,128)}), f32[8,3,16,128]{3,2,1,0:T(8,128)S(1)}, u32[]{:S(2)}, u32[]{:S(2)}) async-start(f32[8,3,16,128]{3,2,1,0:T(8,128)} %get-tuple-element.37), calls=%async_computation.1 | async-start | bytes 393216 | tf_op jit(solution)/shard_map/all_to_all | solution.py:503
  24.4 6.2 %collective-permute-start.1 = (f32[60,128]{1,0:T(8,128)S(1)}, f32[60,128]{1,0:T(8,128)S(1)}, u32[]{:S(2)}, u32[]{:S(2)}) collective-permute-start(f32[60,128]{1,0:T(8,128)S(1)} %get-tuple-element.39), channel_id=1, source_target_pairs={{4,8},{8,4},{12,16},{16,12},{20,24},{24,20},{5,9},{9,5},{13,17},{1... | collective-permute-start | bytes 92168 | tf_op jit(solution)/shard_map/ppermute | solution.py:566
  30.6 2.6 %copy-start = (f32[3,2,8,128]{3,2,1,0:T(8,128)S(1)}, f32[3,2,8,128]{3,2,1,0:T(8,128)}, u32[]{:S(2)}) copy-start(f32[3,2,8,128]{3,2,1,0:T(8,128)} %param.7) | copy-start | bytes 73732
  33.9 10.7 %all-to-all-start.2 = ((f32[8,3,16,128]{3,2,1,0:T(8,128)}), f32[8,3,16,128]{3,2,1,0:T(8,128)S(1)}, u32[]{:S(2)}, u32[]{:S(2)}) async-start(f32[8,3,16,128]{3,2,1,0:T(8,128)} %get-tuple-element.44), calls=%async_computation.2 | async-start | bytes 393216 | tf_op jit(solution)/shard_map/all_to_all | solution.py:503
  49.1 14.0 %all-to-all-start.3 = ((f32[8,3,16,128]{3,2,1,0:T(8,128)}), f32[8,3,16,128]{3,2,1,0:T(8,128)S(1)}, u32[]{:S(2)}, u32[]{:S(2)}) async-start(f32[8,3,16,128]{3,2,1,0:T(8,128)} %get-tuple-element.50), calls=%async_computation.3 | async-start | bytes 393216 | tf_op jit(solution)/shard_map/all_to_all | solution.py:503
  54.5 5.9 %collective-permute-start.2 = (f32[30,128]{1,0:T(8,128)S(1)}, f32[30,128]{1,0:T(8,128)S(1)}, u32[]{:S(2)}, u32[]{:S(2)}) collective-permute-start(f32[30,128]{1,0:T(8,128)S(1)} %get-tuple-element.52), channel_id=1, source_target_pairs={{4,8},{8,4},{12,16},{16,12},{20,24},{24,20},{5,9},{9,5},{13,17},{1... | collective-permute-start | bytes 46088 | tf_op jit(solution)/shard_map/ppermute | solution.py:566

commit v6 on v5

--- a/solution.py
+++ b/solution.py
@@ -259,32 +259,21 @@
     ring += [(r + 1) * wide + p for r in range(ct) for p in (0, cc + 1)]
     build_left(state_ref, left_ref, sum_ref, ring)
 
-    def finish(jobs, places, add):
-        for sums, (slot, index) in zip(pushes(left_ref, sum_ref, right_ref, jobs), places):
-            start = slot * 8 if isinstance(slot, int) else pl.multiple_of(slot * 8, 8)
-            store_rows(out_ref, moment(state_ref[pl.ds(start, 8), :], sums), index, add)
-
-    if ct != 2:
+    jobs = []
+    for c in range(cc):
+        for r in range(ct):
+            near = range(max(r - 1, 0), min(r + 2, ct))
+            others = [(q + 1) * wide for q in near] if c == 0 else []
+            others += [(q + 1) * wide + cc + 1 for q in near] if c == cc - 1 else []
+            others += [c + d for d in range(3)] if r == 0 else []
+            others += [(ct + 1) * wide + c + d for d in range(3)] if r == ct - 1 else []
+            if others:
+                jobs.append((r * cc + c, others))
+    if ct > 2:
         out_ref[...] = jnp.zeros_like(out_ref)
-
-    def several(step, carry):
-        jobs, places = [], []
-        for k in range(columns):
-            c = step * columns + k
-            for r, rr in ((0, 0), (ct - 1, ct + 1)):
-                jobs.append((r * cc + c, [rr * wide + c + d for d in range(3)]))
-                places.append(((r + 1) * wide + c + 1, r * cc + c))
-        finish(jobs, places, ct != 2)
-        return carry
-
-    lax.fori_loop(0, cc // columns, several, 0)
-    jobs, places = [], []
-    for r in range(ct):
-        near = range(max(r - 1, 0), min(r + 2, ct))
-        for c, p in ((0, 0), (cc - 1, cc + 1)):
-            jobs.append((r * cc + c, [(q + 1) * wide + p for q in near]))
-            places.append(((r + 1) * wide + c + 1, r * cc + c))
-    finish(jobs, places, True)
+    for (index, _), sums in zip(jobs, pushes(left_ref, sum_ref, right_ref, jobs)):
+        start = ((index // cc + 1) * wide + index % cc + 1) * 8
+        store_rows(out_ref, moment(state_ref[pl.ds(start, 8), :], sums), index, False)
 
 
 def face_kernel(

time: 64.4 us -> 63.5 us (0.986)
  Pallas kernels: 23.1 us -> 22.2 us
    pallas_call x9, Pallas kernels: 23.1 us -> 22.2 us  [call(): pl.pallas_call(kernel, name=name, out_shape=shapes, in_specs=specs, out_s...]
  transfers between devices with their start and end apart: 7 -> 7, of which waited for: 5 -> 5; matrix products, arithmetic and copies ran while one was open for 0% -> 0% of each run, Pallas kernels for 18% -> 17%
where the time goes in v6:
time: 63.5 us; the launch traced here: 62.9 us
  starting transfers between devices  28.9 us (46%)
  Pallas kernels  22.2 us (35%)
  waiting for transfers between devices  11 us (17%)
  between operations  0.73 us (1%)
    pallas_call x9, Pallas kernels, call(): pl.pallas_call(kernel, name=name, out_shape=shapes, in_specs=specs, out_s...  22.2 us
    all_to_all x4, starting transfers between devices, exchange(): return lax.all_to_all(a, axes, split_axis=0, concat_axis=0, tiled=True)  19.8 us
    ppermute x2, starting transfers between devices, body(): across = lax.ppermute(packed, ('vehicle', 'track'), travel)  6.9 us
    ppermute x2, waiting for transfers between devices, body(): across = lax.ppermute(packed, ('vehicle', 'track'), travel)  5.23 us
    all_to_all x4, waiting for transfers between devices, exchange(): return lax.all_to_all(a, axes, split_axis=0, concat_axis=0, tiled=True)  4.66 us
    ppermute x1, starting transfers between devices, gather_track(): return [a, lax.ppermute(a, 'track', swap)]  2.2 us
  transfers between devices with their start and end apart: 7, of which 5 were waited for; matrix products, arithmetic and copies ran while one was open for 0% of the time, Pallas kernels for 17%

profile of v6, /device:TPU:11, one launch (start us, length us, event | category | flops | bytes accessed | tf_op | source)
XLA Modules:
  0.0 62.9 jit_solution(7117673039613761480)
XLA Ops:
  0.6 1.5 %first.1 = (f32[3,16,128]{2,1,0:T(8,128)S(1)}, f32[16,128]{1,0:T(8,128)S(1)}, f32[4,6,16,128]{3,2,1,0:T(8,128)}) custom-call(s32[2,8]{1,0:T(2,128)} %count_from.1, f32[3,16,128]{2,1,0:T(8,128)} %bitcast.8, f32[3,16,128]{2,1,0:T(8,128)} %bitcast.10), custom_call_target="tpu_custom_call" | custom-call | flops 1000000 | tf_op jit(solution)/shard_map/first/pallas_call | solution.py:448
  2.1 0.0 copy-start.1
  2.1 4.8 %all-to-all-start = ((f32[4,6,16,128]{3,2,1,0:T(8,128)}), f32[4,6,16,128]{3,2,1,0:T(8,128)S(1)}, u32[]{:S(2)}, u32[]{:S(2)}) async-start(f32[4,6,16,128]{3,2,1,0:T(8,128)} %get-tuple-element.32), calls=%async_computation | async-start | bytes 393216 | tf_op jit(solution)/shard_map/all_to_all | solution.py:492
  6.9 3.1 %inner.2 = (f32[3,16,128]{2,1,0:T(8,128)S(1)}, bf16[16,80,256]{2,1,0:T(8,128)(2,1)S(1)}) custom-call(f32[3,16,128]{2,1,0:T(8,128)S(1)} %get-tuple-element.33.x_ref, f32[3,16,128]{2,1,0:T(8,128)S(1)} %bitcast.11), custom_call_target="tpu_custom_call" | custom-call | flops 1000000000 | tf_op jit(solution)/shard_map/inner/pallas_call | solution.py:448
  10.0 1.9 %all-to-all-done.rest_0_ = f32[4,6,16,128]{3,2,1,0:T(8,128)S(1)} async-done(((f32[4,6,16,128]{3,2,1,0:T(8,128)}), f32[4,6,16,128]{3,2,1,0:T(8,128)S(1)}, u32[]{:S(2)}, u32[]{:S(2)}) %all-to-all-start) | async-done | bytes 196640 | tf_op jit(solution)/shard_map/all_to_all | solution.py:492
  11.9 2.2 %collective-permute-start = (f32[4,6,16,128]{3,2,1,0:T(8,128)S(1)}, f32[4,6,16,128]{3,2,1,0:T(8,128)S(1)}, u32[]{:S(2)}, u32[]{:S(2)}) collective-permute-start(f32[4,6,16,128]{3,2,1,0:T(8,128)S(1)} %all-to-all-done.rest_0_), channel_id=1, source_target_pairs={{0,4},{4,0},{1,5},{5,1},{2,6},{6,2},{3,7},{7,3},{8,12},{12,8},{9,1... | collective-permute-start | bytes 589832 | tf_op jit(solution)/shard_map/ppermute | solution.py:496
  14.1 1.1 %collective-permute-done.rest_1_ = f32[4,6,16,128]{3,2,1,0:T(8,128)S(1)} collective-permute-done((f32[4,6,16,128]{3,2,1,0:T(8,128)S(1)}, f32[4,6,16,128]{3,2,1,0:T(8,128)S(1)}, u32[]{:S(2)}, u32[]{:S(2)}) %collective-permute-start) | collective-permute-done | bytes 196640 | tf_op jit(solution)/shard_map/ppermute | solution.py:496
  15.1 4.3 %faces.2 = (f32[8,3,16,128]{3,2,1,0:T(8,128)}, f32[3,64,128]{2,1,0:T(8,128)S(1)}, f32[60,128]{1,0:T(8,128)S(1)}) custom-call(s32[64]{0:T(128)} %bitcast.21, s32[64]{0:T(128)} %cell_from.3, f32[3,64,128]{2,1,0:T(8,128)S(1)} %bitcast.14, f32[3,64,128]{2,1,0:T(8,128)S(1)} %bitcast.16, f32[4,6,16,128]{3,2,1,0:T(8,128)S(1)} %all-to-all-done.rest_0_, ...), custom_call_target="tpu_custom_call" | custom-call | flops 4000000000 | tf_op jit(solution)/shard_map/faces/pallas_call | solution.py:448
  19.5 4.9 %all-to-all-start.1 = ((f32[8,3,16,128]{3,2,1,0:T(8,128)}), f32[8,3,16,128]{3,2,1,0:T(8,128)S(1)}, u32[]{:S(2)}, u32[]{:S(2)}) async-start(f32[8,3,16,128]{3,2,1,0:T(8,128)} %get-tuple-element.37), calls=%async_computation.1 | async-start | bytes 393216 | tf_op jit(solution)/shard_map/all_to_all | solution.py:492
  24.4 3.4 %collective-permute-start.1 = (f32[60,128]{1,0:T(8,128)S(1)}, f32[60,128]{1,0:T(8,128)S(1)}, u32[]{:S(2)}, u32[]{:S(2)}) collective-permute-start(f32[60,128]{1,0:T(8,128)S(1)} %get-tuple-element.39), channel_id=1, source_target_pairs={{4,8},{8,4},{12,16},{16,12},{20,24},{24,20},{5,9},{9,5},{13,17},{1... | collective-permute-start | bytes 92168 | tf_op jit(solution)/shard_map/ppermute | solution.py:555
  27.7 2.8 %collective-permute-done.1.rest_2_ = f32[60,128]{1,0:T(8,128)S(1)} collective-permute-done((f32[60,128]{1,0:T(8,128)S(1)}, f32[60,128]{1,0:T(8,128)S(1)}, u32[]{:S(2)}, u32[]{:S(2)}) %collective-permute-start.1) | collective-permute-done | bytes 30752 | tf_op jit(solution)/shard_map/ppermute | solution.py:555
  30.6 2.2 %outer.2.outer_ref = f32[3,16,128]{2,1,0:T(8,128)S(1)} custom-call(f32[3,16,128]{2,1,0:T(8,128)S(1)} %get-tuple-element.33.x_ref, f32[3,16,128]{2,1,0:T(8,128)S(1)} %bitcast.12, bf16[16,80,256]{2,1,0:T(8,128)(2,1)S(1)} %get-tuple-element.38.right_ref, f32[4,6,16,128]{3,2,1,0:T(8,128)S(1)} %all-to-all-done.rest_0_, ...), custom_call_target="tpu_custom_call" | custom-call | flops 1000000000 | tf_op jit(solution)/shard_map/outer/pallas_call | solution.py:448
  32.8 0.0 all-to-all-done.1.back_ref
  32.8 0.7 %update.2 = (f32[3,16,128]{2,1,0:T(8,128)S(1)}, f32[3,16,128]{2,1,0:T(8,128)S(1)}, f32[3,16,128]{2,1,0:T(8,128)S(1)}, f32[8,3,16,128]{3,2,1,0:T(8,128)}) custom-call(f32[16,128]{1,0:T(8,128)S(1)} %get-tuple-element.31.live_ref, f32[3,16,128]{2,1,0:T(8,128)S(1)} %bitcast.9, f32[3,16,128]{2,1,0:T(8,128)S(1)} %bitcast.13, ...), custom_call_target="tpu_custom_call" | custom-call | flops 1000000 | tf_op jit(solution)/shard_map/update/pallas_call | solution.py:448
  33.5 4.8 %all-to-all-start.2 = ((f32[8,3,16,128]{3,2,1,0:T(8,128)}), f32[8,3,16,128]{3,2,1,0:T(8,128)S(1)}, u32[]{:S(2)}, u32[]{:S(2)}) async-start(f32[8,3,16,128]{3,2,1,0:T(8,128)} %get-tuple-element.44), calls=%async_computation.2 | async-start | bytes 393216 | tf_op jit(solution)/shard_map/all_to_all | solution.py:492
  38.3 3.1 %inner.3 = (f32[3,16,128]{2,1,0:T(8,128)S(1)}, bf16[16,80,256]{2,1,0:T(8,128)(2,1)S(1)}) custom-call(f32[3,16,128]{2,1,0:T(8,128)S(1)} %get-tuple-element.45.x_ref, f32[3,16,128]{2,1,0:T(8,128)S(1)} %get-tuple-element.43.v_ref), custom_call_target="tpu_custom_call" | custom-call | flops 1000000000 | tf_op jit(solution)/shard_map/inner/pallas_call | solution.py:448
  41.4 2.8 %all-to-all-done.2.rest_2_.rest_3_ = f32[8,3,16,128]{3,2,1,0:T(8,128)S(1)} async-done(((f32[8,3,16,128]{3,2,1,0:T(8,128)}), f32[8,3,16,128]{3,2,1,0:T(8,128)S(1)}, u32[]{:S(2)}, u32[]{:S(2)}) %all-to-all-start.2) | async-done | bytes 196640 | tf_op jit(solution)/shard_map/all_to_all | solution.py:492
  44.2 4.5 %faces.3 = (f32[8,3,16,128]{3,2,1,0:T(8,128)}, f32[3,64,128]{2,1,0:T(8,128)S(1)}, f32[30,128]{1,0:T(8,128)S(1)}) custom-call(s32[64]{0:T(128)} %bitcast.22, s32[64]{0:T(128)} %cell_from.3, f32[3,64,128]{2,1,0:T(8,128)S(1)} %bitcast.15, f32[3,64,128]{2,1,0:T(8,128)S(1)} %bitcast.17, f32[4,6,16,128]{3,2,1,0:T(8,128)S(1)} %all-to-all-done.rest_0_, ...), custom_call_target="tpu_custom_call" | custom-call | flops 4000000000 | tf_op jit(solution)/shard_map/faces/pallas_call | solution.py:448
  48.7 5.4 %all-to-all-start.3 = ((f32[8,3,16,128]{3,2,1,0:T(8,128)}), f32[8,3,16,128]{3,2,1,0:T(8,128)S(1)}, u32[]{:S(2)}, u32[]{:S(2)}) async-start(f32[8,3,16,128]{3,2,1,0:T(8,128)} %get-tuple-element.50), calls=%async_computation.3 | async-start | bytes 393216 | tf_op jit(solution)/shard_map/all_to_all | solution.py:492
  54.0 3.5 %collective-permute-start.2 = (f32[30,128]{1,0:T(8,128)S(1)}, f32[30,128]{1,0:T(8,128)S(1)}, u32[]{:S(2)}, u32[]{:S(2)}) collective-permute-start(f32[30,128]{1,0:T(8,128)S(1)} %get-tuple-element.52), channel_id=1, source_target_pairs={{4,8},{8,4},{12,16},{16,12},{20,24},{24,20},{5,9},{9,5},{13,17},{1... | collective-permute-start | bytes 46088 | tf_op jit(solution)/shard_map/ppermute | solution.py:555
  57.6 2.4 %collective-permute-done.2.rest_4_ = f32[30,128]{1,0:T(8,128)S(1)} collective-permute-done((f32[30,128]{1,0:T(8,128)S(1)}, f32[30,128]{1,0:T(8,128)S(1)}, u32[]{:S(2)}, u32[]{:S(2)}) %collective-permute-start.2) | collective-permute-done | bytes 15392 | tf_op jit(solution)/shard_map/ppermute | solution.py:555
  60.0 2.2 %outer.3.outer_ref = f32[3,16,128]{2,1,0:T(8,128)S(1)} custom-call(f32[3,16,128]{2,1,0:T(8,128)S(1)} %get-tuple-element.45.x_ref, f32[3,16,128]{2,1,0:T(8,128)S(1)} %get-tuple-element.43.v_ref, bf16[16,80,256]{2,1,0:T(8,128)(2,1)S(1)} %get-tuple-element.51.right_ref, f32[4,6,16,128]{3,2,1,0:T(8,128)S(1)} %all-to-all-done.rest_0_, ...), custom_call_target="tpu_custom_call" | custom-call | flops 1000000000 | tf_op jit(solution)/shard_map/outer/pallas_call | solution.py:448
  62.2 0.0 all-to-all-done.3.back_ref
  62.2 0.7 %update.3 = (f32[3,16,128]{2,1,0:T(8,128)}, f32[3,16,128]{2,1,0:T(8,128)}, f32[3,64,128]{2,1,0:T(8,128)}) custom-call(f32[16,128]{1,0:T(8,128)S(1)} %get-tuple-element.31.live_ref, f32[3,16,128]{2,1,0:T(8,128)S(1)} %get-tuple-element.42.x_ref, f32[3,16,128]{2,1,0:T(8,128)S(1)} %get-tuple-element.43.v_ref, f32[3,16,128]{2,1,0:T(8,128)S(1)} %get-tuple-element.47.inner_ref, ...), custom_call_target="tpu_custom_call" | custom-call | flops 1000000 | tf_op jit(solution)/shard_map/update/pallas_call | solution.py:448
  (7 shorter events, 0.0 us)
Async XLA Ops:
  2.1 4.8 %copy-start.1 = (f32[3,2,8,128]{3,2,1,0:T(8,128)S(1)}, f32[3,2,8,128]{3,2,1,0:T(8,128)}, u32[]{:S(2)}) copy-start(f32[3,2,8,128]{3,2,1,0:T(8,128)} %param.8) | copy-start | bytes 73732
  2.1 9.8 %all-to-all-start = ((f32[4,6,16,128]{3,2,1,0:T(8,128)}), f32[4,6,16,128]{3,2,1,0:T(8,128)S(1)}, u32[]{:S(2)}, u32[]{:S(2)}) async-start(f32[4,6,16,128]{3,2,1,0:T(8,128)} %get-tuple-element.32), calls=%async_computation | async-start | bytes 393216 | tf_op jit(solution)/shard_map/all_to_all | solution.py:492
  6.9 8.3 %copy-start.2 = (f32[64,3,128]{2,0,1:T(8,128)S(1)}, f32[64,3,128]{2,0,1:T(8,128)}, u32[]{:S(2)}) copy-start(f32[64,3,128]{2,0,1:T(8,128)} %param.10) | copy-start | bytes 294916
  6.9 8.3 %copy-start.3 = (f32[64,3,128]{2,0,1:T(8,128)S(1)}, f32[64,3,128]{2,0,1:T(8,128)}, u32[]{:S(2)}) copy-start(f32[64,3,128]{2,0,1:T(8,128)} %param.11) | copy-start | bytes 294916
  11.9 3.3 %collective-permute-start = (f32[4,6,16,128]{3,2,1,0:T(8,128)S(1)}, f32[4,6,16,128]{3,2,1,0:T(8,128)S(1)}, u32[]{:S(2)}, u32[]{:S(2)}) collective-permute-start(f32[4,6,16,128]{3,2,1,0:T(8,128)S(1)} %all-to-all-done.rest_0_), channel_id=1, source_target_pairs={{0,4},{4,0},{1,5},{5,1},{2,6},{6,2},{3,7},{7,3},{8,12},{12,8},{9,1... | collective-permute-start | bytes 589832 | tf_op jit(solution)/shard_map/ppermute | solution.py:496
  19.5 13.3 %all-to-all-start.1 = ((f32[8,3,16,128]{3,2,1,0:T(8,128)}), f32[8,3,16,128]{3,2,1,0:T(8,128)S(1)}, u32[]{:S(2)}, u32[]{:S(2)}) async-start(f32[8,3,16,128]{3,2,1,0:T(8,128)} %get-tuple-element.37), calls=%async_computation.1 | async-start | bytes 393216 | tf_op jit(solution)/shard_map/all_to_all | solution.py:492
  24.4 6.2 %collective-permute-start.1 = (f32[60,128]{1,0:T(8,128)S(1)}, f32[60,128]{1,0:T(8,128)S(1)}, u32[]{:S(2)}, u32[]{:S(2)}) collective-permute-start(f32[60,128]{1,0:T(8,128)S(1)} %get-tuple-element.39), channel_id=1, source_target_pairs={{4,8},{8,4},{12,16},{16,12},{20,24},{24,20},{5,9},{9,5},{13,17},{1... | collective-permute-start | bytes 92168 | tf_op jit(solution)/shard_map/ppermute | solution.py:555
  30.6 2.2 %copy-start = (f32[3,2,8,128]{3,2,1,0:T(8,128)S(1)}, f32[3,2,8,128]{3,2,1,0:T(8,128)}, u32[]{:S(2)}) copy-start(f32[3,2,8,128]{3,2,1,0:T(8,128)} %param.7) | copy-start | bytes 73732
  33.5 10.7 %all-to-all-start.2 = ((f32[8,3,16,128]{3,2,1,0:T(8,128)}), f32[8,3,16,128]{3,2,1,0:T(8,128)S(1)}, u32[]{:S(2)}, u32[]{:S(2)}) async-start(f32[8,3,16,128]{3,2,1,0:T(8,128)} %get-tuple-element.44), calls=%async_computation.2 | async-start | bytes 393216 | tf_op jit(solution)/shard_map/all_to_all | solution.py:492
  48.7 13.5 %all-to-all-start.3 = ((f32[8,3,16,128]{3,2,1,0:T(8,128)}), f32[8,3,16,128]{3,2,1,0:T(8,128)S(1)}, u32[]{:S(2)}, u32[]{:S(2)}) async-start(f32[8,3,16,128]{3,2,1,0:T(8,128)} %get-tuple-element.50), calls=%async_computation.3 | async-start | bytes 393216 | tf_op jit(solution)/shard_map/all_to_all | solution.py:492
  54.0 5.9 %collective-permute-start.2 = (f32[30,128]{1,0:T(8,128)S(1)}, f32[30,128]{1,0:T(8,128)S(1)}, u32[]{:S(2)}, u32[]{:S(2)}) collective-permute-start(f32[30,128]{1,0:T(8,128)S(1)} %get-tuple-element.52), channel_id=1, source_target_pairs={{4,8},{8,4},{12,16},{16,12},{20,24},{24,20},{5,9},{9,5},{13,17},{1... | collective-permute-start | bytes 46088 | tf_op jit(solution)/shard_map/ppermute | solution.py:555

commit v7 on v6

--- a/solution.py
+++ b/solution.py
@@ -189,7 +189,8 @@
 
     def line(self, shift, device, field, cell):
         if len(self.refs) == 2:
-            return self.refs[0 if shift == 0 else 1][device, field, pl.ds(cell, 1), :]
+            own = isinstance(shift, int) and shift == 0
+            return self.refs[0 if own else 1][device, field, pl.ds(cell, 1), :]
         tracks = self.refs[0].shape[0] // self.crosses
         track = jnp.clip(self.track + shift, 0, tracks - 1)
         return self.refs[0][track * self.crosses + device, field, pl.ds(cell, 1), :]
@@ -274,6 +275,98 @@
     for (index, _), sums in zip(jobs, pushes(left_ref, sum_ref, right_ref, jobs)):
         start = ((index // cc + 1) * wide + index % cc + 1) * 8
         store_rows(out_ref, moment(state_ref[pl.ds(start, 8), :], sums), index, False)
+
+
+def put_ring(state_ref, slot, across, along, load, second, ok):
+    for axis in range(3):
+        x, v = load(axis, 6, 0), load(axis + 3, 6, 0)
+        if second:
+            x, v = advanced(x, v, load(axis, 3, 1), axis)
+        if axis == 0:
+            x = jnp.where(ok, x + across, far)
+        if axis == 1:
+            x = jnp.where(ok, x + along, 0.0)
+        state_ref[pl.ds(slot * 8 + axis, 1), :] = x
+        state_ref[pl.ds(slot * 8 + 3 + axis, 1), :] = jnp.where(ok, v, 0.0)
+
+
+def row_jobs(ct, cc, own_row):
+    jobs = [(own_row * cc + c, [c + d for d in range(3)]) for c in range(cc)]
+    starts = [((own_row + 1) * (cc + 2) + c + 1) * 8 for c in range(cc)]
+    return jobs, [pl.multiple_of(start, 8) for start in starts]
+
+
+def near_kernel(ct, cc, crosses, second, x_ref, v_ref, right_ref, *rest):
+    track, c_index = lax.axis_index("track"), lax.axis_index("cross")
+    gathered = [Gathered(rest[:2], crosses, track)]
+    rest = rest[2:]
+    if second:
+        gathered.append(Gathered(rest[:1], crosses, track))
+        rest = rest[1:]
+    out_ref, state_ref, left_ref, sum_ref, own_ref = rest
+    wide = cc + 2
+    put_own(own_ref, x_ref, v_ref, ct, cc)
+    has_low, has_high = c_index > 0, c_index < crosses - 1
+    middle, centre = (ct + 1) / 2, (cc + 1) / 2
+    first = track == 0
+    shift = jnp.where(first, 1, -1)
+    across = jnp.where(first, ct + 1 - middle, -middle)
+    row = jnp.where(first, 0, ct - 1)
+
+    def from_all(shift, row, p):
+        step = -1 if p == 0 else (1 if p == cc + 1 else 0)
+        device = jnp.clip(c_index + step, 0, crosses - 1)
+        cell = row * cc + (p - 1) % cc
+        return lambda f, n, k: gathered[k].line(shift, device, f, cell)
+
+    for p in range(wide):
+        ok = has_low if p == 0 else (has_high if p == cc + 1 else first | (track > 0))
+        put_ring(state_ref, p, across, p - centre, from_all(shift, row, p), second, ok)
+    sides = {}
+    for r in range(ct):
+        for p, ok in ((0, has_low), (cc + 1, has_high)):
+            sides[r, p] = wide + len(sides)
+            load = from_all(0, r, p)
+            put_ring(state_ref, sides[r, p], r + 1 - middle, p - centre, load, second, ok)
+    build_left(state_ref, left_ref, sum_ref, range(wide + len(sides)))
+    jobs, starts = row_jobs(ct, cc, jnp.where(first, ct - 1, 0))
+    for r in range(ct):
+        near = range(max(r - 1, 0), min(r + 2, ct))
+        for c, p in ((0, 0), (cc - 1, cc + 1)):
+            jobs.append((r * cc + c, [sides[q, p] for q in near]))
+            starts.append(((r + 1) * wide + c + 1) * 8)
+    out_ref[...] = jnp.zeros_like(out_ref)
+    for (index, _), start, sums in zip(jobs, starts, pushes(left_ref, sum_ref, right_ref, jobs)):
+        store_rows(out_ref, moment(own_ref[pl.ds(start, 8), :], sums), index, True)
+
+
+def far_kernel(ct, cc, crosses, second, x_ref, v_ref, right_ref, near_ref, *rest):
+    track, c_index = lax.axis_index("track"), lax.axis_index("cross")
+    vehicle, vehicles = lax.axis_index("vehicle"), lax.axis_size("vehicle")
+    halos, rest = (rest[:2], rest[2:]) if second else (rest[:1], rest[1:])
+    out_ref, state_ref, left_ref, sum_ref, own_ref = rest
+    wide = cc + 2
+    put_own(own_ref, x_ref, v_ref, ct, cc)
+    middle, centre = (ct + 1) / 2, (cc + 1) / 2
+    first = track == 0
+    across = jnp.where(first, -middle, ct + 1 - middle)
+    exists = jnp.where(first, vehicle, vehicles - 1 - vehicle) > 0
+    for p in range(wide):
+        ok = exists
+        if p == 0:
+            ok = ok & (c_index > 0)
+        if p == cc + 1:
+            ok = ok & (c_index < crosses - 1)
+
+        def load(f, n, k, p=p):
+            return halos[k][pl.ds(p * n + f, 1), :]
+
+        put_ring(state_ref, p, across, p - centre, load, second, ok)
+    build_left(state_ref, left_ref, sum_ref, range(wide))
+    jobs, starts = row_jobs(ct, cc, jnp.where(first, 0, ct - 1))
+    out_ref[...] = near_ref[...]
+    for (index, _), start, sums in zip(jobs, starts, pushes(left_ref, sum_ref, right_ref, jobs)):
+        store_rows(out_ref, moment(own_ref[pl.ds(start, 8), :], sums), index, True)
 
 
 def face_kernel(
@@ -557,15 +650,40 @@
             halo_extra = [across]
         else:
             beyond, halo_extra = across, []
-        outer = call(
-            functools.partial(outer_kernel, ct, cc, crosses, nrefs, second),
-            "outer",
-            [],
-            [own, v, rights] + everyone + [beyond] + extra + halo_extra,
-            [block],
-            ring_slots,
-            10**9,
-        )[0]
+        if pair:
+            near = call(
+                functools.partial(near_kernel, ct, cc, crosses, second),
+                "near",
+                [],
+                [own, v, rights] + everyone + extra,
+                [block],
+                ring_slots + ring_slots[:1],
+                10**9,
+            )[0]
+            near, halo_now = lax.optimization_barrier((near, across))
+            if second:
+                halo_extra = [halo_now]
+            else:
+                beyond = halo_now
+            outer = call(
+                functools.partial(far_kernel, ct, cc, crosses, second),
+                "far",
+                [],
+                [own, v, rights, near, beyond] + halo_extra,
+                [block],
+                ring_slots + ring_slots[:1],
+                10**9,
+            )[0]
+        else:
+            outer = call(
+                functools.partial(outer_kernel, ct, cc, crosses, nrefs, second),
+                "outer",
+                [],
+                [own, v, rights] + everyone + [beyond] + extra + halo_extra,
+                [block],
+                ring_slots,
+                10**9,
+            )[0]
         returned, outer = lax.optimization_barrier(
             (exchange(part, ("track", "cross")), outer)
         )

time: 63.5 us -> 62 us (0.976)
  the two profiles are of different devices: /device:TPU:11 before, /device:TPU:5 now
where the time goes in v7:
time: 62 us; the launch traced here: 61.4 us
  starting transfers between devices  25.2 us (41%)
  Pallas kernels  22.9 us (37%)
  waiting for transfers between devices  12.5 us (20%)
  between operations  0.73 us (1%)
    pallas_call x11, Pallas kernels, call(): pl.pallas_call(kernel, name=name, out_shape=shapes, in_specs=specs, out_s...  22.9 us
    all_to_all x4, starting transfers between devices, exchange(): return lax.all_to_all(a, axes, split_axis=0, concat_axis=0, tiled=True)  16.6 us
    all_to_all x4, waiting for transfers between devices, exchange(): return lax.all_to_all(a, axes, split_axis=0, concat_axis=0, tiled=True)  8.78 us
    ppermute x2, starting transfers between devices, body(): across = lax.ppermute(packed, ('vehicle', 'track'), travel)  5.36 us
    ppermute x1, starting transfers between devices, gather_track(): return [a, lax.ppermute(a, 'track', swap)]  3.26 us
    ppermute x2, waiting for transfers between devices, body(): across = lax.ppermute(packed, ('vehicle', 'track'), travel)  2.62 us
  transfers between devices with their start and end apart: 7, of which 7 were waited for; matrix products, arithmetic and copies ran while one was open for 0% of the time, Pallas kernels for 18%

profile of v7, /device:TPU:5, one launch (start us, length us, event | category | flops | bytes accessed | tf_op | source)
XLA Modules:
  0.0 61.4 jit_solution(2388780856485641399)
XLA Ops:
  0.6 1.5 %first.1 = (f32[3,16,128]{2,1,0:T(8,128)S(1)}, f32[16,128]{1,0:T(8,128)S(1)}, f32[4,6,16,128]{3,2,1,0:T(8,128)}) custom-call(s32[2,8]{1,0:T(2,128)} %count_from.1, f32[3,16,128]{2,1,0:T(8,128)} %bitcast.8, f32[3,16,128]{2,1,0:T(8,128)} %bitcast.10), custom_call_target="tpu_custom_call" | custom-call | flops 1000000 | tf_op jit(solution)/shard_map/first/pallas_call | solution.py:541
  2.1 4.6 %all-to-all-start = ((f32[4,6,16,128]{3,2,1,0:T(8,128)}), f32[4,6,16,128]{3,2,1,0:T(8,128)S(1)}, u32[]{:S(2)}, u32[]{:S(2)}) async-start(f32[4,6,16,128]{3,2,1,0:T(8,128)} %get-tuple-element.36), calls=%async_computation | async-start | bytes 393216 | tf_op jit(solution)/shard_map/all_to_all | solution.py:585
  6.7 3.1 %inner.2 = (f32[3,16,128]{2,1,0:T(8,128)S(1)}, bf16[16,80,256]{2,1,0:T(8,128)(2,1)S(1)}) custom-call(f32[3,16,128]{2,1,0:T(8,128)S(1)} %get-tuple-element.37.x_ref, f32[3,16,128]{2,1,0:T(8,128)S(1)} %bitcast.11), custom_call_target="tpu_custom_call" | custom-call | flops 1000000000 | tf_op jit(solution)/shard_map/inner/pallas_call | solution.py:541
  9.8 2.1 %all-to-all-done.rest_0_ = f32[4,6,16,128]{3,2,1,0:T(8,128)S(1)} async-done(((f32[4,6,16,128]{3,2,1,0:T(8,128)}), f32[4,6,16,128]{3,2,1,0:T(8,128)S(1)}, u32[]{:S(2)}, u32[]{:S(2)}) %all-to-all-start) | async-done | bytes 196640 | tf_op jit(solution)/shard_map/all_to_all | solution.py:585
  11.9 3.3 %collective-permute-start = (f32[4,6,16,128]{3,2,1,0:T(8,128)S(1)}, f32[4,6,16,128]{3,2,1,0:T(8,128)S(1)}, u32[]{:S(2)}, u32[]{:S(2)}) collective-permute-start(f32[4,6,16,128]{3,2,1,0:T(8,128)S(1)} %all-to-all-done.rest_0_), channel_id=1, source_target_pairs={{0,4},{4,0},{1,5},{5,1},{2,6},{6,2},{3,7},{7,3},{8,12},{12,8},{9,1... | collective-permute-start | bytes 589832 | tf_op jit(solution)/shard_map/ppermute | solution.py:589
  15.2 1.1 %collective-permute-done.rest_1_ = f32[4,6,16,128]{3,2,1,0:T(8,128)S(1)} collective-permute-done((f32[4,6,16,128]{3,2,1,0:T(8,128)S(1)}, f32[4,6,16,128]{3,2,1,0:T(8,128)S(1)}, u32[]{:S(2)}, u32[]{:S(2)}) %collective-permute-start) | collective-permute-done | bytes 196640 | tf_op jit(solution)/shard_map/ppermute | solution.py:589
  16.3 4.3 %faces.2 = (f32[8,3,16,128]{3,2,1,0:T(8,128)}, f32[3,64,128]{2,1,0:T(8,128)S(1)}, f32[60,128]{1,0:T(8,128)S(1)}) custom-call(s32[64]{0:T(128)} %bitcast.22, s32[64]{0:T(128)} %cell_from.3, f32[3,64,128]{2,1,0:T(8,128)S(1)} %bitcast.15, f32[3,64,128]{2,1,0:T(8,128)S(1)} %bitcast.17, f32[4,6,16,128]{3,2,1,0:T(8,128)S(1)} %all-to-all-done.rest_0_, ...), custom_call_target="tpu_custom_call" | custom-call | flops 4000000000 | tf_op jit(solution)/shard_map/faces/pallas_call | solution.py:541
  20.6 3.7 %all-to-all-start.1 = ((f32[8,3,16,128]{3,2,1,0:T(8,128)}), f32[8,3,16,128]{3,2,1,0:T(8,128)S(1)}, u32[]{:S(2)}, u32[]{:S(2)}) async-start(f32[8,3,16,128]{3,2,1,0:T(8,128)} %get-tuple-element.41), calls=%async_computation.1 | async-start | bytes 393216 | tf_op jit(solution)/shard_map/all_to_all | solution.py:585
  24.3 3.1 %collective-permute-start.1 = (f32[60,128]{1,0:T(8,128)S(1)}, f32[60,128]{1,0:T(8,128)S(1)}, u32[]{:S(2)}, u32[]{:S(2)}) collective-permute-start(f32[60,128]{1,0:T(8,128)S(1)} %get-tuple-element.43), channel_id=1, source_target_pairs={{4,8},{8,4},{12,16},{16,12},{20,24},{24,20},{5,9},{9,5},{13,17},{1... | collective-permute-start | bytes 92168 | tf_op jit(solution)/shard_map/ppermute | solution.py:648
  27.4 1.4 %near.2.near_ref = f32[3,16,128]{2,1,0:T(8,128)S(1)} custom-call(f32[3,16,128]{2,1,0:T(8,128)S(1)} %get-tuple-element.37.x_ref, f32[3,16,128]{2,1,0:T(8,128)S(1)} %bitcast.12, bf16[16,80,256]{2,1,0:T(8,128)(2,1)S(1)} %get-tuple-element.42.right_ref, f32[4,6,16,128]{3,2,1,0:T(8,128)S(1)} %all-to-all-done.rest_0_, ...), custom_call_target="tpu_custom_call" | custom-call | flops 1000000000 | tf_op jit(solution)/shard_map/near/pallas_call | solution.py:541
  28.8 1.0 %collective-permute-done.1.rest_0_ = f32[60,128]{1,0:T(8,128)S(1)} collective-permute-done((f32[60,128]{1,0:T(8,128)S(1)}, f32[60,128]{1,0:T(8,128)S(1)}, u32[]{:S(2)}, u32[]{:S(2)}) %collective-permute-start.1) | collective-permute-done | bytes 30752 | tf_op jit(solution)/shard_map/ppermute | solution.py:648
  29.8 1.1 %far.2.outer_ref = f32[3,16,128]{2,1,0:T(8,128)S(1)} custom-call(f32[3,16,128]{2,1,0:T(8,128)S(1)} %get-tuple-element.37.x_ref, f32[3,16,128]{2,1,0:T(8,128)S(1)} %bitcast.13, bf16[16,80,256]{2,1,0:T(8,128)(2,1)S(1)} %get-tuple-element.42.right_ref, f32[3,16,128]{2,1,0:T(8,128)S(1)} %near.2.near_ref, f32[60,128]{1,0:T(8,128)S(1)} %collective-permute-done.1.rest_0_), custom_call_target="tpu_custom_call" | custom-call | flops 1000000000 | tf_op jit(solution)/shard_map/far/pallas_call | solution.py:541
  30.9 1.0 %all-to-all-done.1.back_ref = f32[8,3,16,128]{3,2,1,0:T(8,128)S(1)} async-done(((f32[8,3,16,128]{3,2,1,0:T(8,128)}), f32[8,3,16,128]{3,2,1,0:T(8,128)S(1)}, u32[]{:S(2)}, u32[]{:S(2)}) %all-to-all-start.1) | async-done | bytes 196640 | tf_op jit(solution)/shard_map/all_to_all | solution.py:585
  31.9 0.7 %update.2 = (f32[3,16,128]{2,1,0:T(8,128)S(1)}, f32[3,16,128]{2,1,0:T(8,128)S(1)}, f32[3,16,128]{2,1,0:T(8,128)S(1)}, f32[8,3,16,128]{3,2,1,0:T(8,128)}) custom-call(f32[16,128]{1,0:T(8,128)S(1)} %get-tuple-element.35.live_ref, f32[3,16,128]{2,1,0:T(8,128)S(1)} %bitcast.9, f32[3,16,128]{2,1,0:T(8,128)S(1)} %bitcast.14, ...), custom_call_target="tpu_custom_call" | custom-call | flops 1000000 | tf_op jit(solution)/shard_map/update/pallas_call | solution.py:541
  32.6 4.7 %all-to-all-start.2 = ((f32[8,3,16,128]{3,2,1,0:T(8,128)}), f32[8,3,16,128]{3,2,1,0:T(8,128)S(1)}, u32[]{:S(2)}, u32[]{:S(2)}) async-start(f32[8,3,16,128]{3,2,1,0:T(8,128)} %get-tuple-element.50), calls=%async_computation.2 | async-start | bytes 393216 | tf_op jit(solution)/shard_map/all_to_all | solution.py:585
  37.3 3.1 %inner.3 = (f32[3,16,128]{2,1,0:T(8,128)S(1)}, bf16[16,80,256]{2,1,0:T(8,128)(2,1)S(1)}) custom-call(f32[3,16,128]{2,1,0:T(8,128)S(1)} %get-tuple-element.51.x_ref, f32[3,16,128]{2,1,0:T(8,128)S(1)} %get-tuple-element.49.v_ref), custom_call_target="tpu_custom_call" | custom-call | flops 1000000000 | tf_op jit(solution)/shard_map/inner/pallas_call | solution.py:541
  40.4 4.5 %all-to-all-done.2.rest_2_ = f32[8,3,16,128]{3,2,1,0:T(8,128)S(1)} async-done(((f32[8,3,16,128]{3,2,1,0:T(8,128)}), f32[8,3,16,128]{3,2,1,0:T(8,128)S(1)}, u32[]{:S(2)}, u32[]{:S(2)}) %all-to-all-start.2) | async-done | bytes 196640 | tf_op jit(solution)/shard_map/all_to_all | solution.py:585
  44.9 4.5 %faces.3 = (f32[8,3,16,128]{3,2,1,0:T(8,128)}, f32[3,64,128]{2,1,0:T(8,128)S(1)}, f32[30,128]{1,0:T(8,128)S(1)}) custom-call(s32[64]{0:T(128)} %bitcast.23, s32[64]{0:T(128)} %cell_from.3, f32[3,64,128]{2,1,0:T(8,128)S(1)} %bitcast.16, f32[3,64,128]{2,1,0:T(8,128)S(1)} %bitcast.18, f32[4,6,16,128]{3,2,1,0:T(8,128)S(1)} %all-to-all-done.rest_0_, ...), custom_call_target="tpu_custom_call" | custom-call | flops 4000000000 | tf_op jit(solution)/shard_map/faces/pallas_call | solution.py:541
  49.4 3.6 %all-to-all-start.3 = ((f32[8,3,16,128]{3,2,1,0:T(8,128)}), f32[8,3,16,128]{3,2,1,0:T(8,128)S(1)}, u32[]{:S(2)}, u32[]{:S(2)}) async-start(f32[8,3,16,128]{3,2,1,0:T(8,128)} %get-tuple-element.56), calls=%async_computation.3 | async-start | bytes 393216 | tf_op jit(solution)/shard_map/all_to_all | solution.py:585
  53.0 2.3 %collective-permute-start.2 = (f32[30,128]{1,0:T(8,128)S(1)}, f32[30,128]{1,0:T(8,128)S(1)}, u32[]{:S(2)}, u32[]{:S(2)}) collective-permute-start(f32[30,128]{1,0:T(8,128)S(1)} %get-tuple-element.58), channel_id=1, source_target_pairs={{4,8},{8,4},{12,16},{16,12},{20,24},{24,20},{5,9},{9,5},{13,17},{1... | collective-permute-start | bytes 46088 | tf_op jit(solution)/shard_map/ppermute | solution.py:648
  55.3 1.4 %near.3.near_ref = f32[3,16,128]{2,1,0:T(8,128)S(1)} custom-call(f32[3,16,128]{2,1,0:T(8,128)S(1)} %get-tuple-element.51.x_ref, f32[3,16,128]{2,1,0:T(8,128)S(1)} %get-tuple-element.49.v_ref, bf16[16,80,256]{2,1,0:T(8,128)(2,1)S(1)} %get-tuple-element.57.right_ref, f32[4,6,16,128]{3,2,1,0:T(8,128)S(1)} %all-to-all-done.rest_0_, ...), custom_call_target="tpu_custom_call" | custom-call | flops 1000000000 | tf_op jit(solution)/shard_map/near/pallas_call | solution.py:541
  56.8 1.6 %collective-permute-done.2.rest_1_ = f32[30,128]{1,0:T(8,128)S(1)} collective-permute-done((f32[30,128]{1,0:T(8,128)S(1)}, f32[30,128]{1,0:T(8,128)S(1)}, u32[]{:S(2)}, u32[]{:S(2)}) %collective-permute-start.2) | collective-permute-done | bytes 15392 | tf_op jit(solution)/shard_map/ppermute | solution.py:648
  58.4 1.1 %far.3.outer_ref = f32[3,16,128]{2,1,0:T(8,128)S(1)} custom-call(f32[3,16,128]{2,1,0:T(8,128)S(1)} %get-tuple-element.51.x_ref, f32[3,16,128]{2,1,0:T(8,128)S(1)} %get-tuple-element.49.v_ref, bf16[16,80,256]{2,1,0:T(8,128)(2,1)S(1)} %get-tuple-element.57.right_ref, f32[3,16,128]{2,1,0:T(8,128)S(1)} %near.3.near_ref, ...), custom_call_target="tpu_custom_call" | custom-call | flops 1000000000 | tf_op jit(solution)/shard_map/far/pallas_call | solution.py:541
  59.5 1.2 %all-to-all-done.3.back_ref = f32[8,3,16,128]{3,2,1,0:T(8,128)S(1)} async-done(((f32[8,3,16,128]{3,2,1,0:T(8,128)}), f32[8,3,16,128]{3,2,1,0:T(8,128)S(1)}, u32[]{:S(2)}, u32[]{:S(2)}) %all-to-all-start.3) | async-done | bytes 196640 | tf_op jit(solution)/shard_map/all_to_all | solution.py:585
  (9 shorter events, 0.7 us)
Async XLA Ops:
  2.1 4.6 %copy-start.1 = (f32[3,2,8,128]{3,2,1,0:T(8,128)S(1)}, f32[3,2,8,128]{3,2,1,0:T(8,128)}, u32[]{:S(2)}) copy-start(f32[3,2,8,128]{3,2,1,0:T(8,128)} %param.8) | copy-start | bytes 73732
  2.1 9.8 %all-to-all-start = ((f32[4,6,16,128]{3,2,1,0:T(8,128)}), f32[4,6,16,128]{3,2,1,0:T(8,128)S(1)}, u32[]{:S(2)}, u32[]{:S(2)}) async-start(f32[4,6,16,128]{3,2,1,0:T(8,128)} %get-tuple-element.36), calls=%async_computation | async-start | bytes 393216 | tf_op jit(solution)/shard_map/all_to_all | solution.py:585
  6.7 9.5 %copy-start.2 = (f32[64,3,128]{2,0,1:T(8,128)S(1)}, f32[64,3,128]{2,0,1:T(8,128)}, u32[]{:S(2)}) copy-start(f32[64,3,128]{2,0,1:T(8,128)} %param.10) | copy-start | bytes 294916
  6.7 9.5 %copy-start.3 = (f32[64,3,128]{2,0,1:T(8,128)S(1)}, f32[64,3,128]{2,0,1:T(8,128)}, u32[]{:S(2)}) copy-start(f32[64,3,128]{2,0,1:T(8,128)} %param.11) | copy-start | bytes 294916
  11.9 4.3 %collective-permute-start = (f32[4,6,16,128]{3,2,1,0:T(8,128)S(1)}, f32[4,6,16,128]{3,2,1,0:T(8,128)S(1)}, u32[]{:S(2)}, u32[]{:S(2)}) collective-permute-start(f32[4,6,16,128]{3,2,1,0:T(8,128)S(1)} %all-to-all-done.rest_0_), channel_id=1, source_target_pairs={{0,4},{4,0},{1,5},{5,1},{2,6},{6,2},{3,7},{7,3},{8,12},{12,8},{9,1... | collective-permute-start | bytes 589832 | tf_op jit(solution)/shard_map/ppermute | solution.py:589
  20.6 11.3 %all-to-all-start.1 = ((f32[8,3,16,128]{3,2,1,0:T(8,128)}), f32[8,3,16,128]{3,2,1,0:T(8,128)S(1)}, u32[]{:S(2)}, u32[]{:S(2)}) async-start(f32[8,3,16,128]{3,2,1,0:T(8,128)} %get-tuple-element.41), calls=%async_computation.1 | async-start | bytes 393216 | tf_op jit(solution)/shard_map/all_to_all | solution.py:585
  24.3 5.5 %collective-permute-start.1 = (f32[60,128]{1,0:T(8,128)S(1)}, f32[60,128]{1,0:T(8,128)S(1)}, u32[]{:S(2)}, u32[]{:S(2)}) collective-permute-start(f32[60,128]{1,0:T(8,128)S(1)} %get-tuple-element.43), channel_id=1, source_target_pairs={{4,8},{8,4},{12,16},{16,12},{20,24},{24,20},{5,9},{9,5},{13,17},{1... | collective-permute-start | bytes 92168 | tf_op jit(solution)/shard_map/ppermute | solution.py:648
  28.8 3.1 %copy-start = (f32[3,2,8,128]{3,2,1,0:T(8,128)S(1)}, f32[3,2,8,128]{3,2,1,0:T(8,128)}, u32[]{:S(2)}) copy-start(f32[3,2,8,128]{3,2,1,0:T(8,128)} %param.7) | copy-start | bytes 73732
  32.6 12.3 %all-to-all-start.2 = ((f32[8,3,16,128]{3,2,1,0:T(8,128)}), f32[8,3,16,128]{3,2,1,0:T(8,128)S(1)}, u32[]{:S(2)}, u32[]{:S(2)}) async-start(f32[8,3,16,128]{3,2,1,0:T(8,128)} %get-tuple-element.50), calls=%async_computation.2 | async-start | bytes 393216 | tf_op jit(solution)/shard_map/all_to_all | solution.py:585
  49.4 11.2 %all-to-all-start.3 = ((f32[8,3,16,128]{3,2,1,0:T(8,128)}), f32[8,3,16,128]{3,2,1,0:T(8,128)S(1)}, u32[]{:S(2)}, u32[]{:S(2)}) async-start(f32[8,3,16,128]{3,2,1,0:T(8,128)} %get-tuple-element.56), calls=%async_computation.3 | async-start | bytes 393216 | tf_op jit(solution)/shard_map/all_to_all | solution.py:585
  53.0 5.3 %collective-permute-start.2 = (f32[30,128]{1,0:T(8,128)S(1)}, f32[30,128]{1,0:T(8,128)S(1)}, u32[]{:S(2)}, u32[]{:S(2)}) collective-permute-start(f32[30,128]{1,0:T(8,128)S(1)} %get-tuple-element.58), channel_id=1, source_target_pairs={{4,8},{8,4},{12,16},{16,12},{20,24},{24,20},{5,9},{9,5},{13,17},{1... | collective-permute-start | bytes 46088 | tf_op jit(solution)/shard_map/ppermute | solution.py:648
